TPU v7x, 32 devices: a whole 2x2x4 slice. The times are simulated.
32 devices in a mesh: vtx: 8 (over z, x), src: 4 (over y, core).
Axes of the slice: x: 2, y: 2, z: 4, core: 2. Of those that a mesh axis runs over, the one named last changes fastest.
Arguments:
- heat: float32 [64, 64, 8192], P(None, ('vtx', 'src')), may hold values from -12 to 12
- cotan: float32 [4, 64, 8192], P(None, 'vtx'), may hold values from 0.2 to 2
- source_index: int32 [64], replicated, may hold values from 0 to 524287
Outputs:
- normalised: float32 [64, 64, 8192], P('src', 'vtx')
- col_norm: float32 [64], P('src')
Inputs may be any that keep to these rules, and one draw needn't show every extreme that they name: `source_index`: row-major vertex indices, sources may share a vertex.
All inputs are finite; a program needn't handle non-finite values.
Results may differ from a plain program's by a relative error of at most 0.0003.
Values sent between devices are 32-bit elements; how exact they have to be, the bound alone decides.
No kernel may reach another device: no remote copies, remote signals or barrier semaphores. Data moves between devices by JAX's collectives and lax.ppermute only.
A program may use at most 64 MiB of HBM per device.

v0:
```python
import functools
import math

import jax
import jax.numpy as jnp
from jax import lax
from jax.experimental import pallas as pl
from jax.experimental.pallas import tpu as pltpu
from jax.sharding import PartitionSpec as P


LANES = 128
SUB = 8
PAD = 8
TAIL = 16


def pack_kernel(meta, heat, *refs):
    blocks, group, cb, own_rows, senders = meta
    n_out = max(out for *_, targets in blocks for out, *_ in targets) + 1
    outs = refs[:n_out]
    wide, in_sem = refs[n_out:]
    me = lax.axis_index("src")
    low = me < senders // 2
    reads, at = [], 0
    for b, (k, lo, n, _) in enumerate(blocks):
        size = n * cb * own_rows
        copy = pltpu.make_async_copy(
            heat.at[pl.ds(((me ^ k) * group + lo) * cb * own_rows, size), :], wide.at[pl.ds(at, size), :], in_sem.at[b]
        )
        copy.start()
        reads.append((copy, at))
        at += size
    for (copy, at), (k, lo, n, targets) in zip(reads, blocks, strict=True):
        copy.wait()
        for out, rows, skip, first, count in targets:
            start = at + skip * cb * own_rows + jnp.where(low, rows[0], rows[1])

            def step(i, _, start=start, ref=outs[out], first=first):
                for u in range(cb // SUB):
                    to = pl.multiple_of((first + i) * cb + u * SUB, SUB)
                    ref[pl.ds(to, SUB), :] = wide[pl.ds(start + (i * cb + u * SUB) * own_rows, SUB, stride=own_rows), :]
                return 0

            lax.fori_loop(0, count, step, 0)


def pack(heat, wanted, blocks, group, cb, own_rows, senders, limit):
    plan = []
    for k, lo, n in blocks:
        targets = []
        for out, (wk, rows, first, count) in enumerate(wanted):
            begin, end = max(lo, first), min(lo + n, first + count)
            if wk == k and begin < end:
                targets.append((out, rows, begin - lo, begin - first, end - begin))
        plan.append((k, lo, n, tuple(targets)))
    reads = sum(n for _, n in ((k, n) for k, _, n in blocks)) * cb * own_rows
    writes = sum(count for *_, count in wanted) * cb
    vmem = pl.BlockSpec(memory_space=pltpu.VMEM)
    return pl.pallas_call(
        functools.partial(pack_kernel, (tuple(plan), group, cb, own_rows, senders)),
        out_shape=tuple(jax.ShapeDtypeStruct((count * cb, LANES), jnp.float32) for *_, count in wanted),
        in_specs=[pl.BlockSpec(memory_space=pltpu.HBM)],
        out_specs=tuple(vmem for _ in wanted),
        scratch_shapes=[
            pltpu.VMEM((reads, LANES), jnp.float32),
            pltpu.SemaphoreType.DMA((len(blocks),)),
        ],
        compiler_params=pltpu.CompilerParams(vmem_limit_bytes=limit << 20),
        cost_estimate=pl.CostEstimate(flops=writes * LANES, bytes_accessed=4 * (reads + writes) * LANES, transcendentals=0),
    )(heat)


def weights_kernel(meta, cotan, lower, out):
    rows_dev, cb, total_rows = meta
    block_start = lax.axis_index("vtx") * rows_dev
    lane = lax.broadcasted_iota(jnp.int32, (SUB, LANES), 1)
    index = lax.broadcasted_iota(jnp.int32, (SUB, LANES), 0) * LANES + lane
    last_lane = lane == LANES - 1

    def column_step(q, _):
        at = pl.ds(pl.multiple_of(q * SUB, SUB), SUB)
        inside_left = index + q * SUB * LANES > 0
        inside_right = index + q * SUB * LANES < cb * LANES - 1

        def row_of(array, row, back=0):
            return cotan[pl.ds((array * cb + q * SUB - back) * rows_dev + row, SUB, stride=rows_dev), :]

        def from_left(value, before):
            moved = pltpu.roll(jnp.where(last_lane, before, value), 1, 1)
            return jnp.where(inside_left, moved, 0.0)

        south = lower[pl.ds(pl.multiple_of(q * SUB, SUB), SUB), :]
        southwest = from_left(
            lower[pl.ds(pl.multiple_of(cb + q * SUB, SUB), SUB), :], lower[pl.ds(cb - 1 + q * SUB, SUB), :]
        )
        for row in range(rows_dev):
            inside_row = jnp.full((SUB, LANES), block_start + row, jnp.int32) < total_rows - 1
            east = row_of(1, row)
            west = from_left(east, row_of(1, row, 1))
            east = jnp.where(inside_right, east, 0.0)
            north = jnp.where(inside_row, row_of(2, row), 0.0)
            raw = row_of(3, row)
            diag = jnp.where(inside_right & inside_row, raw, 0.0)
            centre = row_of(0, row) + east + west + north + south + diag + southwest
            for w, value in enumerate((centre, east, west, north, south, diag, southwest)):
                out[w, row, at, :] = value
            south, southwest = north, from_left(raw, row_of(3, row, 1))
        return 0

    lax.fori_loop(0, cb // SUB, column_step, 0)


def defect_kernel(meta, lo, n, group, amplitude, *refs):
    pieces, rows_dev, cb, senders, own_rows = meta
    n_in = len(pieces)
    sources, weights = refs[:2]
    ins = refs[2 : 2 + n_in]
    prev = refs[2 + n_in] if lo else None
    out, sums, grid = refs[-3:]
    me = lax.axis_index("src")
    for ref, (kind, k, first, count, skip) in zip(ins, pieces, strict=True):
        t = me ^ k
        low = t < senders // 2
        if kind == "below":
            row = 0
        elif kind == "above":
            row = rows_dev + 1
        elif kind == "outer":
            row = 1 + t * own_rows + jnp.where(low, 0, own_rows - 1)
        else:
            row = 1 + t * own_rows + kind + jnp.where(low, 1, 0)

        def move(i, _, ref=ref, row=row, first=first, skip=skip):
            for u in range(cb // SUB):
                to = pl.multiple_of(PAD + (first - lo + i) * cb + u * SUB, SUB)
                grid[row, pl.ds(to, SUB), :] = ref[pl.ds(pl.multiple_of((skip + i) * cb + u * SUB, SUB), SUB), :]
            return 0

        lax.fori_loop(0, count, move, 0)
    zero = jnp.zeros((SUB, LANES), jnp.float32)
    for row in range(rows_dev + 2):
        grid[row, pl.ds(0, PAD), :] = zero
        grid[row, pl.ds(PAD + n * cb, PAD), :] = zero
    if lo:
        sums[...] = prev[...]
    else:
        sums[...] = jnp.zeros(sums.shape, jnp.float32)
    lane = lax.broadcasted_iota(jnp.int32, (SUB, LANES), 1)
    index = lax.broadcasted_iota(jnp.int32, (SUB, LANES), 0) * LANES + lane
    first_lane, last_lane = lane == 0, lane == LANES - 1
    width = cb * LANES
    start = lax.axis_index("vtx") * rows_dev * width

    def source_step(i, _):
        source = sources[me * group + lo + i] - start

        def column_step(q, total):
            base = pl.multiple_of(PAD + i * cb + q * SUB, SUB)
            at = pl.ds(pl.multiple_of(q * SUB, SUB), SUB)
            here, right, left = [], [], []
            for row in range(rows_dev + 2):
                value = grid[row, pl.ds(base, SUB), :]
                here.append(value)
                after = grid[row, pl.ds(base + 1, SUB), :] if row else None
                right.append(pltpu.roll(jnp.where(first_lane, after, value), LANES - 1, 1) if row else None)
                if row <= rows_dev:
                    before = grid[row, pl.ds(base - 1, SUB), :]
                    left.append(pltpu.roll(jnp.where(last_lane, before, value), 1, 1))
            for row in range(rows_dev):
                c = [weights[w, row, at, :] for w in range(7)]
                value = c[0] * here[row + 1] - c[1] * right[row + 1] - c[2] * left[row + 1]
                value = value - c[3] * here[row + 2] - c[4] * here[row]
                value = value - c[5] * right[row + 2] - c[6] * left[row]
                spot = source - row * width - q * SUB * LANES
                value = value - jnp.where(index == spot, amplitude, 0.0)
                out[pl.ds((i * cb + q * SUB) * rows_dev + row, SUB, stride=rows_dev), :] = value
                total = total + value * value
            return total

        total = lax.fori_loop(0, cb // SUB, column_step, zero, unroll=math.gcd(cb // SUB, 8))
        sums[pl.ds(lo + i, 1), :] = jnp.sum(total, axis=0, keepdims=True)
        return 0

    lax.fori_loop(0, n, source_step, 0)


def scale_kernel(chunks, size, *refs):
    mine, other, parts, out, norms, buf, out_sem = refs[0], refs[1], refs[2:-4], *refs[-4:]
    group, per = mine.shape[0], out.shape[0] // mine.shape[0]
    sums = jnp.sum(mine[...] + other[...], axis=1, keepdims=True)
    norm = jnp.sqrt(sums / size + 1e-06)
    lane = lax.broadcasted_iota(jnp.int32, (group, LANES), 1)
    sub = lax.broadcasted_iota(jnp.int32, (group, LANES), 0)
    spread = jnp.where(lane == sub, jnp.broadcast_to(norm, (group, LANES)), 0.0)
    norms[...] = jnp.sum(spread, axis=0, keepdims=True)[:, :group]
    inverse = jnp.broadcast_to(1.0 / norm, (group, LANES))
    writes = []
    for i in range(group):
        part, (lo, n) = [(p, c) for p, c in zip(parts, chunks, strict=True) if c[0] <= i < sum(c)][0]
        factor = jnp.broadcast_to(inverse[i : i + 1], (SUB, LANES))

        def step(j, _, i=i, lo=lo, part=part, factor=factor):
            for u in range(8):
                at = (j * 8 + u) * SUB
                to = pl.ds(pl.multiple_of(i * per + at, SUB), SUB)
                buf[to, :] = part[pl.ds(pl.multiple_of((i - lo) * per + at, SUB), SUB), :] * factor
            return 0

        lax.fori_loop(0, per // (SUB * 8), step, 0)
        spot = pl.ds(i * per, per)
        writes.append(pltpu.make_async_copy(buf.at[spot, :], out.at[spot, :], out_sem.at[i]))
        writes[-1].start()
    for write in writes:
        write.wait()


def program(heat, cotan, source_index):
    peers, senders = lax.axis_size("vtx"), lax.axis_size("src")
    all_sources, own_rows, width = heat.shape
    rows_dev = cotan.shape[1]
    total_rows = rows_dev * peers
    group = all_sources // senders
    cb = width // LANES
    amplitude = math.sqrt(total_rows * width) / 8.0
    me = lax.axis_index("src")
    view = heat.reshape(all_sources, own_rows, cb, LANES).transpose(0, 2, 1, 3).reshape(-1, LANES)
    outer_rows = (0, own_rows - 1)
    order = [k for k in range(1, senders) if k >= 2] + [1]
    halves = [(0, group // 2), (group // 2, group - group // 2)]
    chunks = [(0, group - group // 4), (group - group // 4, group // 4)]
    common = (group, cb, own_rows, senders)

    def send(k, piece):
        return lax.ppermute(piece, "src", [(i, i ^ k) for i in range(senders)]) if k else piece

    first_wanted = [(k, outer_rows, *halves[0]) for k in order[:-1]]
    wanted = [(k, outer_rows, *halves[1]) for k in order]
    wanted += [(k, outer_rows, *halves[0]) for k in (1, 0)] + [(0, outer_rows, *halves[1])]
    wanted += [(k, (1 + j, j), *chunk) for chunk in chunks for j in range(own_rows - 1) for k in order + [0]]
    packed = pack(view, first_wanted, [(k, *halves[0]) for k in order[:-1]], *common, 60)
    table = dict(zip(first_wanted, packed, strict=True))
    packed = pack(view, wanted, [(k, *half) for half in reversed(halves) for k in order + [0]], *common, 16)
    table.update(zip(wanted, packed, strict=True))
    for key, piece in table.items():
        table[key] = send(key[0], piece)
    outer = [{k: table[k, outer_rows, *half] for k in range(senders)} for half in halves]
    inner = [
        [{k: table[k, (1 + j, j), *chunk] for k in range(senders)} for j in range(own_rows - 1)] for chunk in chunks
    ]
    up = [(i, i + 1) for i in range(peers - 1)]
    down = [(j, i) for i, j in up]
    vmem = pl.BlockSpec(memory_space=pltpu.VMEM)
    smem = pl.BlockSpec(memory_space=pltpu.SMEM)
    per = cb * rows_dev
    lower = lax.ppermute(cotan[2:4, rows_dev - 1].reshape(2 * cb, LANES), "vtx", up)
    tiles = cotan.reshape(4, rows_dev, cb, LANES).transpose(0, 2, 1, 3).reshape(4 * per, LANES)
    weights = pl.pallas_call(
        functools.partial(weights_kernel, (rows_dev, cb, total_rows)),
        out_shape=jax.ShapeDtypeStruct((7, rows_dev, cb + PAD, LANES), jnp.float32),
        in_specs=[vmem, vmem],
        out_specs=vmem,
        compiler_params=pltpu.CompilerParams(vmem_limit_bytes=8 << 20),
        cost_estimate=pl.CostEstimate(flops=20 * per * LANES, bytes_accessed=44 * per * LANES, transcendentals=0),
        name="weights",
    )(tiles, lower)
    below, above = [], []
    for got in outer:
        first = lax.select_n(me, *[got[k] for k in range(senders)])
        last = lax.select_n(me, *[got[k] for k in reversed(range(senders))])
        above.append(lax.ppermute(first, "vtx", down))
        below.append(lax.ppermute(last, "vtx", up))

    parts, sums = [], None
    for c, (lo, n) in enumerate(chunks):
        pieces, ins = [], []

        def take(kind, k, first, count, array):
            begin, end = max(first, lo), min(first + count, lo + n)
            if begin < end:
                pieces.append((kind, k, begin, end - begin, begin - first))
                ins.append(array)

        for half, got, b, a in zip(halves, outer, below, above, strict=True):
            for k in range(senders):
                take("outer", k, *half, got[k])
            take("below", 0, *half, b)
            take("above", 0, *half, a)
        for j in range(own_rows - 1):
            for k in range(senders):
                take(j, k, lo, n, inner[c][j][k])
        meta = (tuple(pieces), rows_dev, cb, senders, own_rows)
        part, sums = pl.pallas_call(
            functools.partial(defect_kernel, meta, lo, n, group, amplitude),
            out_shape=(
                jax.ShapeDtypeStruct((n * per, LANES), jnp.float32),
                jax.ShapeDtypeStruct((group, LANES), jnp.float32),
            ),
            in_specs=[smem, vmem] + [vmem] * len(ins) + ([vmem] if lo else []),
            out_specs=(vmem, vmem),
            scratch_shapes=[
                pltpu.VMEM((rows_dev + 2, n * cb + PAD + TAIL, LANES), jnp.float32),
            ],
            cost_estimate=pl.CostEstimate(flops=20 * n * per * LANES, bytes_accessed=8 * n * per * LANES, transcendentals=0),
            compiler_params=pltpu.CompilerParams(vmem_limit_bytes=24 << 20),
            name="defect",
        )(source_index, weights, *ins, *([sums] if lo else []))
        parts.append(part)
    step, other = 1, None
    while step < peers:
        sums = sums if other is None else sums + other
        other = lax.ppermute(sums, "vtx", [(i, i ^ step) for i in range(peers)])
        step *= 2
    out, norms = pl.pallas_call(
        functools.partial(scale_kernel, chunks, float(total_rows * width)),
        out_shape=(
            jax.ShapeDtypeStruct((group * per, LANES), jnp.float32),
            jax.ShapeDtypeStruct((1, group), jnp.float32),
        ),
        in_specs=[vmem, vmem] + [vmem] * len(parts),
        out_specs=(pl.BlockSpec(memory_space=pltpu.HBM), vmem),
        scratch_shapes=[
            pltpu.VMEM((group * per, LANES), jnp.float32),
            pltpu.SemaphoreType.DMA((group,)),
        ],
        cost_estimate=pl.CostEstimate(flops=group * per * LANES, bytes_accessed=8 * group * per * LANES, transcendentals=0),
        compiler_params=pltpu.CompilerParams(vmem_limit_bytes=12 << 20),
        name="scale",
    )(sums, other, *parts)
    out = out.reshape(group, cb, rows_dev, LANES).transpose(0, 2, 1, 3).reshape(group, rows_dev, width)
    return out, norms.reshape(group)


def solution(mesh):
    return jax.shard_map(
        program,
        mesh=mesh,
        in_specs=(P(None, ("vtx", "src"), None), P(None, "vtx", None), P()),
        out_specs=(P("src", "vtx", None), P("src")),
        check_vma=False,
    )
```

profile of v0, /device:TPU:0, one launch (start us, length us, event | category | flops | bytes accessed | tf_op | source)
XLA Modules:
  0.0 79.9 jit_solution(14405858365438635300)
XLA Ops:
  0.6 0.0 copy-start.1
  0.6 2.2 %shard_map.51 = (f32[512,128]{1,0:T(8,128)}, f32[512,128]{1,0:T(8,128)}) custom-call(f32[8192,128]{1,0:T(8,128)} %bitcast.17), custom_call_target="tpu_custom_call" | custom-call | flops 131072 | bytes 1572864 | tf_op jit(solution)/shard_map/pallas_call | solution.py:60
  2.8 3.1 %collective-permute-start.10 = (f32[512,128]{1,0:T(8,128)}, f32[512,128]{1,0:T(8,128)S(1)}, u32[]{:S(2)}, u32[]{:S(2)}) collective-permute-start(f32[512,128]{1,0:T(8,128)} %get-tuple-element.34), channel_id=1, source_target_pairs={{0,2},{1,3},{2,0},{3,1},{4,6},{5,7},{6,4},{7,5},{8,10},{9,11},{10,... | collective-permute-start | bytes 786440 | tf_op jit(solution)/shard_map/ppermute | solution.py:235
  5.9 0.0 collective-permute-start.11
  5.9 0.0 copy-start
  5.9 2.2 %copy-done = f32[64,2,8192]{2,1,0:T(2,128)S(1)} copy-done((f32[64,2,8192]{2,1,0:T(2,128)S(1)}, f32[64,2,8192]{2,1,0:T(2,128)}, u32[]{:S(2)}) %copy-start) | copy-done | bytes 4194328
  8.1 2.0 %shard_map.50 = (f32[512,128]{1,0:T(8,128)S(1)}, f32[512,128]{1,0:T(8,128)S(1)}, f32[512,128]{1,0:T(8,128)}, f32[512,128]{1,0:T(8,128)}, f32[512,128]{1,0:T(8,12...) custom-call(f32[8192,128]{1,0:T(8,128)S(1)} %bitcast.18), custom_call_target="tpu_custom_call" | custom-call | flops 917504 | bytes 7864320 | tf_op jit(solution)/shard_map/pallas_call | solution.py:60
  10.1 0.0 copy-start.3
  10.1 0.7 copy-done.3
  10.8 0.0 copy-start.4
  10.8 0.7 copy-done.4
  11.6 0.0 copy-start.5
  11.6 0.7 copy-done.5
  12.3 0.7 copy-done.6
  13.0 0.7 copy-done.8
  13.7 0.7 copy-done.9
  14.3 0.2 collective-permute-start.9
  14.5 0.0 copy-done.1
  14.5 0.1 slice.3
  14.6 3.8 %collective-permute-start = (f32[128,128]{1,0:T(8,128)S(1)}, f32[128,128]{1,0:T(8,128)S(1)}, u32[]{:S(2)}, u32[]{:S(2)}) collective-permute-start(f32[128,128]{1,0:T(8,128)S(1)} %bitcast.20), channel_id=1, source_target_pairs={{0,4},{4,8},{8,12},{12,16},{16,20},{20,24},{24,28},{1,5},{5,9},{9,... | collective-permute-start | bytes 196616 | tf_op jit(solution)/shard_map/ppermute | solution.py:256
  18.4 0.0 copy-done.7
  18.4 0.1 collective-permute-start.1
  18.5 1.8 %collective-permute-done.lower = f32[128,128]{1,0:T(8,128)S(1)} collective-permute-done((f32[128,128]{1,0:T(8,128)S(1)}, f32[128,128]{1,0:T(8,128)S(1)}, u32[]{:S(2)}, u32[]{:S(2)}) %collective-permute-start) | collective-permute-done | bytes 65568 | tf_op jit(solution)/shard_map/ppermute | solution.py:256
  20.3 1.5 %collective-permute-start.2 = (f32[512,128]{1,0:T(8,128)}, f32[512,128]{1,0:T(8,128)S(1)}, u32[]{:S(2)}, u32[]{:S(2)}) collective-permute-start(f32[512,128]{1,0:T(8,128)} %copy-done.6), channel_id=1, source_target_pairs={{0,2},{1,3},{2,0},{3,1},{4,6},{5,7},{6,4},{7,5},{8,10},{9,11},{10,... | collective-permute-start | bytes 786440 | tf_op jit(solution)/shard_map/ppermute | solution.py:235
  21.8 0.0 collective-permute-done.10.refs_4_
  21.8 0.0 collective-permute-start.3
  21.8 0.0 collective-permute-done.11.refs_5_
  21.8 0.6 collective-permute-start.14
  22.4 0.0 collective-permute-done.9.refs_3_
  22.4 1.5 %collective-permute-start.15 = (f32[768,128]{1,0:T(8,128)}, f32[768,128]{1,0:T(8,128)S(1)}, u32[]{:S(2)}, u32[]{:S(2)}) collective-permute-start(f32[768,128]{1,0:T(8,128)} %copy-done.4), channel_id=1, source_target_pairs={{0,2},{1,3},{2,0},{3,1},{4,6},{5,7},{6,4},{7,5},{8,10},{9,11},{10,... | collective-permute-start | bytes 1179656 | tf_op jit(solution)/shard_map/ppermute | solution.py:235
  24.0 0.1 select_select_fusion
  24.0 0.0 collective-permute-done.1.refs_9_.refs_3_
  24.0 0.1 collective-permute-start.16
  24.1 5.6 %collective-permute-done.2.refs_10_.refs_4_ = f32[512,128]{1,0:T(8,128)S(1)} collective-permute-done((f32[512,128]{1,0:T(8,128)}, f32[512,128]{1,0:T(8,128)S(1)}, u32[]{:S(2)}, u32[]{:S(2)}) %collective-permute-start.2) | collective-permute-done | bytes 262176 | tf_op jit(solution)/shard_map/ppermute | solution.py:235
  29.7 1.3 %collective-permute-start.13 = (f32[512,128]{1,0:T(8,128)S(1)}, f32[512,128]{1,0:T(8,128)S(1)}, u32[]{:S(2)}, u32[]{:S(2)}) collective-permute-start(f32[512,128]{1,0:T(8,128)S(1)} %get-tuple-element.46), channel_id=1, source_target_pairs={{4,0},{8,4},{12,8},{16,12},{20,16},{24,20},{28,24},{5,1},{9,5},{13... | collective-permute-start | bytes 786440 | tf_op jit(solution)/shard_map/ppermute | solution.py:271
  31.0 3.4 %collective-permute-done.3.refs_11_.refs_5_ = f32[512,128]{1,0:T(8,128)S(1)} collective-permute-done((f32[512,128]{1,0:T(8,128)S(1)}, f32[512,128]{1,0:T(8,128)S(1)}, u32[]{:S(2)}, u32[]{:S(2)}) %collective-permute-start.3) | collective-permute-done | bytes 262176 | tf_op jit(solution)/shard_map/ppermute | solution.py:235
  34.3 4.3 %collective-permute-start.12 = (f32[512,128]{1,0:T(8,128)S(1)}, f32[512,128]{1,0:T(8,128)S(1)}, u32[]{:S(2)}, u32[]{:S(2)}) collective-permute-start(f32[512,128]{1,0:T(8,128)S(1)} %get-tuple-element.47), channel_id=1, source_target_pairs={{0,4},{4,8},{8,12},{12,16},{16,20},{20,24},{24,28},{1,5},{5,9},{9,... | collective-permute-start | bytes 786440 | tf_op jit(solution)/shard_map/ppermute | solution.py:272
  38.6 0.1 select_select_fusion.2
  38.7 0.0 collective-permute-done.14.refs_15_
  38.7 1.3 %collective-permute-start.5 = (f32[512,128]{1,0:T(8,128)S(1)}, f32[512,128]{1,0:T(8,128)S(1)}, u32[]{:S(2)}, u32[]{:S(2)}) collective-permute-start(f32[512,128]{1,0:T(8,128)S(1)} %get-tuple-element.48), channel_id=1, source_target_pairs={{4,0},{8,4},{12,8},{16,12},{20,16},{24,20},{28,24},{5,1},{9,5},{13... | collective-permute-start | bytes 786440 | tf_op jit(solution)/shard_map/ppermute | solution.py:271
  40.0 3.7 %collective-permute-done.15.refs_16_ = f32[768,128]{1,0:T(8,128)S(1)} collective-permute-done((f32[768,128]{1,0:T(8,128)}, f32[768,128]{1,0:T(8,128)S(1)}, u32[]{:S(2)}, u32[]{:S(2)}) %collective-permute-start.15) | collective-permute-done | bytes 393248 | tf_op jit(solution)/shard_map/ppermute | solution.py:235
  43.7 4.3 %collective-permute-start.4 = (f32[512,128]{1,0:T(8,128)S(1)}, f32[512,128]{1,0:T(8,128)S(1)}, u32[]{:S(2)}, u32[]{:S(2)}) collective-permute-start(f32[512,128]{1,0:T(8,128)S(1)} %get-tuple-element.49), channel_id=1, source_target_pairs={{0,4},{4,8},{8,12},{12,16},{16,20},{20,24},{24,28},{1,5},{5,9},{9,... | collective-permute-start | bytes 786440 | tf_op jit(solution)/shard_map/ppermute | solution.py:272
  48.0 1.5 %collective-permute-done.16.refs_17_ = f32[768,128]{1,0:T(8,128)S(1)} collective-permute-done((f32[768,128]{1,0:T(8,128)}, f32[768,128]{1,0:T(8,128)S(1)}, u32[]{:S(2)}, u32[]{:S(2)}) %collective-permute-start.16) | collective-permute-done | bytes 393248 | tf_op jit(solution)/shard_map/ppermute | solution.py:235
  49.5 0.7 collective-permute-start.6
  50.2 0.0 collective-permute-done.13.refs_7_
  50.2 1.5 %collective-permute-start.7 = (f32[256,128]{1,0:T(8,128)}, f32[256,128]{1,0:T(8,128)S(1)}, u32[]{:S(2)}, u32[]{:S(2)}) collective-permute-start(f32[256,128]{1,0:T(8,128)} %copy-done.8), channel_id=1, source_target_pairs={{0,2},{1,3},{2,0},{3,1},{4,6},{5,7},{6,4},{7,5},{8,10},{9,11},{10,... | collective-permute-start | bytes 393224 | tf_op jit(solution)/shard_map/ppermute | solution.py:235
  51.7 0.0 collective-permute-done.12.refs_6_
  51.7 0.0 collective-permute-start.8
  51.7 0.7 weights.1.refs_1_
  52.4 0.0 collective-permute-done.5.refs_13_.refs_7_
  52.4 3.9 %collective-permute-done.4.refs_12_.refs_6_ = f32[512,128]{1,0:T(8,128)S(1)} collective-permute-done((f32[512,128]{1,0:T(8,128)S(1)}, f32[512,128]{1,0:T(8,128)S(1)}, u32[]{:S(2)}, u32[]{:S(2)}) %collective-permute-start.4) | collective-permute-done | bytes 262176 | tf_op jit(solution)/shard_map/ppermute | solution.py:272
  56.3 0.0 copy-done.2
  56.3 4.4 %defect.2 = (f32[6144,128]{1,0:T(8,128)S(1)}, f32[16,128]{1,0:T(8,128)S(1)}) custom-call(s32[64]{0:T(128)S(1)} %copy-done.2, f32[7,8,72,128]{3,2,1,0:T(8,128)S(1)} %weights.1.refs_1_, f32[512,128]{1,0:T(8,128)S(1)} %get-tuple-element.32.refs_2_, f32[512,128]{1,0:T(8,128)S(1)} %collective-permute-done.9.refs_3_, ...), custom_call_target="tpu_custom_call" | custom-call | flops 15728640 | bytes 6291456 | tf_op jit(solution)/shard_map/defect/pallas_call | solution.py:293
  60.7 0.0 collective-permute-done.6.refs_9_
  60.7 0.0 collective-permute-done.7.refs_10_
  60.7 0.0 collective-permute-done.8.refs_11_
  60.7 1.8 %defect.3 = (f32[2048,128]{1,0:T(8,128)S(1)}, f32[16,128]{1,0:T(8,128)S(1)}) custom-call(s32[64]{0:T(128)S(1)} %copy-done.2, f32[7,8,72,128]{3,2,1,0:T(8,128)S(1)} %weights.1.refs_1_, f32[512,128]{1,0:T(8,128)S(1)} %get-tuple-element.24.refs_8_.refs_2_, f32[512,128]{1,0:T(8,128)S(1)} %collective-permute-done.1.refs_9_.refs_3_, ...), custom_call_target="tpu_custom_call" | custom-call | flops 5242880 | bytes 2097152 | tf_op jit(solution)/shard_map/defect/pallas_call | solution.py:293
  62.6 2.5 %collective-permute-start.17 = (f32[16,128]{1,0:T(8,128)S(1)}, f32[16,128]{1,0:T(8,128)S(1)}, u32[]{:S(2)}, u32[]{:S(2)}) collective-permute-start(f32[16,128]{1,0:T(8,128)S(1)} %get-tuple-element.41), channel_id=1, source_target_pairs={{0,4},{4,0},{8,12},{12,8},{16,20},{20,16},{24,28},{28,24},{1,5},{5... | collective-permute-start | bytes 24584 | tf_op jit(solution)/shard_map/ppermute | solution.py:312
  65.1 1.6 %collective-permute-done.17 = f32[16,128]{1,0:T(8,128)S(1)} collective-permute-done((f32[16,128]{1,0:T(8,128)S(1)}, f32[16,128]{1,0:T(8,128)S(1)}, u32[]{:S(2)}, u32[]{:S(2)}) %collective-permute-start.17) | collective-permute-done | bytes 8224 | tf_op jit(solution)/shard_map/ppermute | solution.py:312
  66.8 4.1 %collective-permute-start.18 = (f32[16,128]{1,0:T(8,128)S(1)}, f32[16,128]{1,0:T(8,128)S(1)}, u32[]{:S(2)}, u32[]{:S(2)}) collective-permute-start(f32[16,128]{1,0:T(8,128)S(1)} %add.6), channel_id=1, source_target_pairs={{0,8},{4,12},{8,0},{12,4},{16,24},{20,28},{24,16},{28,20},{1,9},{5... | collective-permute-start | bytes 24584 | tf_op jit(solution)/shard_map/ppermute | solution.py:312
  70.8 1.6 %collective-permute-done.18 = f32[16,128]{1,0:T(8,128)S(1)} collective-permute-done((f32[16,128]{1,0:T(8,128)S(1)}, f32[16,128]{1,0:T(8,128)S(1)}, u32[]{:S(2)}, u32[]{:S(2)}) %collective-permute-start.18) | collective-permute-done | bytes 8224 | tf_op jit(solution)/shard_map/ppermute | solution.py:312
  72.5 3.0 %collective-permute-start.19 = (f32[16,128]{1,0:T(8,128)S(1)}, f32[16,128]{1,0:T(8,128)S(1)}, u32[]{:S(2)}, u32[]{:S(2)}) collective-permute-start(f32[16,128]{1,0:T(8,128)S(1)} %add.7.refs_0_), channel_id=1, source_target_pairs={{0,16},{4,20},{8,24},{12,28},{16,0},{20,4},{24,8},{28,12},{1,17},{... | collective-permute-start | bytes 24584 | tf_op jit(solution)/shard_map/ppermute | solution.py:312
  75.5 1.6 %collective-permute-done.19.refs_1_ = f32[16,128]{1,0:T(8,128)S(1)} collective-permute-done((f32[16,128]{1,0:T(8,128)S(1)}, f32[16,128]{1,0:T(8,128)S(1)}, u32[]{:S(2)}, u32[]{:S(2)}) %collective-permute-start.19) | collective-permute-done | bytes 8224 | tf_op jit(solution)/shard_map/ppermute | solution.py:312
  77.1 2.8 %scale.1 = (f32[8192,128]{1,0:T(8,128)}, f32[1,16]{1,0:T(1,128)}) custom-call(f32[16,128]{1,0:T(8,128)S(1)} %add.7.refs_0_, f32[16,128]{1,0:T(8,128)S(1)} %collective-permute-done.19.refs_1_, f32[6144,128]{1,0:T(8,128)S(1)} %get-tuple-element.42.refs_2_, f32[2048,128]{1,0:T(8,128)S(1)} %get-tuple-element.43.refs_3_), custom_call_target="tpu_custom_call" | custom-call | flops 1048576 | bytes 8388608 | tf_op jit(solution)/shard_map/scale/pallas_call | solution.py:314
  (7 shorter events, 0.0 us)
Async XLA Ops:
  0.6 13.9 %copy-start.1 = (f32[4,8,8192]{2,1,0:T(8,128)S(1)}, f32[4,8,8192]{2,1,0:T(8,128)}, u32[]{:S(2)}) copy-start(f32[4,8,8192]{2,1,0:T(8,128)} %param.4) | copy-start | bytes 3145732
  2.8 19.0 %collective-permute-start.10 = (f32[512,128]{1,0:T(8,128)}, f32[512,128]{1,0:T(8,128)S(1)}, u32[]{:S(2)}, u32[]{:S(2)}) collective-permute-start(f32[512,128]{1,0:T(8,128)} %get-tuple-element.34), channel_id=1, source_target_pairs={{0,2},{1,3},{2,0},{3,1},{4,6},{5,7},{6,4},{7,5},{8,10},{9,11},{10,... | collective-permute-start | bytes 786440 | tf_op jit(solution)/shard_map/ppermute | solution.py:235
  5.9 15.9 %collective-permute-start.11 = (f32[512,128]{1,0:T(8,128)}, f32[512,128]{1,0:T(8,128)S(1)}, u32[]{:S(2)}, u32[]{:S(2)}) collective-permute-start(f32[512,128]{1,0:T(8,128)} %get-tuple-element.35), channel_id=1, source_target_pairs={{0,3},{1,2},{2,1},{3,0},{4,7},{5,6},{6,5},{7,4},{8,11},{9,10},{10,... | collective-permute-start | bytes 786440 | tf_op jit(solution)/shard_map/ppermute | solution.py:235
  5.9 2.2 %copy-start = (f32[64,2,8192]{2,1,0:T(2,128)S(1)}, f32[64,2,8192]{2,1,0:T(2,128)}, u32[]{:S(2)}) copy-start(f32[64,2,8192]{2,1,0:T(2,128)} %param.3) | copy-start | bytes 12582916
  10.1 0.7 copy-start.3
  10.8 0.7 copy-start.4
  11.6 0.7 copy-start.5
  12.3 0.7 copy-start.6
  13.0 0.7 copy-start.8
  13.7 0.7 copy-start.9
  14.3 4.1 %copy-start.7 = (f32[256,128]{1,0:T(8,128)}, f32[256,128]{1,0:T(8,128)S(1)}, u32[]{:S(2)}) copy-start(f32[256,128]{1,0:T(8,128)S(1)} %get-tuple-element.31) | copy-start | bytes 393220
  14.3 42.0 %copy-start.2 = (s32[64]{0:T(128)S(1)}, s32[64]{0:T(128)}, u32[]{:S(2)}) copy-start(s32[64]{0:T(128)} %refs_0_.3) | copy-start | bytes 772
  14.3 8.1 %collective-permute-start.9 = (f32[512,128]{1,0:T(8,128)}, f32[512,128]{1,0:T(8,128)S(1)}, u32[]{:S(2)}, u32[]{:S(2)}) collective-permute-start(f32[512,128]{1,0:T(8,128)} %get-tuple-element.33), channel_id=1, source_target_pairs={{0,1},{1,0},{2,3},{3,2},{4,5},{5,4},{6,7},{7,6},{8,9},{9,8},{10,11... | collective-permute-start | bytes 786440 | tf_op jit(solution)/shard_map/ppermute | solution.py:235
  14.6 5.7 %collective-permute-start = (f32[128,128]{1,0:T(8,128)S(1)}, f32[128,128]{1,0:T(8,128)S(1)}, u32[]{:S(2)}, u32[]{:S(2)}) collective-permute-start(f32[128,128]{1,0:T(8,128)S(1)} %bitcast.20), channel_id=1, source_target_pairs={{0,4},{4,8},{8,12},{12,16},{16,20},{20,24},{24,28},{1,5},{5,9},{9,... | collective-permute-start | bytes 196616 | tf_op jit(solution)/shard_map/ppermute | solution.py:256
  18.4 5.6 %collective-permute-start.1 = (f32[512,128]{1,0:T(8,128)}, f32[512,128]{1,0:T(8,128)S(1)}, u32[]{:S(2)}, u32[]{:S(2)}) collective-permute-start(f32[512,128]{1,0:T(8,128)} %get-tuple-element.25), channel_id=1, source_target_pairs={{0,1},{1,0},{2,3},{3,2},{4,5},{5,4},{6,7},{7,6},{8,9},{9,8},{10,11... | collective-permute-start | bytes 786440 | tf_op jit(solution)/shard_map/ppermute | solution.py:235
  20.3 9.4 %collective-permute-start.2 = (f32[512,128]{1,0:T(8,128)}, f32[512,128]{1,0:T(8,128)S(1)}, u32[]{:S(2)}, u32[]{:S(2)}) collective-permute-start(f32[512,128]{1,0:T(8,128)} %copy-done.6), channel_id=1, source_target_pairs={{0,2},{1,3},{2,0},{3,1},{4,6},{5,7},{6,4},{7,5},{8,10},{9,11},{10,... | collective-permute-start | bytes 786440 | tf_op jit(solution)/shard_map/ppermute | solution.py:235
  21.8 12.5 %collective-permute-start.3 = (f32[512,128]{1,0:T(8,128)S(1)}, f32[512,128]{1,0:T(8,128)S(1)}, u32[]{:S(2)}, u32[]{:S(2)}) collective-permute-start(f32[512,128]{1,0:T(8,128)S(1)} %get-tuple-element.27), channel_id=1, source_target_pairs={{0,3},{1,2},{2,1},{3,0},{4,7},{5,6},{6,5},{7,4},{8,11},{9,10},{10,... | collective-permute-start | bytes 786440 | tf_op jit(solution)/shard_map/ppermute | solution.py:235
  21.8 16.9 %collective-permute-start.14 = (f32[768,128]{1,0:T(8,128)}, f32[768,128]{1,0:T(8,128)S(1)}, u32[]{:S(2)}, u32[]{:S(2)}) collective-permute-start(f32[768,128]{1,0:T(8,128)} %copy-done.5), channel_id=1, source_target_pairs={{0,1},{1,0},{2,3},{3,2},{4,5},{5,4},{6,7},{7,6},{8,9},{9,8},{10,11... | collective-permute-start | bytes 1179656 | tf_op jit(solution)/shard_map/ppermute | solution.py:235
  22.4 21.3 %collective-permute-start.15 = (f32[768,128]{1,0:T(8,128)}, f32[768,128]{1,0:T(8,128)S(1)}, u32[]{:S(2)}, u32[]{:S(2)}) collective-permute-start(f32[768,128]{1,0:T(8,128)} %copy-done.4), channel_id=1, source_target_pairs={{0,2},{1,3},{2,0},{3,1},{4,6},{5,7},{6,4},{7,5},{8,10},{9,11},{10,... | collective-permute-start | bytes 1179656 | tf_op jit(solution)/shard_map/ppermute | solution.py:235
  24.0 25.4 %collective-permute-start.16 = (f32[768,128]{1,0:T(8,128)}, f32[768,128]{1,0:T(8,128)S(1)}, u32[]{:S(2)}, u32[]{:S(2)}) collective-permute-start(f32[768,128]{1,0:T(8,128)} %copy-done.3), channel_id=1, source_target_pairs={{0,3},{1,2},{2,1},{3,0},{4,7},{5,6},{6,5},{7,4},{8,11},{9,10},{10,... | collective-permute-start | bytes 1179656 | tf_op jit(solution)/shard_map/ppermute | solution.py:235
  29.7 20.5 %collective-permute-start.13 = (f32[512,128]{1,0:T(8,128)S(1)}, f32[512,128]{1,0:T(8,128)S(1)}, u32[]{:S(2)}, u32[]{:S(2)}) collective-permute-start(f32[512,128]{1,0:T(8,128)S(1)} %get-tuple-element.46), channel_id=1, source_target_pairs={{4,0},{8,4},{12,8},{16,12},{20,16},{24,20},{28,24},{5,1},{9,5},{13... | collective-permute-start | bytes 786440 | tf_op jit(solution)/shard_map/ppermute | solution.py:271
  34.3 17.4 %collective-permute-start.12 = (f32[512,128]{1,0:T(8,128)S(1)}, f32[512,128]{1,0:T(8,128)S(1)}, u32[]{:S(2)}, u32[]{:S(2)}) collective-permute-start(f32[512,128]{1,0:T(8,128)S(1)} %get-tuple-element.47), channel_id=1, source_target_pairs={{0,4},{4,8},{8,12},{12,16},{16,20},{20,24},{24,28},{1,5},{5,9},{9,... | collective-permute-start | bytes 786440 | tf_op jit(solution)/shard_map/ppermute | solution.py:272
  38.7 13.7 %collective-permute-start.5 = (f32[512,128]{1,0:T(8,128)S(1)}, f32[512,128]{1,0:T(8,128)S(1)}, u32[]{:S(2)}, u32[]{:S(2)}) collective-permute-start(f32[512,128]{1,0:T(8,128)S(1)} %get-tuple-element.48), channel_id=1, source_target_pairs={{4,0},{8,4},{12,8},{16,12},{20,16},{24,20},{28,24},{5,1},{9,5},{13... | collective-permute-start | bytes 786440 | tf_op jit(solution)/shard_map/ppermute | solution.py:271
  43.7 12.6 %collective-permute-start.4 = (f32[512,128]{1,0:T(8,128)S(1)}, f32[512,128]{1,0:T(8,128)S(1)}, u32[]{:S(2)}, u32[]{:S(2)}) collective-permute-start(f32[512,128]{1,0:T(8,128)S(1)} %get-tuple-element.49), channel_id=1, source_target_pairs={{0,4},{4,8},{8,12},{12,16},{16,20},{20,24},{24,28},{1,5},{5,9},{9,... | collective-permute-start | bytes 786440 | tf_op jit(solution)/shard_map/ppermute | solution.py:272
  49.5 11.2 %collective-permute-start.6 = (f32[256,128]{1,0:T(8,128)}, f32[256,128]{1,0:T(8,128)S(1)}, u32[]{:S(2)}, u32[]{:S(2)}) collective-permute-start(f32[256,128]{1,0:T(8,128)} %copy-done.9), channel_id=1, source_target_pairs={{0,1},{1,0},{2,3},{3,2},{4,5},{5,4},{6,7},{7,6},{8,9},{9,8},{10,11... | collective-permute-start | bytes 393224 | tf_op jit(solution)/shard_map/ppermute | solution.py:235
  50.2 10.5 %collective-permute-start.7 = (f32[256,128]{1,0:T(8,128)}, f32[256,128]{1,0:T(8,128)S(1)}, u32[]{:S(2)}, u32[]{:S(2)}) collective-permute-start(f32[256,128]{1,0:T(8,128)} %copy-done.8), channel_id=1, source_target_pairs={{0,2},{1,3},{2,0},{3,1},{4,6},{5,7},{6,4},{7,5},{8,10},{9,11},{10,... | collective-permute-start | bytes 393224 | tf_op jit(solution)/shard_map/ppermute | solution.py:235
  51.7 9.0 %collective-permute-start.8 = (f32[256,128]{1,0:T(8,128)}, f32[256,128]{1,0:T(8,128)S(1)}, u32[]{:S(2)}, u32[]{:S(2)}) collective-permute-start(f32[256,128]{1,0:T(8,128)} %copy-done.7), channel_id=1, source_target_pairs={{0,3},{1,2},{2,1},{3,0},{4,7},{5,6},{6,5},{7,4},{8,11},{9,10},{10,... | collective-permute-start | bytes 393224 | tf_op jit(solution)/shard_map/ppermute | solution.py:235
  62.6 4.2 %collective-permute-start.17 = (f32[16,128]{1,0:T(8,128)S(1)}, f32[16,128]{1,0:T(8,128)S(1)}, u32[]{:S(2)}, u32[]{:S(2)}) collective-permute-start(f32[16,128]{1,0:T(8,128)S(1)} %get-tuple-element.41), channel_id=1, source_target_pairs={{0,4},{4,0},{8,12},{12,8},{16,20},{20,16},{24,28},{28,24},{1,5},{5... | collective-permute-start | bytes 24584 | tf_op jit(solution)/shard_map/ppermute | solution.py:312
  66.8 5.7 %collective-permute-start.18 = (f32[16,128]{1,0:T(8,128)S(1)}, f32[16,128]{1,0:T(8,128)S(1)}, u32[]{:S(2)}, u32[]{:S(2)}) collective-permute-start(f32[16,128]{1,0:T(8,128)S(1)} %add.6), channel_id=1, source_target_pairs={{0,8},{4,12},{8,0},{12,4},{16,24},{20,28},{24,16},{28,20},{1,9},{5... | collective-permute-start | bytes 24584 | tf_op jit(solution)/shard_map/ppermute | solution.py:312
  72.5 4.7 %collective-permute-start.19 = (f32[16,128]{1,0:T(8,128)S(1)}, f32[16,128]{1,0:T(8,128)S(1)}, u32[]{:S(2)}, u32[]{:S(2)}) collective-permute-start(f32[16,128]{1,0:T(8,128)S(1)} %add.7.refs_0_), channel_id=1, source_target_pairs={{0,16},{4,20},{8,24},{12,28},{16,0},{20,4},{24,8},{28,12},{1,17},{... | collective-permute-start | bytes 24584 | tf_op jit(solution)/shard_map/ppermute | solution.py:312
where the time goes:
time: 80.2 us; the launch traced here: 79.9 us
  starting transfers between devices  33.9 us (42%)
  waiting for transfers between devices  24.7 us (31%)
  Pallas kernels  13.9 us (17%)
  local copies, waits for them, and re-layouts  6.49 us (8%)
  between operations  0.83 us (1%)
    ppermute x12, waiting for transfers between devices, send(): lax.ppermute(piece, 'src', [(i, i ^ k) for i in range(senders)])  14.2 us
    ppermute x3, starting transfers between devices, program(): other = lax.ppermute(sums, 'vtx', [(i, i ^ step) for i in range(peers)])  9.67 us
    ppermute x12, starting transfers between devices, send(): lax.ppermute(piece, 'src', [(i, i ^ k) for i in range(senders)])  9.25 us
    ppermute x2, starting transfers between devices, program(): below.append(lax.ppermute(last, 'vtx', up))  8.54 us
    unnamed x20, local copies, waits for them, and re-layouts  6.43 us
    pallas_call x2, Pallas kernels, program(): pl.pallas_call(functools.partial(defect_kernel, meta, lo, n, group, ampli...  6.2 us
    ppermute x3, waiting for transfers between devices, program(): other = lax.ppermute(sums, 'vtx', [(i, i ^ step) for i in range(peers)])  4.89 us
    pallas_call x2, Pallas kernels, pack(): pl.pallas_call(functools.partial(pack_kernel, (tuple(plan), group, cb, ow...  4.16 us
  transfers between devices with their start and end apart: 20, of which 9 were waited for; matrix products, arithmetic and copies ran while one was open for 0% of the time, Pallas kernels for 9%

commit v1 on v0

--- a/solution.py
+++ b/solution.py
@@ -234,13 +234,14 @@
     def send(k, piece):
         return lax.ppermute(piece, "src", [(i, i ^ k) for i in range(senders)]) if k else piece
 
-    first_wanted = [(k, outer_rows, *halves[0]) for k in order[:-1]]
-    wanted = [(k, outer_rows, *halves[1]) for k in order]
-    wanted += [(k, outer_rows, *halves[0]) for k in (1, 0)] + [(0, outer_rows, *halves[1])]
+    wanted = [(k, outer_rows, *half) for half in halves for k in (1, 0)]
     wanted += [(k, (1 + j, j), *chunk) for chunk in chunks for j in range(own_rows - 1) for k in order + [0]]
-    packed = pack(view, first_wanted, [(k, *halves[0]) for k in order[:-1]], *common, 60)
-    table = dict(zip(first_wanted, packed, strict=True))
-    packed = pack(view, wanted, [(k, *half) for half in reversed(halves) for k in order + [0]], *common, 16)
+    table = {}
+    for half in halves:
+        early = [(k, outer_rows, *half) for k in order[:-1]]
+        packed = pack(view, early, [(k, *half) for k in order[:-1]], *common, 60)
+        table.update(zip(early, packed, strict=True))
+    packed = pack(view, wanted, [(k, *half) for half in halves for k in order + [0]], *common, 60)
     table.update(zip(wanted, packed, strict=True))
     for key, piece in table.items():
         table[key] = send(key[0], piece)

time: 80.2 us -> 80.5 us (level)
  local copies, waits for them, and re-layouts: 6.49 us -> 0.09 us
  Pallas kernels: 13.9 us -> 18.8 us
  waiting for transfers between devices: 24.7 us -> 29.4 us
  starting transfers between devices: 33.9 us -> 31 us
    unnamed x20 -> x14, local copies, waits for them, and re-layouts: 6.43 us -> 0.03 us
    ppermute x2, waiting for transfers between devices: 3.9 us -> 8.42 us  [program(): below.append(lax.ppermute(last, 'vtx', up))]
    pallas_call x2 -> x3, Pallas kernels: 4.16 us -> 8.15 us  [pack(): pl.pallas_call(functools.partial(pack_kernel, (tuple(plan), group, cb, ow...]
    ppermute x3, starting transfers between devices: 9.67 us -> 6.68 us  [program(): other = lax.ppermute(sums, 'vtx', [(i, i ^ step) for i in range(peers)])]
    ppermute x1, waiting for transfers between devices: 1.79 us -> 0.01 us  [program(): lax.ppermute(cotan[2:4, rows_dev - 1].reshape(2 * cb, LANES), 'vtx', up)]
    ppermute x12, waiting for transfers between devices: 14.2 us -> 15.3 us  [send(): lax.ppermute(piece, 'src', [(i, i ^ k) for i in range(senders)])]
    pallas_call x2, Pallas kernels: 6.2 us -> 7.11 us  [program(): pl.pallas_call(functools.partial(defect_kernel, meta, lo, n, group, ampli...]
  transfers between devices with their start and end apart: 20 -> 20, of which waited for: 9 -> 9; matrix products, arithmetic and copies ran while one was open for 0% -> 0% of each run, Pallas kernels for 9% -> 15%
where the time goes in v1:
time: 80.5 us; the launch traced here: 80.2 us
  starting transfers between devices  31 us (39%)
  waiting for transfers between devices  29.4 us (37%)
  Pallas kernels  18.8 us (23%)
  between operations  0.85 us (1%)
    ppermute x12, waiting for transfers between devices, send(): lax.ppermute(piece, 'src', [(i, i ^ k) for i in range(senders)])  15.3 us
    ppermute x12, starting transfers between devices, send(): lax.ppermute(piece, 'src', [(i, i ^ k) for i in range(senders)])  9.92 us
    ppermute x2, waiting for transfers between devices, program(): below.append(lax.ppermute(last, 'vtx', up))  8.42 us
    pallas_call x3, Pallas kernels, pack(): pl.pallas_call(functools.partial(pack_kernel, (tuple(plan), group, cb, ow...  8.15 us
    ppermute x2, starting transfers between devices, program(): below.append(lax.ppermute(last, 'vtx', up))  8.02 us
    pallas_call x2, Pallas kernels, program(): pl.pallas_call(functools.partial(defect_kernel, meta, lo, n, group, ampli...  7.11 us
    ppermute x3, starting transfers between devices, program(): other = lax.ppermute(sums, 'vtx', [(i, i ^ step) for i in range(peers)])  6.68 us
    ppermute x3, waiting for transfers between devices, program(): other = lax.ppermute(sums, 'vtx', [(i, i ^ step) for i in range(peers)])  5.67 us
  transfers between devices with their start and end apart: 20, of which 9 were waited for; matrix products, arithmetic and copies ran while one was open for 0% of the time, Pallas kernels for 15%

profile of v1, /device:TPU:0, one launch (start us, length us, event | category | flops | bytes accessed | tf_op | source)
XLA Modules:
  0.0 80.2 jit_solution(17536869131577817779)
XLA Ops:
  0.6 0.0 copy-start.1
  0.6 2.1 %shard_map.52 = (f32[512,128]{1,0:T(8,128)}, f32[512,128]{1,0:T(8,128)}) custom-call(f32[8192,128]{1,0:T(8,128)} %bitcast.18), custom_call_target="tpu_custom_call" | custom-call | flops 131072 | bytes 1572864 | tf_op jit(solution)/shard_map/pallas_call | solution.py:60
  2.8 3.1 %collective-permute-start.10 = (f32[512,128]{1,0:T(8,128)}, f32[512,128]{1,0:T(8,128)S(1)}, u32[]{:S(2)}, u32[]{:S(2)}) collective-permute-start(f32[512,128]{1,0:T(8,128)} %get-tuple-element.34), channel_id=1, source_target_pairs={{0,2},{1,3},{2,0},{3,1},{4,6},{5,7},{6,4},{7,5},{8,10},{9,11},{10,... | collective-permute-start | bytes 786440 | tf_op jit(solution)/shard_map/ppermute | solution.py:235
  5.9 0.0 collective-permute-start.11
  5.9 3.9 %shard_map.50 = (f32[512,128]{1,0:T(8,128)}, f32[512,128]{1,0:T(8,128)}, f32[512,128]{1,0:T(8,128)}, f32[512,128]{1,0:T(8,128)}, f32[768,128]{1,0:T(8,128)}, /*i...) custom-call(f32[8192,128]{1,0:T(8,128)} %bitcast.19), custom_call_target="tpu_custom_call" | custom-call | flops 786432 | bytes 7340032 | tf_op jit(solution)/shard_map/pallas_call | solution.py:60
  9.8 0.0 copy-start.2
  9.8 0.0 copy-start.6
  9.8 0.0 copy-start
  9.8 0.3 collective-permute-start.9
  10.1 0.0 copy-done.1
  10.1 0.1 slice.3
  10.2 3.8 %collective-permute-start = (f32[128,128]{1,0:T(8,128)S(1)}, f32[128,128]{1,0:T(8,128)S(1)}, u32[]{:S(2)}, u32[]{:S(2)}) collective-permute-start(f32[128,128]{1,0:T(8,128)S(1)} %bitcast.21), channel_id=1, source_target_pairs={{0,4},{4,8},{8,12},{12,16},{16,20},{20,24},{24,28},{1,5},{5,9},{9,... | collective-permute-start | bytes 196616 | tf_op jit(solution)/shard_map/ppermute | solution.py:257
  14.0 2.1 %shard_map.51 = (f32[512,128]{1,0:T(8,128)}, f32[512,128]{1,0:T(8,128)}) custom-call(f32[8192,128]{1,0:T(8,128)} %bitcast.20), custom_call_target="tpu_custom_call" | custom-call | flops 131072 | bytes 1572864 | tf_op jit(solution)/shard_map/pallas_call | solution.py:60
  16.1 0.0 copy-start.3
  16.1 0.0 copy-start.5
  16.1 1.6 %collective-permute-start.2 = (f32[512,128]{1,0:T(8,128)}, f32[512,128]{1,0:T(8,128)S(1)}, u32[]{:S(2)}, u32[]{:S(2)}) collective-permute-start(f32[512,128]{1,0:T(8,128)} %get-tuple-element.26), channel_id=1, source_target_pairs={{0,2},{1,3},{2,0},{3,1},{4,6},{5,7},{6,4},{7,5},{8,10},{9,11},{10,... | collective-permute-start | bytes 786440 | tf_op jit(solution)/shard_map/ppermute | solution.py:235
  17.7 0.0 collective-permute-done.lower
  17.7 0.0 collective-permute-start.3
  17.7 0.0 collective-permute-done.10.refs_4_
  17.7 0.6 collective-permute-start.1
  18.3 0.0 collective-permute-done.11.refs_5_
  18.3 0.1 collective-permute-start.14
  18.4 0.0 collective-permute-done.9.refs_3_
  18.4 1.5 %collective-permute-start.15 = (f32[768,128]{1,0:T(8,128)}, f32[768,128]{1,0:T(8,128)S(1)}, u32[]{:S(2)}, u32[]{:S(2)}) collective-permute-start(f32[768,128]{1,0:T(8,128)} %get-tuple-element.38), channel_id=1, source_target_pairs={{0,2},{1,3},{2,0},{3,1},{4,6},{5,7},{6,4},{7,5},{8,10},{9,11},{10,... | collective-permute-start | bytes 1179656 | tf_op jit(solution)/shard_map/ppermute | solution.py:235
  19.9 0.0 copy-done.2
  19.9 0.1 select_select_fusion
  20.0 5.6 %collective-permute-done.2.refs_10_.refs_4_ = f32[512,128]{1,0:T(8,128)S(1)} collective-permute-done((f32[512,128]{1,0:T(8,128)}, f32[512,128]{1,0:T(8,128)S(1)}, u32[]{:S(2)}, u32[]{:S(2)}) %collective-permute-start.2) | collective-permute-done | bytes 262176 | tf_op jit(solution)/shard_map/ppermute | solution.py:235
  25.5 0.0 copy-done.6
  25.5 0.0 collective-permute-start.16
  25.5 4.8 %collective-permute-done.3.refs_11_.refs_5_ = f32[512,128]{1,0:T(8,128)S(1)} collective-permute-done((f32[512,128]{1,0:T(8,128)}, f32[512,128]{1,0:T(8,128)S(1)}, u32[]{:S(2)}, u32[]{:S(2)}) %collective-permute-start.3) | collective-permute-done | bytes 262176 | tf_op jit(solution)/shard_map/ppermute | solution.py:235
  30.3 1.3 %collective-permute-start.13 = (f32[512,128]{1,0:T(8,128)S(1)}, f32[512,128]{1,0:T(8,128)S(1)}, u32[]{:S(2)}, u32[]{:S(2)}) collective-permute-start(f32[512,128]{1,0:T(8,128)S(1)} %get-tuple-element.46), channel_id=1, source_target_pairs={{4,0},{8,4},{12,8},{16,12},{20,16},{24,20},{28,24},{5,1},{9,5},{13... | collective-permute-start | bytes 786440 | tf_op jit(solution)/shard_map/ppermute | solution.py:272
  31.6 0.0 collective-permute-done.1.refs_9_.refs_3_
  31.6 4.6 %collective-permute-start.12 = (f32[512,128]{1,0:T(8,128)S(1)}, f32[512,128]{1,0:T(8,128)S(1)}, u32[]{:S(2)}, u32[]{:S(2)}) collective-permute-start(f32[512,128]{1,0:T(8,128)S(1)} %get-tuple-element.47), channel_id=1, source_target_pairs={{0,4},{4,8},{8,12},{12,16},{16,20},{20,24},{24,28},{1,5},{5,9},{9,... | collective-permute-start | bytes 786440 | tf_op jit(solution)/shard_map/ppermute | solution.py:273
  36.2 0.0 copy-done
  36.2 0.1 select_select_fusion.2
  36.2 0.0 collective-permute-done.14.refs_15_
  36.3 1.3 %collective-permute-start.5 = (f32[512,128]{1,0:T(8,128)S(1)}, f32[512,128]{1,0:T(8,128)S(1)}, u32[]{:S(2)}, u32[]{:S(2)}) collective-permute-start(f32[512,128]{1,0:T(8,128)S(1)} %get-tuple-element.48), channel_id=1, source_target_pairs={{4,0},{8,4},{12,8},{16,12},{20,16},{24,20},{28,24},{5,1},{9,5},{13... | collective-permute-start | bytes 786440 | tf_op jit(solution)/shard_map/ppermute | solution.py:272
  37.6 2.0 %collective-permute-done.15.refs_16_ = f32[768,128]{1,0:T(8,128)S(1)} collective-permute-done((f32[768,128]{1,0:T(8,128)}, f32[768,128]{1,0:T(8,128)S(1)}, u32[]{:S(2)}, u32[]{:S(2)}) %collective-permute-start.15) | collective-permute-done | bytes 393248 | tf_op jit(solution)/shard_map/ppermute | solution.py:235
  39.6 3.5 %collective-permute-start.4 = (f32[512,128]{1,0:T(8,128)S(1)}, f32[512,128]{1,0:T(8,128)S(1)}, u32[]{:S(2)}, u32[]{:S(2)}) collective-permute-start(f32[512,128]{1,0:T(8,128)S(1)} %get-tuple-element.49), channel_id=1, source_target_pairs={{0,4},{4,8},{8,12},{12,16},{16,20},{20,24},{24,28},{1,5},{5,9},{9,... | collective-permute-start | bytes 786440 | tf_op jit(solution)/shard_map/ppermute | solution.py:273
  43.1 2.9 %collective-permute-done.16.refs_17_ = f32[768,128]{1,0:T(8,128)S(1)} collective-permute-done((f32[768,128]{1,0:T(8,128)S(1)}, f32[768,128]{1,0:T(8,128)S(1)}, u32[]{:S(2)}, u32[]{:S(2)}) %collective-permute-start.16) | collective-permute-done | bytes 393248 | tf_op jit(solution)/shard_map/ppermute | solution.py:235
  46.0 1.1 %collective-permute-start.6 = (f32[256,128]{1,0:T(8,128)}, f32[256,128]{1,0:T(8,128)S(1)}, u32[]{:S(2)}, u32[]{:S(2)}) collective-permute-start(f32[256,128]{1,0:T(8,128)} %get-tuple-element.29), channel_id=1, source_target_pairs={{0,1},{1,0},{2,3},{3,2},{4,5},{5,4},{6,7},{7,6},{8,9},{9,8},{10,11... | collective-permute-start | bytes 393224 | tf_op jit(solution)/shard_map/ppermute | solution.py:235
  47.0 0.0 collective-permute-done.13.refs_7_
  47.0 1.2 %collective-permute-start.7 = (f32[256,128]{1,0:T(8,128)}, f32[256,128]{1,0:T(8,128)S(1)}, u32[]{:S(2)}, u32[]{:S(2)}) collective-permute-start(f32[256,128]{1,0:T(8,128)} %get-tuple-element.30), channel_id=1, source_target_pairs={{0,2},{1,3},{2,0},{3,1},{4,6},{5,7},{6,4},{7,5},{8,10},{9,11},{10,... | collective-permute-start | bytes 393224 | tf_op jit(solution)/shard_map/ppermute | solution.py:235
  48.3 4.1 %collective-permute-done.12.refs_6_ = f32[512,128]{1,0:T(8,128)S(1)} collective-permute-done((f32[512,128]{1,0:T(8,128)S(1)}, f32[512,128]{1,0:T(8,128)S(1)}, u32[]{:S(2)}, u32[]{:S(2)}) %collective-permute-start.12) | collective-permute-done | bytes 262176 | tf_op jit(solution)/shard_map/ppermute | solution.py:273
  52.3 0.5 collective-permute-start.8
  52.8 0.0 copy-start.4
  52.8 0.7 weights.1.refs_1_
  53.5 0.0 collective-permute-done.5.refs_13_.refs_7_
  53.6 4.4 %collective-permute-done.4.refs_12_.refs_6_ = f32[512,128]{1,0:T(8,128)S(1)} collective-permute-done((f32[512,128]{1,0:T(8,128)S(1)}, f32[512,128]{1,0:T(8,128)S(1)}, u32[]{:S(2)}, u32[]{:S(2)}) %collective-permute-start.4) | collective-permute-done | bytes 262176 | tf_op jit(solution)/shard_map/ppermute | solution.py:273
  57.9 0.0 copy-done.3
  57.9 0.0 copy-done.5
  57.9 5.1 %defect.2 = (f32[6144,128]{1,0:T(8,128)S(1)}, f32[16,128]{1,0:T(8,128)S(1)}) custom-call(s32[64]{0:T(128)S(1)} %copy-done.5, f32[7,8,72,128]{3,2,1,0:T(8,128)S(1)} %weights.1.refs_1_, f32[512,128]{1,0:T(8,128)S(1)} %copy-done.2, f32[512,128]{1,0:T(8,128)S(1)} %collective-permute-done.9.refs_3_, f32[512,128]{1,0:T(8,128)S(1)} %collective-permute-done.10.refs_4_, ...), custom_call_target="tpu_custom_call" | custom-call | flops 15728640 | bytes 6291456 | tf_op jit(solution)/shard_map/defect/pallas_call | solution.py:294
  63.0 0.0 collective-permute-done.6.refs_9_
  63.0 0.0 collective-permute-done.7.refs_10_
  63.0 0.0 collective-permute-done.8.refs_11_
  63.0 0.0 copy-done.4
  63.0 2.1 %defect.3 = (f32[2048,128]{1,0:T(8,128)S(1)}, f32[16,128]{1,0:T(8,128)S(1)}) custom-call(s32[64]{0:T(128)S(1)} %copy-done.5, f32[7,8,72,128]{3,2,1,0:T(8,128)S(1)} %weights.1.refs_1_, f32[512,128]{1,0:T(8,128)S(1)} %copy-done, f32[512,128]{1,0:T(8,128)S(1)} %collective-permute-done.1.refs_9_.refs_3_, f32[512,128]{1,0:T(8,128)S(1)} %collective-permute-done.2.refs_10_.refs_4_, ...), custom_call_target="tpu_custom_call" | custom-call | flops 5242880 | bytes 2097152 | tf_op jit(solution)/shard_map/defect/pallas_call | solution.py:294
  65.1 2.5 %collective-permute-start.17 = (f32[16,128]{1,0:T(8,128)S(1)}, f32[16,128]{1,0:T(8,128)S(1)}, u32[]{:S(2)}, u32[]{:S(2)}) collective-permute-start(f32[16,128]{1,0:T(8,128)S(1)} %get-tuple-element.41), channel_id=1, source_target_pairs={{0,4},{4,0},{8,12},{12,8},{16,20},{20,16},{24,28},{28,24},{1,5},{5... | collective-permute-start | bytes 24584 | tf_op jit(solution)/shard_map/ppermute | solution.py:313
  67.6 1.6 %collective-permute-done.17 = f32[16,128]{1,0:T(8,128)S(1)} collective-permute-done((f32[16,128]{1,0:T(8,128)S(1)}, f32[16,128]{1,0:T(8,128)S(1)}, u32[]{:S(2)}, u32[]{:S(2)}) %collective-permute-start.17) | collective-permute-done | bytes 8224 | tf_op jit(solution)/shard_map/ppermute | solution.py:313
  69.2 1.6 %collective-permute-start.18 = (f32[16,128]{1,0:T(8,128)S(1)}, f32[16,128]{1,0:T(8,128)S(1)}, u32[]{:S(2)}, u32[]{:S(2)}) collective-permute-start(f32[16,128]{1,0:T(8,128)S(1)} %add.6), channel_id=1, source_target_pairs={{0,8},{4,12},{8,0},{12,4},{16,24},{20,28},{24,16},{28,20},{1,9},{5... | collective-permute-start | bytes 24584 | tf_op jit(solution)/shard_map/ppermute | solution.py:313
  70.8 2.1 %collective-permute-done.18 = f32[16,128]{1,0:T(8,128)S(1)} collective-permute-done((f32[16,128]{1,0:T(8,128)S(1)}, f32[16,128]{1,0:T(8,128)S(1)}, u32[]{:S(2)}, u32[]{:S(2)}) %collective-permute-start.18) | collective-permute-done | bytes 8224 | tf_op jit(solution)/shard_map/ppermute | solution.py:313
  72.9 2.6 %collective-permute-start.19 = (f32[16,128]{1,0:T(8,128)S(1)}, f32[16,128]{1,0:T(8,128)S(1)}, u32[]{:S(2)}, u32[]{:S(2)}) collective-permute-start(f32[16,128]{1,0:T(8,128)S(1)} %add.7.refs_0_), channel_id=1, source_target_pairs={{0,16},{4,20},{8,24},{12,28},{16,0},{20,4},{24,8},{28,12},{1,17},{... | collective-permute-start | bytes 24584 | tf_op jit(solution)/shard_map/ppermute | solution.py:313
  75.5 2.0 %collective-permute-done.19.refs_1_ = f32[16,128]{1,0:T(8,128)S(1)} collective-permute-done((f32[16,128]{1,0:T(8,128)S(1)}, f32[16,128]{1,0:T(8,128)S(1)}, u32[]{:S(2)}, u32[]{:S(2)}) %collective-permute-start.19) | collective-permute-done | bytes 8224 | tf_op jit(solution)/shard_map/ppermute | solution.py:313
  77.4 2.8 %scale.1 = (f32[8192,128]{1,0:T(8,128)}, f32[1,16]{1,0:T(1,128)}) custom-call(f32[16,128]{1,0:T(8,128)S(1)} %add.7.refs_0_, f32[16,128]{1,0:T(8,128)S(1)} %collective-permute-done.19.refs_1_, f32[6144,128]{1,0:T(8,128)S(1)} %get-tuple-element.42.refs_2_, f32[2048,128]{1,0:T(8,128)S(1)} %get-tuple-element.43.refs_3_), custom_call_target="tpu_custom_call" | custom-call | flops 1048576 | bytes 8388608 | tf_op jit(solution)/shard_map/scale/pallas_call | solution.py:315
  (2 shorter events, 0.0 us)
Async XLA Ops:
  0.6 9.5 %copy-start.1 = (f32[4,8,8192]{2,1,0:T(8,128)S(1)}, f32[4,8,8192]{2,1,0:T(8,128)}, u32[]{:S(2)}) copy-start(f32[4,8,8192]{2,1,0:T(8,128)} %param.4) | copy-start | bytes 3145732
  2.8 14.9 %collective-permute-start.10 = (f32[512,128]{1,0:T(8,128)}, f32[512,128]{1,0:T(8,128)S(1)}, u32[]{:S(2)}, u32[]{:S(2)}) collective-permute-start(f32[512,128]{1,0:T(8,128)} %get-tuple-element.34), channel_id=1, source_target_pairs={{0,2},{1,3},{2,0},{3,1},{4,6},{5,7},{6,4},{7,5},{8,10},{9,11},{10,... | collective-permute-start | bytes 786440 | tf_op jit(solution)/shard_map/ppermute | solution.py:235
  5.9 12.4 %collective-permute-start.11 = (f32[512,128]{1,0:T(8,128)}, f32[512,128]{1,0:T(8,128)S(1)}, u32[]{:S(2)}, u32[]{:S(2)}) collective-permute-start(f32[512,128]{1,0:T(8,128)} %get-tuple-element.35), channel_id=1, source_target_pairs={{0,3},{1,2},{2,1},{3,0},{4,7},{5,6},{6,5},{7,4},{8,11},{9,10},{10,... | collective-permute-start | bytes 786440 | tf_op jit(solution)/shard_map/ppermute | solution.py:235
  9.8 10.1 %copy-start.2 = (f32[512,128]{1,0:T(8,128)S(1)}, f32[512,128]{1,0:T(8,128)}, u32[]{:S(2)}) copy-start(f32[512,128]{1,0:T(8,128)} %get-tuple-element.32.refs_2_) | copy-start | bytes 786436
  9.8 15.7 %copy-start.6 = (f32[768,128]{1,0:T(8,128)S(1)}, f32[768,128]{1,0:T(8,128)}, u32[]{:S(2)}) copy-start(f32[768,128]{1,0:T(8,128)} %get-tuple-element.39) | copy-start | bytes 1179652
  9.8 26.3 %copy-start = (f32[512,128]{1,0:T(8,128)S(1)}, f32[512,128]{1,0:T(8,128)}, u32[]{:S(2)}) copy-start(f32[512,128]{1,0:T(8,128)} %get-tuple-element.24.refs_8_.refs_2_) | copy-start | bytes 786436
  9.8 8.5 %collective-permute-start.9 = (f32[512,128]{1,0:T(8,128)}, f32[512,128]{1,0:T(8,128)S(1)}, u32[]{:S(2)}, u32[]{:S(2)}) collective-permute-start(f32[512,128]{1,0:T(8,128)} %get-tuple-element.33), channel_id=1, source_target_pairs={{0,1},{1,0},{2,3},{3,2},{4,5},{5,4},{6,7},{7,6},{8,9},{9,8},{10,11... | collective-permute-start | bytes 786440 | tf_op jit(solution)/shard_map/ppermute | solution.py:235
  10.2 7.5 %collective-permute-start = (f32[128,128]{1,0:T(8,128)S(1)}, f32[128,128]{1,0:T(8,128)S(1)}, u32[]{:S(2)}, u32[]{:S(2)}) collective-permute-start(f32[128,128]{1,0:T(8,128)S(1)} %bitcast.21), channel_id=1, source_target_pairs={{0,4},{4,8},{8,12},{12,16},{16,20},{20,24},{24,28},{1,5},{5,9},{9,... | collective-permute-start | bytes 196616 | tf_op jit(solution)/shard_map/ppermute | solution.py:257
  16.1 41.9 %copy-start.3 = (f32[768,128]{1,0:T(8,128)S(1)}, f32[768,128]{1,0:T(8,128)}, u32[]{:S(2)}) copy-start(f32[768,128]{1,0:T(8,128)} %get-tuple-element.36.refs_14_) | copy-start | bytes 1179652
  16.1 41.9 %copy-start.5 = (s32[64]{0:T(128)S(1)}, s32[64]{0:T(128)}, u32[]{:S(2)}) copy-start(s32[64]{0:T(128)} %refs_0_.3) | copy-start | bytes 772
  16.1 9.5 %collective-permute-start.2 = (f32[512,128]{1,0:T(8,128)}, f32[512,128]{1,0:T(8,128)S(1)}, u32[]{:S(2)}, u32[]{:S(2)}) collective-permute-start(f32[512,128]{1,0:T(8,128)} %get-tuple-element.26), channel_id=1, source_target_pairs={{0,2},{1,3},{2,0},{3,1},{4,6},{5,7},{6,4},{7,5},{8,10},{9,11},{10,... | collective-permute-start | bytes 786440 | tf_op jit(solution)/shard_map/ppermute | solution.py:235
  17.7 12.6 %collective-permute-start.3 = (f32[512,128]{1,0:T(8,128)}, f32[512,128]{1,0:T(8,128)S(1)}, u32[]{:S(2)}, u32[]{:S(2)}) collective-permute-start(f32[512,128]{1,0:T(8,128)} %get-tuple-element.27), channel_id=1, source_target_pairs={{0,3},{1,2},{2,1},{3,0},{4,7},{5,6},{6,5},{7,4},{8,11},{9,10},{10,... | collective-permute-start | bytes 786440 | tf_op jit(solution)/shard_map/ppermute | solution.py:235
  17.7 13.9 %collective-permute-start.1 = (f32[512,128]{1,0:T(8,128)}, f32[512,128]{1,0:T(8,128)S(1)}, u32[]{:S(2)}, u32[]{:S(2)}) collective-permute-start(f32[512,128]{1,0:T(8,128)} %get-tuple-element.25), channel_id=1, source_target_pairs={{0,1},{1,0},{2,3},{3,2},{4,5},{5,4},{6,7},{7,6},{8,9},{9,8},{10,11... | collective-permute-start | bytes 786440 | tf_op jit(solution)/shard_map/ppermute | solution.py:235
  18.3 17.9 %collective-permute-start.14 = (f32[768,128]{1,0:T(8,128)}, f32[768,128]{1,0:T(8,128)S(1)}, u32[]{:S(2)}, u32[]{:S(2)}) collective-permute-start(f32[768,128]{1,0:T(8,128)} %get-tuple-element.37), channel_id=1, source_target_pairs={{0,1},{1,0},{2,3},{3,2},{4,5},{5,4},{6,7},{7,6},{8,9},{9,8},{10,11... | collective-permute-start | bytes 1179656 | tf_op jit(solution)/shard_map/ppermute | solution.py:235
  18.4 21.2 %collective-permute-start.15 = (f32[768,128]{1,0:T(8,128)}, f32[768,128]{1,0:T(8,128)S(1)}, u32[]{:S(2)}, u32[]{:S(2)}) collective-permute-start(f32[768,128]{1,0:T(8,128)} %get-tuple-element.38), channel_id=1, source_target_pairs={{0,2},{1,3},{2,0},{3,1},{4,6},{5,7},{6,4},{7,5},{8,10},{9,11},{10,... | collective-permute-start | bytes 1179656 | tf_op jit(solution)/shard_map/ppermute | solution.py:235
  25.5 20.4 %collective-permute-start.16 = (f32[768,128]{1,0:T(8,128)S(1)}, f32[768,128]{1,0:T(8,128)S(1)}, u32[]{:S(2)}, u32[]{:S(2)}) collective-permute-start(f32[768,128]{1,0:T(8,128)S(1)} %copy-done.6), channel_id=1, source_target_pairs={{0,3},{1,2},{2,1},{3,0},{4,7},{5,6},{6,5},{7,4},{8,11},{9,10},{10,... | collective-permute-start | bytes 1179656 | tf_op jit(solution)/shard_map/ppermute | solution.py:235
  30.3 16.7 %collective-permute-start.13 = (f32[512,128]{1,0:T(8,128)S(1)}, f32[512,128]{1,0:T(8,128)S(1)}, u32[]{:S(2)}, u32[]{:S(2)}) collective-permute-start(f32[512,128]{1,0:T(8,128)S(1)} %get-tuple-element.46), channel_id=1, source_target_pairs={{4,0},{8,4},{12,8},{16,12},{20,16},{24,20},{28,24},{5,1},{9,5},{13... | collective-permute-start | bytes 786440 | tf_op jit(solution)/shard_map/ppermute | solution.py:272
  31.6 20.7 %collective-permute-start.12 = (f32[512,128]{1,0:T(8,128)S(1)}, f32[512,128]{1,0:T(8,128)S(1)}, u32[]{:S(2)}, u32[]{:S(2)}) collective-permute-start(f32[512,128]{1,0:T(8,128)S(1)} %get-tuple-element.47), channel_id=1, source_target_pairs={{0,4},{4,8},{8,12},{12,16},{16,20},{20,24},{24,28},{1,5},{5,9},{9,... | collective-permute-start | bytes 786440 | tf_op jit(solution)/shard_map/ppermute | solution.py:273
  36.3 17.3 %collective-permute-start.5 = (f32[512,128]{1,0:T(8,128)S(1)}, f32[512,128]{1,0:T(8,128)S(1)}, u32[]{:S(2)}, u32[]{:S(2)}) collective-permute-start(f32[512,128]{1,0:T(8,128)S(1)} %get-tuple-element.48), channel_id=1, source_target_pairs={{4,0},{8,4},{12,8},{16,12},{20,16},{24,20},{28,24},{5,1},{9,5},{13... | collective-permute-start | bytes 786440 | tf_op jit(solution)/shard_map/ppermute | solution.py:272
  39.6 18.3 %collective-permute-start.4 = (f32[512,128]{1,0:T(8,128)S(1)}, f32[512,128]{1,0:T(8,128)S(1)}, u32[]{:S(2)}, u32[]{:S(2)}) collective-permute-start(f32[512,128]{1,0:T(8,128)S(1)} %get-tuple-element.49), channel_id=1, source_target_pairs={{0,4},{4,8},{8,12},{12,16},{16,20},{20,24},{24,28},{1,5},{5,9},{9,... | collective-permute-start | bytes 786440 | tf_op jit(solution)/shard_map/ppermute | solution.py:273
  46.0 17.0 %collective-permute-start.6 = (f32[256,128]{1,0:T(8,128)}, f32[256,128]{1,0:T(8,128)S(1)}, u32[]{:S(2)}, u32[]{:S(2)}) collective-permute-start(f32[256,128]{1,0:T(8,128)} %get-tuple-element.29), channel_id=1, source_target_pairs={{0,1},{1,0},{2,3},{3,2},{4,5},{5,4},{6,7},{7,6},{8,9},{9,8},{10,11... | collective-permute-start | bytes 393224 | tf_op jit(solution)/shard_map/ppermute | solution.py:235
  47.0 16.0 %collective-permute-start.7 = (f32[256,128]{1,0:T(8,128)}, f32[256,128]{1,0:T(8,128)S(1)}, u32[]{:S(2)}, u32[]{:S(2)}) collective-permute-start(f32[256,128]{1,0:T(8,128)} %get-tuple-element.30), channel_id=1, source_target_pairs={{0,2},{1,3},{2,0},{3,1},{4,6},{5,7},{6,4},{7,5},{8,10},{9,11},{10,... | collective-permute-start | bytes 393224 | tf_op jit(solution)/shard_map/ppermute | solution.py:235
  52.3 10.7 %collective-permute-start.8 = (f32[256,128]{1,0:T(8,128)}, f32[256,128]{1,0:T(8,128)S(1)}, u32[]{:S(2)}, u32[]{:S(2)}) collective-permute-start(f32[256,128]{1,0:T(8,128)} %get-tuple-element.31), channel_id=1, source_target_pairs={{0,3},{1,2},{2,1},{3,0},{4,7},{5,6},{6,5},{7,4},{8,11},{9,10},{10,... | collective-permute-start | bytes 393224 | tf_op jit(solution)/shard_map/ppermute | solution.py:235
  52.8 10.2 %copy-start.4 = (f32[256,128]{1,0:T(8,128)S(1)}, f32[256,128]{1,0:T(8,128)}, u32[]{:S(2)}) copy-start(f32[256,128]{1,0:T(8,128)} %get-tuple-element.28.refs_8_) | copy-start | bytes 393220
  65.1 4.1 %collective-permute-start.17 = (f32[16,128]{1,0:T(8,128)S(1)}, f32[16,128]{1,0:T(8,128)S(1)}, u32[]{:S(2)}, u32[]{:S(2)}) collective-permute-start(f32[16,128]{1,0:T(8,128)S(1)} %get-tuple-element.41), channel_id=1, source_target_pairs={{0,4},{4,0},{8,12},{12,8},{16,20},{20,16},{24,28},{28,24},{1,5},{5... | collective-permute-start | bytes 24584 | tf_op jit(solution)/shard_map/ppermute | solution.py:313
  69.2 3.7 %collective-permute-start.18 = (f32[16,128]{1,0:T(8,128)S(1)}, f32[16,128]{1,0:T(8,128)S(1)}, u32[]{:S(2)}, u32[]{:S(2)}) collective-permute-start(f32[16,128]{1,0:T(8,128)S(1)} %add.6), channel_id=1, source_target_pairs={{0,8},{4,12},{8,0},{12,4},{16,24},{20,28},{24,16},{28,20},{1,9},{5... | collective-permute-start | bytes 24584 | tf_op jit(solution)/shard_map/ppermute | solution.py:313
  72.9 4.5 %collective-permute-start.19 = (f32[16,128]{1,0:T(8,128)S(1)}, f32[16,128]{1,0:T(8,128)S(1)}, u32[]{:S(2)}, u32[]{:S(2)}) collective-permute-start(f32[16,128]{1,0:T(8,128)S(1)} %add.7.refs_0_), channel_id=1, source_target_pairs={{0,16},{4,20},{8,24},{12,28},{16,0},{20,4},{24,8},{28,12},{1,17},{... | collective-permute-start | bytes 24584 | tf_op jit(solution)/shard_map/ppermute | solution.py:313

commit v2 on v1

--- a/solution.py
+++ b/solution.py
@@ -194,25 +194,29 @@
     sub = lax.broadcasted_iota(jnp.int32, (group, LANES), 0)
     spread = jnp.where(lane == sub, jnp.broadcast_to(norm, (group, LANES)), 0.0)
     norms[...] = jnp.sum(spread, axis=0, keepdims=True)[:, :group]
-    inverse = jnp.broadcast_to(1.0 / norm, (group, LANES))
-    writes = []
-    for i in range(group):
-        part, (lo, n) = [(p, c) for p, c in zip(parts, chunks, strict=True) if c[0] <= i < sum(c)][0]
-        factor = jnp.broadcast_to(inverse[i : i + 1], (SUB, LANES))
-
-        def step(j, _, i=i, lo=lo, part=part, factor=factor):
-            for u in range(8):
-                at = (j * 8 + u) * SUB
-                to = pl.ds(pl.multiple_of(i * per + at, SUB), SUB)
-                buf[to, :] = part[pl.ds(pl.multiple_of((i - lo) * per + at, SUB), SUB), :] * factor
+    buf[pl.ds(group * per, group), :] = jnp.broadcast_to(1.0 / norm, (group, LANES))
+
+    def copy_of(i):
+        spot = pl.ds(pl.multiple_of(i * per, per), per)
+        return pltpu.make_async_copy(buf.at[spot, :], out.at[spot, :], out_sem.at[i])
+
+    for part, (lo, n) in zip(parts, chunks, strict=True):
+
+        def step(i, _, part=part, lo=lo):
+            factor = jnp.broadcast_to(buf[pl.ds(group * per + lo + i, 1), :], (SUB, LANES))
+            for at in range(0, per, SUB):
+                to = pl.ds(pl.multiple_of((lo + i) * per + at, SUB), SUB)
+                buf[to, :] = part[pl.ds(pl.multiple_of(i * per + at, SUB), SUB), :] * factor
+            copy_of(lo + i).start()
             return 0
 
-        lax.fori_loop(0, per // (SUB * 8), step, 0)
-        spot = pl.ds(i * per, per)
-        writes.append(pltpu.make_async_copy(buf.at[spot, :], out.at[spot, :], out_sem.at[i]))
-        writes[-1].start()
-    for write in writes:
-        write.wait()
+        lax.fori_loop(0, n, step, 0)
+
+    def finish(i, _):
+        copy_of(i).wait()
+        return 0
+
+    lax.fori_loop(0, group, finish, 0)
 
 
 def program(heat, cotan, source_index):
@@ -321,7 +325,7 @@
         in_specs=[vmem, vmem] + [vmem] * len(parts),
         out_specs=(pl.BlockSpec(memory_space=pltpu.HBM), vmem),
         scratch_shapes=[
-            pltpu.VMEM((group * per, LANES), jnp.float32),
+            pltpu.VMEM((group * per + group, LANES), jnp.float32),
             pltpu.SemaphoreType.DMA((group,)),
         ],
         cost_estimate=pl.CostEstimate(flops=group * per * LANES, bytes_accessed=8 * group * per * LANES, transcendentals=0),

time: 80.5 us -> 80.5 us (level)
  no operation moved by 1% of the time
where the time goes in v2:
time: 80.5 us; the launch traced here: 80.2 us
  starting transfers between devices  31 us (39%)
  waiting for transfers between devices  29.4 us (37%)
  Pallas kernels  18.7 us (23%)
  between operations  0.85 us (1%)
    ppermute x12, waiting for transfers between devices, send(): lax.ppermute(piece, 'src', [(i, i ^ k) for i in range(senders)])  15.3 us
    ppermute x12, starting transfers between devices, send(): lax.ppermute(piece, 'src', [(i, i ^ k) for i in range(senders)])  9.92 us
    ppermute x2, waiting for transfers between devices, program(): below.append(lax.ppermute(last, 'vtx', up))  8.42 us
    pallas_call x3, Pallas kernels, pack(): pl.pallas_call(functools.partial(pack_kernel, (tuple(plan), group, cb, ow...  8.15 us
    ppermute x2, starting transfers between devices, program(): below.append(lax.ppermute(last, 'vtx', up))  8.02 us
    pallas_call x2, Pallas kernels, program(): pl.pallas_call(functools.partial(defect_kernel, meta, lo, n, group, ampli...  7.11 us
    ppermute x3, starting transfers between devices, program(): other = lax.ppermute(sums, 'vtx', [(i, i ^ step) for i in range(peers)])  6.68 us
    ppermute x3, waiting for transfers between devices, program(): other = lax.ppermute(sums, 'vtx', [(i, i ^ step) for i in range(peers)])  5.67 us
  transfers between devices with their start and end apart: 20, of which 9 were waited for; matrix products, arithmetic and copies ran while one was open for 0% of the time, Pallas kernels for 15%

profile of v2, /device:TPU:0, one launch (start us, length us, event | category | flops | bytes accessed | tf_op | source)
XLA Modules:
  0.0 80.2 jit_solution(16852221247603225943)
XLA Ops:
  0.6 0.0 copy-start.1
  0.6 2.1 %shard_map.52 = (f32[512,128]{1,0:T(8,128)}, f32[512,128]{1,0:T(8,128)}) custom-call(f32[8192,128]{1,0:T(8,128)} %bitcast.18), custom_call_target="tpu_custom_call" | custom-call | flops 131072 | bytes 1572864 | tf_op jit(solution)/shard_map/pallas_call | solution.py:60
  2.8 3.1 %collective-permute-start.10 = (f32[512,128]{1,0:T(8,128)}, f32[512,128]{1,0:T(8,128)S(1)}, u32[]{:S(2)}, u32[]{:S(2)}) collective-permute-start(f32[512,128]{1,0:T(8,128)} %get-tuple-element.34), channel_id=1, source_target_pairs={{0,2},{1,3},{2,0},{3,1},{4,6},{5,7},{6,4},{7,5},{8,10},{9,11},{10,... | collective-permute-start | bytes 786440 | tf_op jit(solution)/shard_map/ppermute | solution.py:239
  5.9 0.0 collective-permute-start.11
  5.9 3.9 %shard_map.50 = (f32[512,128]{1,0:T(8,128)}, f32[512,128]{1,0:T(8,128)}, f32[512,128]{1,0:T(8,128)}, f32[512,128]{1,0:T(8,128)}, f32[768,128]{1,0:T(8,128)}, /*i...) custom-call(f32[8192,128]{1,0:T(8,128)} %bitcast.19), custom_call_target="tpu_custom_call" | custom-call | flops 786432 | bytes 7340032 | tf_op jit(solution)/shard_map/pallas_call | solution.py:60
  9.8 0.0 copy-start.2
  9.8 0.0 copy-start.6
  9.8 0.0 copy-start
  9.8 0.3 collective-permute-start.9
  10.1 0.0 copy-done.1
  10.1 0.1 slice.3
  10.2 3.8 %collective-permute-start = (f32[128,128]{1,0:T(8,128)S(1)}, f32[128,128]{1,0:T(8,128)S(1)}, u32[]{:S(2)}, u32[]{:S(2)}) collective-permute-start(f32[128,128]{1,0:T(8,128)S(1)} %bitcast.21), channel_id=1, source_target_pairs={{0,4},{4,8},{8,12},{12,16},{16,20},{20,24},{24,28},{1,5},{5,9},{9,... | collective-permute-start | bytes 196616 | tf_op jit(solution)/shard_map/ppermute | solution.py:261
  14.0 2.1 %shard_map.51 = (f32[512,128]{1,0:T(8,128)}, f32[512,128]{1,0:T(8,128)}) custom-call(f32[8192,128]{1,0:T(8,128)} %bitcast.20), custom_call_target="tpu_custom_call" | custom-call | flops 131072 | bytes 1572864 | tf_op jit(solution)/shard_map/pallas_call | solution.py:60
  16.1 0.0 copy-start.3
  16.1 0.0 copy-start.5
  16.1 1.6 %collective-permute-start.2 = (f32[512,128]{1,0:T(8,128)}, f32[512,128]{1,0:T(8,128)S(1)}, u32[]{:S(2)}, u32[]{:S(2)}) collective-permute-start(f32[512,128]{1,0:T(8,128)} %get-tuple-element.26), channel_id=1, source_target_pairs={{0,2},{1,3},{2,0},{3,1},{4,6},{5,7},{6,4},{7,5},{8,10},{9,11},{10,... | collective-permute-start | bytes 786440 | tf_op jit(solution)/shard_map/ppermute | solution.py:239
  17.7 0.0 collective-permute-done.lower
  17.7 0.0 collective-permute-start.3
  17.7 0.0 collective-permute-done.10.refs_4_
  17.7 0.6 collective-permute-start.1
  18.3 0.0 collective-permute-done.11.refs_5_
  18.3 0.1 collective-permute-start.14
  18.4 0.0 collective-permute-done.9.refs_3_
  18.4 1.5 %collective-permute-start.15 = (f32[768,128]{1,0:T(8,128)}, f32[768,128]{1,0:T(8,128)S(1)}, u32[]{:S(2)}, u32[]{:S(2)}) collective-permute-start(f32[768,128]{1,0:T(8,128)} %get-tuple-element.38), channel_id=1, source_target_pairs={{0,2},{1,3},{2,0},{3,1},{4,6},{5,7},{6,4},{7,5},{8,10},{9,11},{10,... | collective-permute-start | bytes 1179656 | tf_op jit(solution)/shard_map/ppermute | solution.py:239
  19.9 0.0 copy-done.2
  19.9 0.1 select_select_fusion
  20.0 5.6 %collective-permute-done.2.refs_10_.refs_4_ = f32[512,128]{1,0:T(8,128)S(1)} collective-permute-done((f32[512,128]{1,0:T(8,128)}, f32[512,128]{1,0:T(8,128)S(1)}, u32[]{:S(2)}, u32[]{:S(2)}) %collective-permute-start.2) | collective-permute-done | bytes 262176 | tf_op jit(solution)/shard_map/ppermute | solution.py:239
  25.5 0.0 copy-done.6
  25.5 0.0 collective-permute-start.16
  25.5 4.8 %collective-permute-done.3.refs_11_.refs_5_ = f32[512,128]{1,0:T(8,128)S(1)} collective-permute-done((f32[512,128]{1,0:T(8,128)}, f32[512,128]{1,0:T(8,128)S(1)}, u32[]{:S(2)}, u32[]{:S(2)}) %collective-permute-start.3) | collective-permute-done | bytes 262176 | tf_op jit(solution)/shard_map/ppermute | solution.py:239
  30.3 1.3 %collective-permute-start.13 = (f32[512,128]{1,0:T(8,128)S(1)}, f32[512,128]{1,0:T(8,128)S(1)}, u32[]{:S(2)}, u32[]{:S(2)}) collective-permute-start(f32[512,128]{1,0:T(8,128)S(1)} %get-tuple-element.46), channel_id=1, source_target_pairs={{4,0},{8,4},{12,8},{16,12},{20,16},{24,20},{28,24},{5,1},{9,5},{13... | collective-permute-start | bytes 786440 | tf_op jit(solution)/shard_map/ppermute | solution.py:276
  31.6 0.0 collective-permute-done.1.refs_9_.refs_3_
  31.6 4.6 %collective-permute-start.12 = (f32[512,128]{1,0:T(8,128)S(1)}, f32[512,128]{1,0:T(8,128)S(1)}, u32[]{:S(2)}, u32[]{:S(2)}) collective-permute-start(f32[512,128]{1,0:T(8,128)S(1)} %get-tuple-element.47), channel_id=1, source_target_pairs={{0,4},{4,8},{8,12},{12,16},{16,20},{20,24},{24,28},{1,5},{5,9},{9,... | collective-permute-start | bytes 786440 | tf_op jit(solution)/shard_map/ppermute | solution.py:277
  36.2 0.0 copy-done
  36.2 0.1 select_select_fusion.2
  36.2 0.0 collective-permute-done.14.refs_15_
  36.3 1.3 %collective-permute-start.5 = (f32[512,128]{1,0:T(8,128)S(1)}, f32[512,128]{1,0:T(8,128)S(1)}, u32[]{:S(2)}, u32[]{:S(2)}) collective-permute-start(f32[512,128]{1,0:T(8,128)S(1)} %get-tuple-element.48), channel_id=1, source_target_pairs={{4,0},{8,4},{12,8},{16,12},{20,16},{24,20},{28,24},{5,1},{9,5},{13... | collective-permute-start | bytes 786440 | tf_op jit(solution)/shard_map/ppermute | solution.py:276
  37.6 2.0 %collective-permute-done.15.refs_16_ = f32[768,128]{1,0:T(8,128)S(1)} collective-permute-done((f32[768,128]{1,0:T(8,128)}, f32[768,128]{1,0:T(8,128)S(1)}, u32[]{:S(2)}, u32[]{:S(2)}) %collective-permute-start.15) | collective-permute-done | bytes 393248 | tf_op jit(solution)/shard_map/ppermute | solution.py:239
  39.6 3.5 %collective-permute-start.4 = (f32[512,128]{1,0:T(8,128)S(1)}, f32[512,128]{1,0:T(8,128)S(1)}, u32[]{:S(2)}, u32[]{:S(2)}) collective-permute-start(f32[512,128]{1,0:T(8,128)S(1)} %get-tuple-element.49), channel_id=1, source_target_pairs={{0,4},{4,8},{8,12},{12,16},{16,20},{20,24},{24,28},{1,5},{5,9},{9,... | collective-permute-start | bytes 786440 | tf_op jit(solution)/shard_map/ppermute | solution.py:277
  43.1 2.9 %collective-permute-done.16.refs_17_ = f32[768,128]{1,0:T(8,128)S(1)} collective-permute-done((f32[768,128]{1,0:T(8,128)S(1)}, f32[768,128]{1,0:T(8,128)S(1)}, u32[]{:S(2)}, u32[]{:S(2)}) %collective-permute-start.16) | collective-permute-done | bytes 393248 | tf_op jit(solution)/shard_map/ppermute | solution.py:239
  46.0 1.1 %collective-permute-start.6 = (f32[256,128]{1,0:T(8,128)}, f32[256,128]{1,0:T(8,128)S(1)}, u32[]{:S(2)}, u32[]{:S(2)}) collective-permute-start(f32[256,128]{1,0:T(8,128)} %get-tuple-element.29), channel_id=1, source_target_pairs={{0,1},{1,0},{2,3},{3,2},{4,5},{5,4},{6,7},{7,6},{8,9},{9,8},{10,11... | collective-permute-start | bytes 393224 | tf_op jit(solution)/shard_map/ppermute | solution.py:239
  47.0 0.0 collective-permute-done.13.refs_7_
  47.0 1.2 %collective-permute-start.7 = (f32[256,128]{1,0:T(8,128)}, f32[256,128]{1,0:T(8,128)S(1)}, u32[]{:S(2)}, u32[]{:S(2)}) collective-permute-start(f32[256,128]{1,0:T(8,128)} %get-tuple-element.30), channel_id=1, source_target_pairs={{0,2},{1,3},{2,0},{3,1},{4,6},{5,7},{6,4},{7,5},{8,10},{9,11},{10,... | collective-permute-start | bytes 393224 | tf_op jit(solution)/shard_map/ppermute | solution.py:239
  48.3 4.1 %collective-permute-done.12.refs_6_ = f32[512,128]{1,0:T(8,128)S(1)} collective-permute-done((f32[512,128]{1,0:T(8,128)S(1)}, f32[512,128]{1,0:T(8,128)S(1)}, u32[]{:S(2)}, u32[]{:S(2)}) %collective-permute-start.12) | collective-permute-done | bytes 262176 | tf_op jit(solution)/shard_map/ppermute | solution.py:277
  52.3 0.5 collective-permute-start.8
  52.8 0.0 copy-start.4
  52.8 0.7 weights.1.refs_1_
  53.5 0.0 collective-permute-done.5.refs_13_.refs_7_
  53.6 4.4 %collective-permute-done.4.refs_12_.refs_6_ = f32[512,128]{1,0:T(8,128)S(1)} collective-permute-done((f32[512,128]{1,0:T(8,128)S(1)}, f32[512,128]{1,0:T(8,128)S(1)}, u32[]{:S(2)}, u32[]{:S(2)}) %collective-permute-start.4) | collective-permute-done | bytes 262176 | tf_op jit(solution)/shard_map/ppermute | solution.py:277
  57.9 0.0 copy-done.3
  57.9 0.0 copy-done.5
  57.9 5.1 %defect.2 = (f32[6144,128]{1,0:T(8,128)S(1)}, f32[16,128]{1,0:T(8,128)S(1)}) custom-call(s32[64]{0:T(128)S(1)} %copy-done.5, f32[7,8,72,128]{3,2,1,0:T(8,128)S(1)} %weights.1.refs_1_, f32[512,128]{1,0:T(8,128)S(1)} %copy-done.2, f32[512,128]{1,0:T(8,128)S(1)} %collective-permute-done.9.refs_3_, f32[512,128]{1,0:T(8,128)S(1)} %collective-permute-done.10.refs_4_, ...), custom_call_target="tpu_custom_call" | custom-call | flops 15728640 | bytes 6291456 | tf_op jit(solution)/shard_map/defect/pallas_call | solution.py:298
  63.0 0.0 collective-permute-done.6.refs_9_
  63.0 0.0 collective-permute-done.7.refs_10_
  63.0 0.0 collective-permute-done.8.refs_11_
  63.0 0.0 copy-done.4
  63.0 2.1 %defect.3 = (f32[2048,128]{1,0:T(8,128)S(1)}, f32[16,128]{1,0:T(8,128)S(1)}) custom-call(s32[64]{0:T(128)S(1)} %copy-done.5, f32[7,8,72,128]{3,2,1,0:T(8,128)S(1)} %weights.1.refs_1_, f32[512,128]{1,0:T(8,128)S(1)} %copy-done, f32[512,128]{1,0:T(8,128)S(1)} %collective-permute-done.1.refs_9_.refs_3_, f32[512,128]{1,0:T(8,128)S(1)} %collective-permute-done.2.refs_10_.refs_4_, ...), custom_call_target="tpu_custom_call" | custom-call | flops 5242880 | bytes 2097152 | tf_op jit(solution)/shard_map/defect/pallas_call | solution.py:298
  65.1 2.5 %collective-permute-start.17 = (f32[16,128]{1,0:T(8,128)S(1)}, f32[16,128]{1,0:T(8,128)S(1)}, u32[]{:S(2)}, u32[]{:S(2)}) collective-permute-start(f32[16,128]{1,0:T(8,128)S(1)} %get-tuple-element.41), channel_id=1, source_target_pairs={{0,4},{4,0},{8,12},{12,8},{16,20},{20,16},{24,28},{28,24},{1,5},{5... | collective-permute-start | bytes 24584 | tf_op jit(solution)/shard_map/ppermute | solution.py:317
  67.6 1.6 %collective-permute-done.17 = f32[16,128]{1,0:T(8,128)S(1)} collective-permute-done((f32[16,128]{1,0:T(8,128)S(1)}, f32[16,128]{1,0:T(8,128)S(1)}, u32[]{:S(2)}, u32[]{:S(2)}) %collective-permute-start.17) | collective-permute-done | bytes 8224 | tf_op jit(solution)/shard_map/ppermute | solution.py:317
  69.2 1.6 %collective-permute-start.18 = (f32[16,128]{1,0:T(8,128)S(1)}, f32[16,128]{1,0:T(8,128)S(1)}, u32[]{:S(2)}, u32[]{:S(2)}) collective-permute-start(f32[16,128]{1,0:T(8,128)S(1)} %add.6), channel_id=1, source_target_pairs={{0,8},{4,12},{8,0},{12,4},{16,24},{20,28},{24,16},{28,20},{1,9},{5... | collective-permute-start | bytes 24584 | tf_op jit(solution)/shard_map/ppermute | solution.py:317
  70.8 2.1 %collective-permute-done.18 = f32[16,128]{1,0:T(8,128)S(1)} collective-permute-done((f32[16,128]{1,0:T(8,128)S(1)}, f32[16,128]{1,0:T(8,128)S(1)}, u32[]{:S(2)}, u32[]{:S(2)}) %collective-permute-start.18) | collective-permute-done | bytes 8224 | tf_op jit(solution)/shard_map/ppermute | solution.py:317
  72.9 2.6 %collective-permute-start.19 = (f32[16,128]{1,0:T(8,128)S(1)}, f32[16,128]{1,0:T(8,128)S(1)}, u32[]{:S(2)}, u32[]{:S(2)}) collective-permute-start(f32[16,128]{1,0:T(8,128)S(1)} %add.7.refs_0_), channel_id=1, source_target_pairs={{0,16},{4,20},{8,24},{12,28},{16,0},{20,4},{24,8},{28,12},{1,17},{... | collective-permute-start | bytes 24584 | tf_op jit(solution)/shard_map/ppermute | solution.py:317
  75.5 2.0 %collective-permute-done.19.refs_1_ = f32[16,128]{1,0:T(8,128)S(1)} collective-permute-done((f32[16,128]{1,0:T(8,128)S(1)}, f32[16,128]{1,0:T(8,128)S(1)}, u32[]{:S(2)}, u32[]{:S(2)}) %collective-permute-start.19) | collective-permute-done | bytes 8224 | tf_op jit(solution)/shard_map/ppermute | solution.py:317
  77.4 2.8 %scale.1 = (f32[8192,128]{1,0:T(8,128)}, f32[1,16]{1,0:T(1,128)}) custom-call(f32[16,128]{1,0:T(8,128)S(1)} %add.7.refs_0_, f32[16,128]{1,0:T(8,128)S(1)} %collective-permute-done.19.refs_1_, f32[6144,128]{1,0:T(8,128)S(1)} %get-tuple-element.42.refs_2_, f32[2048,128]{1,0:T(8,128)S(1)} %get-tuple-element.43.refs_3_), custom_call_target="tpu_custom_call" | custom-call | flops 1048576 | bytes 8388608 | tf_op jit(solution)/shard_map/scale/pallas_call | solution.py:319
  (2 shorter events, 0.0 us)
Async XLA Ops:
  0.6 9.5 %copy-start.1 = (f32[4,8,8192]{2,1,0:T(8,128)S(1)}, f32[4,8,8192]{2,1,0:T(8,128)}, u32[]{:S(2)}) copy-start(f32[4,8,8192]{2,1,0:T(8,128)} %param.4) | copy-start | bytes 3145732
  2.8 14.9 %collective-permute-start.10 = (f32[512,128]{1,0:T(8,128)}, f32[512,128]{1,0:T(8,128)S(1)}, u32[]{:S(2)}, u32[]{:S(2)}) collective-permute-start(f32[512,128]{1,0:T(8,128)} %get-tuple-element.34), channel_id=1, source_target_pairs={{0,2},{1,3},{2,0},{3,1},{4,6},{5,7},{6,4},{7,5},{8,10},{9,11},{10,... | collective-permute-start | bytes 786440 | tf_op jit(solution)/shard_map/ppermute | solution.py:239
  5.9 12.4 %collective-permute-start.11 = (f32[512,128]{1,0:T(8,128)}, f32[512,128]{1,0:T(8,128)S(1)}, u32[]{:S(2)}, u32[]{:S(2)}) collective-permute-start(f32[512,128]{1,0:T(8,128)} %get-tuple-element.35), channel_id=1, source_target_pairs={{0,3},{1,2},{2,1},{3,0},{4,7},{5,6},{6,5},{7,4},{8,11},{9,10},{10,... | collective-permute-start | bytes 786440 | tf_op jit(solution)/shard_map/ppermute | solution.py:239
  9.8 10.1 %copy-start.2 = (f32[512,128]{1,0:T(8,128)S(1)}, f32[512,128]{1,0:T(8,128)}, u32[]{:S(2)}) copy-start(f32[512,128]{1,0:T(8,128)} %get-tuple-element.32.refs_2_) | copy-start | bytes 786436
  9.8 15.7 %copy-start.6 = (f32[768,128]{1,0:T(8,128)S(1)}, f32[768,128]{1,0:T(8,128)}, u32[]{:S(2)}) copy-start(f32[768,128]{1,0:T(8,128)} %get-tuple-element.39) | copy-start | bytes 1179652
  9.8 26.3 %copy-start = (f32[512,128]{1,0:T(8,128)S(1)}, f32[512,128]{1,0:T(8,128)}, u32[]{:S(2)}) copy-start(f32[512,128]{1,0:T(8,128)} %get-tuple-element.24.refs_8_.refs_2_) | copy-start | bytes 786436
  9.8 8.5 %collective-permute-start.9 = (f32[512,128]{1,0:T(8,128)}, f32[512,128]{1,0:T(8,128)S(1)}, u32[]{:S(2)}, u32[]{:S(2)}) collective-permute-start(f32[512,128]{1,0:T(8,128)} %get-tuple-element.33), channel_id=1, source_target_pairs={{0,1},{1,0},{2,3},{3,2},{4,5},{5,4},{6,7},{7,6},{8,9},{9,8},{10,11... | collective-permute-start | bytes 786440 | tf_op jit(solution)/shard_map/ppermute | solution.py:239
  10.2 7.5 %collective-permute-start = (f32[128,128]{1,0:T(8,128)S(1)}, f32[128,128]{1,0:T(8,128)S(1)}, u32[]{:S(2)}, u32[]{:S(2)}) collective-permute-start(f32[128,128]{1,0:T(8,128)S(1)} %bitcast.21), channel_id=1, source_target_pairs={{0,4},{4,8},{8,12},{12,16},{16,20},{20,24},{24,28},{1,5},{5,9},{9,... | collective-permute-start | bytes 196616 | tf_op jit(solution)/shard_map/ppermute | solution.py:261
  16.1 41.9 %copy-start.3 = (f32[768,128]{1,0:T(8,128)S(1)}, f32[768,128]{1,0:T(8,128)}, u32[]{:S(2)}) copy-start(f32[768,128]{1,0:T(8,128)} %get-tuple-element.36.refs_14_) | copy-start | bytes 1179652
  16.1 41.9 %copy-start.5 = (s32[64]{0:T(128)S(1)}, s32[64]{0:T(128)}, u32[]{:S(2)}) copy-start(s32[64]{0:T(128)} %refs_0_.3) | copy-start | bytes 772
  16.1 9.5 %collective-permute-start.2 = (f32[512,128]{1,0:T(8,128)}, f32[512,128]{1,0:T(8,128)S(1)}, u32[]{:S(2)}, u32[]{:S(2)}) collective-permute-start(f32[512,128]{1,0:T(8,128)} %get-tuple-element.26), channel_id=1, source_target_pairs={{0,2},{1,3},{2,0},{3,1},{4,6},{5,7},{6,4},{7,5},{8,10},{9,11},{10,... | collective-permute-start | bytes 786440 | tf_op jit(solution)/shard_map/ppermute | solution.py:239
  17.7 12.6 %collective-permute-start.3 = (f32[512,128]{1,0:T(8,128)}, f32[512,128]{1,0:T(8,128)S(1)}, u32[]{:S(2)}, u32[]{:S(2)}) collective-permute-start(f32[512,128]{1,0:T(8,128)} %get-tuple-element.27), channel_id=1, source_target_pairs={{0,3},{1,2},{2,1},{3,0},{4,7},{5,6},{6,5},{7,4},{8,11},{9,10},{10,... | collective-permute-start | bytes 786440 | tf_op jit(solution)/shard_map/ppermute | solution.py:239
  17.7 13.9 %collective-permute-start.1 = (f32[512,128]{1,0:T(8,128)}, f32[512,128]{1,0:T(8,128)S(1)}, u32[]{:S(2)}, u32[]{:S(2)}) collective-permute-start(f32[512,128]{1,0:T(8,128)} %get-tuple-element.25), channel_id=1, source_target_pairs={{0,1},{1,0},{2,3},{3,2},{4,5},{5,4},{6,7},{7,6},{8,9},{9,8},{10,11... | collective-permute-start | bytes 786440 | tf_op jit(solution)/shard_map/ppermute | solution.py:239
  18.3 17.9 %collective-permute-start.14 = (f32[768,128]{1,0:T(8,128)}, f32[768,128]{1,0:T(8,128)S(1)}, u32[]{:S(2)}, u32[]{:S(2)}) collective-permute-start(f32[768,128]{1,0:T(8,128)} %get-tuple-element.37), channel_id=1, source_target_pairs={{0,1},{1,0},{2,3},{3,2},{4,5},{5,4},{6,7},{7,6},{8,9},{9,8},{10,11... | collective-permute-start | bytes 1179656 | tf_op jit(solution)/shard_map/ppermute | solution.py:239
  18.4 21.2 %collective-permute-start.15 = (f32[768,128]{1,0:T(8,128)}, f32[768,128]{1,0:T(8,128)S(1)}, u32[]{:S(2)}, u32[]{:S(2)}) collective-permute-start(f32[768,128]{1,0:T(8,128)} %get-tuple-element.38), channel_id=1, source_target_pairs={{0,2},{1,3},{2,0},{3,1},{4,6},{5,7},{6,4},{7,5},{8,10},{9,11},{10,... | collective-permute-start | bytes 1179656 | tf_op jit(solution)/shard_map/ppermute | solution.py:239
  25.5 20.4 %collective-permute-start.16 = (f32[768,128]{1,0:T(8,128)S(1)}, f32[768,128]{1,0:T(8,128)S(1)}, u32[]{:S(2)}, u32[]{:S(2)}) collective-permute-start(f32[768,128]{1,0:T(8,128)S(1)} %copy-done.6), channel_id=1, source_target_pairs={{0,3},{1,2},{2,1},{3,0},{4,7},{5,6},{6,5},{7,4},{8,11},{9,10},{10,... | collective-permute-start | bytes 1179656 | tf_op jit(solution)/shard_map/ppermute | solution.py:239
  30.3 16.7 %collective-permute-start.13 = (f32[512,128]{1,0:T(8,128)S(1)}, f32[512,128]{1,0:T(8,128)S(1)}, u32[]{:S(2)}, u32[]{:S(2)}) collective-permute-start(f32[512,128]{1,0:T(8,128)S(1)} %get-tuple-element.46), channel_id=1, source_target_pairs={{4,0},{8,4},{12,8},{16,12},{20,16},{24,20},{28,24},{5,1},{9,5},{13... | collective-permute-start | bytes 786440 | tf_op jit(solution)/shard_map/ppermute | solution.py:276
  31.6 20.7 %collective-permute-start.12 = (f32[512,128]{1,0:T(8,128)S(1)}, f32[512,128]{1,0:T(8,128)S(1)}, u32[]{:S(2)}, u32[]{:S(2)}) collective-permute-start(f32[512,128]{1,0:T(8,128)S(1)} %get-tuple-element.47), channel_id=1, source_target_pairs={{0,4},{4,8},{8,12},{12,16},{16,20},{20,24},{24,28},{1,5},{5,9},{9,... | collective-permute-start | bytes 786440 | tf_op jit(solution)/shard_map/ppermute | solution.py:277
  36.3 17.3 %collective-permute-start.5 = (f32[512,128]{1,0:T(8,128)S(1)}, f32[512,128]{1,0:T(8,128)S(1)}, u32[]{:S(2)}, u32[]{:S(2)}) collective-permute-start(f32[512,128]{1,0:T(8,128)S(1)} %get-tuple-element.48), channel_id=1, source_target_pairs={{4,0},{8,4},{12,8},{16,12},{20,16},{24,20},{28,24},{5,1},{9,5},{13... | collective-permute-start | bytes 786440 | tf_op jit(solution)/shard_map/ppermute | solution.py:276
  39.6 18.3 %collective-permute-start.4 = (f32[512,128]{1,0:T(8,128)S(1)}, f32[512,128]{1,0:T(8,128)S(1)}, u32[]{:S(2)}, u32[]{:S(2)}) collective-permute-start(f32[512,128]{1,0:T(8,128)S(1)} %get-tuple-element.49), channel_id=1, source_target_pairs={{0,4},{4,8},{8,12},{12,16},{16,20},{20,24},{24,28},{1,5},{5,9},{9,... | collective-permute-start | bytes 786440 | tf_op jit(solution)/shard_map/ppermute | solution.py:277
  46.0 17.0 %collective-permute-start.6 = (f32[256,128]{1,0:T(8,128)}, f32[256,128]{1,0:T(8,128)S(1)}, u32[]{:S(2)}, u32[]{:S(2)}) collective-permute-start(f32[256,128]{1,0:T(8,128)} %get-tuple-element.29), channel_id=1, source_target_pairs={{0,1},{1,0},{2,3},{3,2},{4,5},{5,4},{6,7},{7,6},{8,9},{9,8},{10,11... | collective-permute-start | bytes 393224 | tf_op jit(solution)/shard_map/ppermute | solution.py:239
  47.0 16.0 %collective-permute-start.7 = (f32[256,128]{1,0:T(8,128)}, f32[256,128]{1,0:T(8,128)S(1)}, u32[]{:S(2)}, u32[]{:S(2)}) collective-permute-start(f32[256,128]{1,0:T(8,128)} %get-tuple-element.30), channel_id=1, source_target_pairs={{0,2},{1,3},{2,0},{3,1},{4,6},{5,7},{6,4},{7,5},{8,10},{9,11},{10,... | collective-permute-start | bytes 393224 | tf_op jit(solution)/shard_map/ppermute | solution.py:239
  52.3 10.7 %collective-permute-start.8 = (f32[256,128]{1,0:T(8,128)}, f32[256,128]{1,0:T(8,128)S(1)}, u32[]{:S(2)}, u32[]{:S(2)}) collective-permute-start(f32[256,128]{1,0:T(8,128)} %get-tuple-element.31), channel_id=1, source_target_pairs={{0,3},{1,2},{2,1},{3,0},{4,7},{5,6},{6,5},{7,4},{8,11},{9,10},{10,... | collective-permute-start | bytes 393224 | tf_op jit(solution)/shard_map/ppermute | solution.py:239
  52.8 10.2 %copy-start.4 = (f32[256,128]{1,0:T(8,128)S(1)}, f32[256,128]{1,0:T(8,128)}, u32[]{:S(2)}) copy-start(f32[256,128]{1,0:T(8,128)} %get-tuple-element.28.refs_8_) | copy-start | bytes 393220
  65.1 4.1 %collective-permute-start.17 = (f32[16,128]{1,0:T(8,128)S(1)}, f32[16,128]{1,0:T(8,128)S(1)}, u32[]{:S(2)}, u32[]{:S(2)}) collective-permute-start(f32[16,128]{1,0:T(8,128)S(1)} %get-tuple-element.41), channel_id=1, source_target_pairs={{0,4},{4,0},{8,12},{12,8},{16,20},{20,16},{24,28},{28,24},{1,5},{5... | collective-permute-start | bytes 24584 | tf_op jit(solution)/shard_map/ppermute | solution.py:317
  69.2 3.7 %collective-permute-start.18 = (f32[16,128]{1,0:T(8,128)S(1)}, f32[16,128]{1,0:T(8,128)S(1)}, u32[]{:S(2)}, u32[]{:S(2)}) collective-permute-start(f32[16,128]{1,0:T(8,128)S(1)} %add.6), channel_id=1, source_target_pairs={{0,8},{4,12},{8,0},{12,4},{16,24},{20,28},{24,16},{28,20},{1,9},{5... | collective-permute-start | bytes 24584 | tf_op jit(solution)/shard_map/ppermute | solution.py:317
  72.9 4.5 %collective-permute-start.19 = (f32[16,128]{1,0:T(8,128)S(1)}, f32[16,128]{1,0:T(8,128)S(1)}, u32[]{:S(2)}, u32[]{:S(2)}) collective-permute-start(f32[16,128]{1,0:T(8,128)S(1)} %add.7.refs_0_), channel_id=1, source_target_pairs={{0,16},{4,20},{8,24},{12,28},{16,0},{20,4},{24,8},{28,12},{1,17},{... | collective-permute-start | bytes 24584 | tf_op jit(solution)/shard_map/ppermute | solution.py:317

commit v3 on v2

--- a/solution.py
+++ b/solution.py
@@ -143,7 +143,7 @@
         grid[row, pl.ds(0, PAD), :] = zero
         grid[row, pl.ds(PAD + n * cb, PAD), :] = zero
     if lo:
-        sums[...] = prev[...]
+        sums[pl.ds(0, group), :] = prev[...]
     else:
         sums[...] = jnp.zeros(sums.shape, jnp.float32)
     lane = lax.broadcasted_iota(jnp.int32, (SUB, LANES), 1)
@@ -183,12 +183,18 @@
         return 0
 
     lax.fori_loop(0, n, source_step, 0)
+    for first in range(group, sums.shape[0], group):
+        sums[pl.ds(first, group), :] = sums[pl.ds(0, group), :]
 
 
 def scale_kernel(chunks, size, *refs):
-    mine, other, parts, out, norms, buf, out_sem = refs[0], refs[1], refs[2:-4], *refs[-4:]
-    group, per = mine.shape[0], out.shape[0] // mine.shape[0]
-    sums = jnp.sum(mine[...] + other[...], axis=1, keepdims=True)
+    total, parts, out, norms, buf, out_sem = refs[0], refs[1:-4], *refs[-4:]
+    group = sum(n for _, n in chunks)
+    per = out.shape[0] // group
+    sums = total[pl.ds(0, group), :]
+    for first in range(group, total.shape[0], group):
+        sums = sums + total[pl.ds(first, group), :]
+    sums = jnp.sum(sums, axis=1, keepdims=True)
     norm = jnp.sqrt(sums / size + 1e-06)
     lane = lax.broadcasted_iota(jnp.int32, (group, LANES), 1)
     sub = lax.broadcasted_iota(jnp.int32, (group, LANES), 0)
@@ -299,7 +305,7 @@
             functools.partial(defect_kernel, meta, lo, n, group, amplitude),
             out_shape=(
                 jax.ShapeDtypeStruct((n * per, LANES), jnp.float32),
-                jax.ShapeDtypeStruct((group, LANES), jnp.float32),
+                jax.ShapeDtypeStruct((group * peers if lo + n == group else group, LANES), jnp.float32),
             ),
             in_specs=[smem, vmem] + [vmem] * len(ins) + ([vmem] if lo else []),
             out_specs=(vmem, vmem),
@@ -311,18 +317,14 @@
             name="defect",
         )(source_index, weights, *ins, *([sums] if lo else []))
         parts.append(part)
-    step, other = 1, None
-    while step < peers:
-        sums = sums if other is None else sums + other
-        other = lax.ppermute(sums, "vtx", [(i, i ^ step) for i in range(peers)])
-        step *= 2
+    sums = lax.all_to_all(sums, "vtx", 0, 0, tiled=True)
     out, norms = pl.pallas_call(
         functools.partial(scale_kernel, chunks, float(total_rows * width)),
         out_shape=(
             jax.ShapeDtypeStruct((group * per, LANES), jnp.float32),
             jax.ShapeDtypeStruct((1, group), jnp.float32),
         ),
-        in_specs=[vmem, vmem] + [vmem] * len(parts),
+        in_specs=[vmem] + [vmem] * len(parts),
         out_specs=(pl.BlockSpec(memory_space=pltpu.HBM), vmem),
         scratch_shapes=[
             pltpu.VMEM((group * per + group, LANES), jnp.float32),
@@ -331,7 +333,7 @@
         cost_estimate=pl.CostEstimate(flops=group * per * LANES, bytes_accessed=8 * group * per * LANES, transcendentals=0),
         compiler_params=pltpu.CompilerParams(vmem_limit_bytes=12 << 20),
         name="scale",
-    )(sums, other, *parts)
+    )(sums, *parts)
     out = out.reshape(group, cb, rows_dev, LANES).transpose(0, 2, 1, 3).reshape(group, rows_dev, width)
     return out, norms.reshape(group)
 

time: 80.5 us -> 79.7 us (0.990)
  blocking collectives: 0 us -> 12.5 us
  starting transfers between devices: 31 us -> 24.3 us
  waiting for transfers between devices: 29.4 us -> 23.7 us
  Pallas kernels: 18.7 us -> 17.8 us
    all_to_all x0 -> x1, blocking collectives: none -> 12.5 us  [program(): sums = lax.all_to_all(sums, 'vtx', 0, 0, tiled=True)]
    ppermute x3 -> x0, starting transfers between devices: 6.68 us -> none  [program(): other = lax.ppermute(sums, 'vtx', [(i, i ^ step) for i in range(peers)])]
    ppermute x3 -> x0, waiting for transfers between devices: 5.67 us -> none  [program(): other = lax.ppermute(sums, 'vtx', [(i, i ^ step) for i in range(peers)])]
    pallas_call x2, Pallas kernels: 7.11 us -> 6.21 us  [program(): pl.pallas_call(functools.partial(defect_kernel, meta, lo, n, group, ampli...]
  transfers between devices with their start and end apart: 20 -> 17, of which waited for: 9 -> 6; matrix products, arithmetic and copies ran while one was open for 0% -> 0% of each run, Pallas kernels for 15% -> 14%
where the time goes in v3:
time: 79.7 us; the launch traced here: 79.4 us
  starting transfers between devices  24.3 us (30%)
  waiting for transfers between devices  23.7 us (30%)
  Pallas kernels  17.8 us (22%)
  blocking collectives  12.5 us (16%)
  between operations  0.84 us (1%)
    ppermute x12, waiting for transfers between devices, send(): lax.ppermute(piece, 'src', [(i, i ^ k) for i in range(senders)])  15.3 us
    all_to_all x1, blocking collectives, program(): sums = lax.all_to_all(sums, 'vtx', 0, 0, tiled=True)  12.5 us
    ppermute x12, starting transfers between devices, send(): lax.ppermute(piece, 'src', [(i, i ^ k) for i in range(senders)])  9.92 us
    ppermute x2, waiting for transfers between devices, program(): below.append(lax.ppermute(last, 'vtx', up))  8.42 us
    pallas_call x3, Pallas kernels, pack(): pl.pallas_call(functools.partial(pack_kernel, (tuple(plan), group, cb, ow...  8.16 us
    ppermute x2, starting transfers between devices, program(): below.append(lax.ppermute(last, 'vtx', up))  8.02 us
    pallas_call x2, Pallas kernels, program(): pl.pallas_call(functools.partial(defect_kernel, meta, lo, n, group, ampli...  6.21 us
    ppermute x1, starting transfers between devices, program(): lax.ppermute(cotan[2:4, rows_dev - 1].reshape(2 * cb, LANES), 'vtx', up)  3.83 us
  transfers between devices with their start and end apart: 17, of which 6 were waited for; matrix products, arithmetic and copies ran while one was open for 0% of the time, Pallas kernels for 14%

profile of v3, /device:TPU:0, one launch (start us, length us, event | category | flops | bytes accessed | tf_op | source)
XLA Modules:
  0.0 79.4 jit_solution(6795734982499049594)
XLA Ops:
  0.6 0.0 copy-start.1
  0.6 2.2 %shard_map.52 = (f32[512,128]{1,0:T(8,128)}, f32[512,128]{1,0:T(8,128)}) custom-call(f32[8192,128]{1,0:T(8,128)} %bitcast.22), custom_call_target="tpu_custom_call" | custom-call | flops 131072 | bytes 1572864 | tf_op jit(solution)/shard_map/pallas_call | solution.py:60
  2.8 3.1 %collective-permute-start.10 = (f32[512,128]{1,0:T(8,128)}, f32[512,128]{1,0:T(8,128)S(1)}, u32[]{:S(2)}, u32[]{:S(2)}) collective-permute-start(f32[512,128]{1,0:T(8,128)} %get-tuple-element.34), channel_id=1, source_target_pairs={{0,2},{1,3},{2,0},{3,1},{4,6},{5,7},{6,4},{7,5},{8,10},{9,11},{10,... | collective-permute-start | bytes 786440 | tf_op jit(solution)/shard_map/ppermute | solution.py:245
  5.9 0.0 collective-permute-start.11
  5.9 3.9 %shard_map.50 = (f32[512,128]{1,0:T(8,128)}, f32[512,128]{1,0:T(8,128)}, f32[512,128]{1,0:T(8,128)}, f32[512,128]{1,0:T(8,128)}, f32[768,128]{1,0:T(8,128)}, /*i...) custom-call(f32[8192,128]{1,0:T(8,128)} %bitcast.23), custom_call_target="tpu_custom_call" | custom-call | flops 786432 | bytes 7340032 | tf_op jit(solution)/shard_map/pallas_call | solution.py:60
  9.8 0.0 copy-start.2
  9.8 0.0 copy-start.6
  9.8 0.0 copy-start
  9.8 0.3 collective-permute-start.9
  10.1 0.0 copy-done.1
  10.1 0.1 slice.3
  10.2 3.8 %collective-permute-start = (f32[128,128]{1,0:T(8,128)S(1)}, f32[128,128]{1,0:T(8,128)S(1)}, u32[]{:S(2)}, u32[]{:S(2)}) collective-permute-start(f32[128,128]{1,0:T(8,128)S(1)} %bitcast.25), channel_id=1, source_target_pairs={{0,4},{4,8},{8,12},{12,16},{16,20},{20,24},{24,28},{1,5},{5,9},{9,... | collective-permute-start | bytes 196616 | tf_op jit(solution)/shard_map/ppermute | solution.py:267
  14.0 2.1 %shard_map.51 = (f32[512,128]{1,0:T(8,128)}, f32[512,128]{1,0:T(8,128)}) custom-call(f32[8192,128]{1,0:T(8,128)} %bitcast.24), custom_call_target="tpu_custom_call" | custom-call | flops 131072 | bytes 1572864 | tf_op jit(solution)/shard_map/pallas_call | solution.py:60
  16.1 0.0 copy-start.3
  16.1 0.0 copy-start.5
  16.1 1.6 %collective-permute-start.2 = (f32[512,128]{1,0:T(8,128)}, f32[512,128]{1,0:T(8,128)S(1)}, u32[]{:S(2)}, u32[]{:S(2)}) collective-permute-start(f32[512,128]{1,0:T(8,128)} %get-tuple-element.26), channel_id=1, source_target_pairs={{0,2},{1,3},{2,0},{3,1},{4,6},{5,7},{6,4},{7,5},{8,10},{9,11},{10,... | collective-permute-start | bytes 786440 | tf_op jit(solution)/shard_map/ppermute | solution.py:245
  17.7 0.0 collective-permute-done.lower
  17.7 0.0 collective-permute-start.3
  17.7 0.0 collective-permute-done.10.refs_4_
  17.7 0.6 collective-permute-start.1
  18.3 0.0 collective-permute-done.11.refs_5_
  18.3 0.1 collective-permute-start.14
  18.4 0.0 collective-permute-done.9.refs_3_
  18.4 1.5 %collective-permute-start.15 = (f32[768,128]{1,0:T(8,128)}, f32[768,128]{1,0:T(8,128)S(1)}, u32[]{:S(2)}, u32[]{:S(2)}) collective-permute-start(f32[768,128]{1,0:T(8,128)} %get-tuple-element.38), channel_id=1, source_target_pairs={{0,2},{1,3},{2,0},{3,1},{4,6},{5,7},{6,4},{7,5},{8,10},{9,11},{10,... | collective-permute-start | bytes 1179656 | tf_op jit(solution)/shard_map/ppermute | solution.py:245
  19.9 0.0 copy-done.2
  19.9 0.1 select_select_fusion
  20.0 5.6 %collective-permute-done.2.refs_10_.refs_4_ = f32[512,128]{1,0:T(8,128)S(1)} collective-permute-done((f32[512,128]{1,0:T(8,128)}, f32[512,128]{1,0:T(8,128)S(1)}, u32[]{:S(2)}, u32[]{:S(2)}) %collective-permute-start.2) | collective-permute-done | bytes 262176 | tf_op jit(solution)/shard_map/ppermute | solution.py:245
  25.5 0.0 copy-done.6
  25.5 0.0 collective-permute-start.16
  25.6 4.8 %collective-permute-done.3.refs_11_.refs_5_ = f32[512,128]{1,0:T(8,128)S(1)} collective-permute-done((f32[512,128]{1,0:T(8,128)}, f32[512,128]{1,0:T(8,128)S(1)}, u32[]{:S(2)}, u32[]{:S(2)}) %collective-permute-start.3) | collective-permute-done | bytes 262176 | tf_op jit(solution)/shard_map/ppermute | solution.py:245
  30.3 1.3 %collective-permute-start.13 = (f32[512,128]{1,0:T(8,128)S(1)}, f32[512,128]{1,0:T(8,128)S(1)}, u32[]{:S(2)}, u32[]{:S(2)}) collective-permute-start(f32[512,128]{1,0:T(8,128)S(1)} %get-tuple-element.46), channel_id=1, source_target_pairs={{4,0},{8,4},{12,8},{16,12},{20,16},{24,20},{28,24},{5,1},{9,5},{13... | collective-permute-start | bytes 786440 | tf_op jit(solution)/shard_map/ppermute | solution.py:282
  31.6 0.0 collective-permute-done.1.refs_9_.refs_3_
  31.6 4.6 %collective-permute-start.12 = (f32[512,128]{1,0:T(8,128)S(1)}, f32[512,128]{1,0:T(8,128)S(1)}, u32[]{:S(2)}, u32[]{:S(2)}) collective-permute-start(f32[512,128]{1,0:T(8,128)S(1)} %get-tuple-element.47), channel_id=1, source_target_pairs={{0,4},{4,8},{8,12},{12,16},{16,20},{20,24},{24,28},{1,5},{5,9},{9,... | collective-permute-start | bytes 786440 | tf_op jit(solution)/shard_map/ppermute | solution.py:283
  36.2 0.0 copy-done
  36.2 0.1 select_select_fusion.2
  36.3 0.0 collective-permute-done.14.refs_15_
  36.3 1.3 %collective-permute-start.5 = (f32[512,128]{1,0:T(8,128)S(1)}, f32[512,128]{1,0:T(8,128)S(1)}, u32[]{:S(2)}, u32[]{:S(2)}) collective-permute-start(f32[512,128]{1,0:T(8,128)S(1)} %get-tuple-element.48), channel_id=1, source_target_pairs={{4,0},{8,4},{12,8},{16,12},{20,16},{24,20},{28,24},{5,1},{9,5},{13... | collective-permute-start | bytes 786440 | tf_op jit(solution)/shard_map/ppermute | solution.py:282
  37.6 2.0 %collective-permute-done.15.refs_16_ = f32[768,128]{1,0:T(8,128)S(1)} collective-permute-done((f32[768,128]{1,0:T(8,128)}, f32[768,128]{1,0:T(8,128)S(1)}, u32[]{:S(2)}, u32[]{:S(2)}) %collective-permute-start.15) | collective-permute-done | bytes 393248 | tf_op jit(solution)/shard_map/ppermute | solution.py:245
  39.6 3.5 %collective-permute-start.4 = (f32[512,128]{1,0:T(8,128)S(1)}, f32[512,128]{1,0:T(8,128)S(1)}, u32[]{:S(2)}, u32[]{:S(2)}) collective-permute-start(f32[512,128]{1,0:T(8,128)S(1)} %get-tuple-element.49), channel_id=1, source_target_pairs={{0,4},{4,8},{8,12},{12,16},{16,20},{20,24},{24,28},{1,5},{5,9},{9,... | collective-permute-start | bytes 786440 | tf_op jit(solution)/shard_map/ppermute | solution.py:283
  43.1 2.9 %collective-permute-done.16.refs_17_ = f32[768,128]{1,0:T(8,128)S(1)} collective-permute-done((f32[768,128]{1,0:T(8,128)S(1)}, f32[768,128]{1,0:T(8,128)S(1)}, u32[]{:S(2)}, u32[]{:S(2)}) %collective-permute-start.16) | collective-permute-done | bytes 393248 | tf_op jit(solution)/shard_map/ppermute | solution.py:245
  46.0 1.1 %collective-permute-start.6 = (f32[256,128]{1,0:T(8,128)}, f32[256,128]{1,0:T(8,128)S(1)}, u32[]{:S(2)}, u32[]{:S(2)}) collective-permute-start(f32[256,128]{1,0:T(8,128)} %get-tuple-element.29), channel_id=1, source_target_pairs={{0,1},{1,0},{2,3},{3,2},{4,5},{5,4},{6,7},{7,6},{8,9},{9,8},{10,11... | collective-permute-start | bytes 393224 | tf_op jit(solution)/shard_map/ppermute | solution.py:245
  47.0 0.0 collective-permute-done.13.refs_7_
  47.0 1.2 %collective-permute-start.7 = (f32[256,128]{1,0:T(8,128)}, f32[256,128]{1,0:T(8,128)S(1)}, u32[]{:S(2)}, u32[]{:S(2)}) collective-permute-start(f32[256,128]{1,0:T(8,128)} %get-tuple-element.30), channel_id=1, source_target_pairs={{0,2},{1,3},{2,0},{3,1},{4,6},{5,7},{6,4},{7,5},{8,10},{9,11},{10,... | collective-permute-start | bytes 393224 | tf_op jit(solution)/shard_map/ppermute | solution.py:245
  48.3 4.1 %collective-permute-done.12.refs_6_ = f32[512,128]{1,0:T(8,128)S(1)} collective-permute-done((f32[512,128]{1,0:T(8,128)S(1)}, f32[512,128]{1,0:T(8,128)S(1)}, u32[]{:S(2)}, u32[]{:S(2)}) %collective-permute-start.12) | collective-permute-done | bytes 262176 | tf_op jit(solution)/shard_map/ppermute | solution.py:283
  52.3 0.5 collective-permute-start.8
  52.8 0.0 copy-start.4
  52.8 0.7 weights.1.refs_1_
  53.6 0.0 collective-permute-done.5.refs_13_.refs_7_
  53.6 4.4 %collective-permute-done.4.refs_12_.refs_6_ = f32[512,128]{1,0:T(8,128)S(1)} collective-permute-done((f32[512,128]{1,0:T(8,128)S(1)}, f32[512,128]{1,0:T(8,128)S(1)}, u32[]{:S(2)}, u32[]{:S(2)}) %collective-permute-start.4) | collective-permute-done | bytes 262176 | tf_op jit(solution)/shard_map/ppermute | solution.py:283
  57.9 0.0 copy-done.3
  57.9 0.0 copy-done.5
  57.9 4.4 %defect.2 = (f32[6144,128]{1,0:T(8,128)S(1)}, f32[16,128]{1,0:T(8,128)S(1)}) custom-call(s32[64]{0:T(128)S(1)} %copy-done.5, f32[7,8,72,128]{3,2,1,0:T(8,128)S(1)} %weights.1.refs_1_, f32[512,128]{1,0:T(8,128)S(1)} %copy-done.2, f32[512,128]{1,0:T(8,128)S(1)} %collective-permute-done.9.refs_3_, f32[512,128]{1,0:T(8,128)S(1)} %collective-permute-done.10.refs_4_, ...), custom_call_target="tpu_custom_call" | custom-call | flops 15728640 | bytes 6291456 | tf_op jit(solution)/shard_map/defect/pallas_call | solution.py:304
  62.3 0.0 collective-permute-done.6.refs_9_
  62.3 0.0 collective-permute-done.7.refs_10_
  62.3 0.0 collective-permute-done.8.refs_11_
  62.3 0.0 copy-done.4
  62.4 1.8 %defect.3 = (f32[2048,128]{1,0:T(8,128)S(1)}, f32[128,128]{1,0:T(8,128)S(1)}) custom-call(s32[64]{0:T(128)S(1)} %copy-done.5, f32[7,8,72,128]{3,2,1,0:T(8,128)S(1)} %weights.1.refs_1_, f32[512,128]{1,0:T(8,128)S(1)} %copy-done, f32[512,128]{1,0:T(8,128)S(1)} %collective-permute-done.1.refs_9_.refs_3_, ...), custom_call_target="tpu_custom_call" | custom-call | flops 5242880 | bytes 2097152 | tf_op jit(solution)/shard_map/defect/pallas_call | solution.py:304
  64.2 12.5 %all_to_all.11 = f32[8,16,128]{2,1,0:T(8,128)S(1)} all-to-all(f32[8,16,128]{2,1,0:T(8,128)S(1)} %bitcast.21), channel_id=1, replica_groups=mesh['vtx'=8,'src'=4] {'vtx'}, dimensions={0} | all-to-all | bytes 131072 | tf_op jit(solution)/shard_map/all_to_all | solution.py:320
  76.6 2.8 %scale.1 = (f32[8192,128]{1,0:T(8,128)}, f32[1,16]{1,0:T(1,128)}) custom-call(f32[128,128]{1,0:T(8,128)S(1)} %bitcast.20, f32[6144,128]{1,0:T(8,128)S(1)} %get-tuple-element.42.refs_1_, f32[2048,128]{1,0:T(8,128)S(1)} %get-tuple-element.43.refs_2_), custom_call_target="tpu_custom_call" | custom-call | flops 1048576 | bytes 8388608 | tf_op jit(solution)/shard_map/scale/pallas_call | solution.py:321
Async XLA Ops:
  0.6 9.5 %copy-start.1 = (f32[4,8,8192]{2,1,0:T(8,128)S(1)}, f32[4,8,8192]{2,1,0:T(8,128)}, u32[]{:S(2)}) copy-start(f32[4,8,8192]{2,1,0:T(8,128)} %param.4) | copy-start | bytes 3145732
  2.8 14.9 %collective-permute-start.10 = (f32[512,128]{1,0:T(8,128)}, f32[512,128]{1,0:T(8,128)S(1)}, u32[]{:S(2)}, u32[]{:S(2)}) collective-permute-start(f32[512,128]{1,0:T(8,128)} %get-tuple-element.34), channel_id=1, source_target_pairs={{0,2},{1,3},{2,0},{3,1},{4,6},{5,7},{6,4},{7,5},{8,10},{9,11},{10,... | collective-permute-start | bytes 786440 | tf_op jit(solution)/shard_map/ppermute | solution.py:245
  5.9 12.4 %collective-permute-start.11 = (f32[512,128]{1,0:T(8,128)}, f32[512,128]{1,0:T(8,128)S(1)}, u32[]{:S(2)}, u32[]{:S(2)}) collective-permute-start(f32[512,128]{1,0:T(8,128)} %get-tuple-element.35), channel_id=1, source_target_pairs={{0,3},{1,2},{2,1},{3,0},{4,7},{5,6},{6,5},{7,4},{8,11},{9,10},{10,... | collective-permute-start | bytes 786440 | tf_op jit(solution)/shard_map/ppermute | solution.py:245
  9.8 10.1 %copy-start.2 = (f32[512,128]{1,0:T(8,128)S(1)}, f32[512,128]{1,0:T(8,128)}, u32[]{:S(2)}) copy-start(f32[512,128]{1,0:T(8,128)} %get-tuple-element.32.refs_2_) | copy-start | bytes 786436
  9.8 15.7 %copy-start.6 = (f32[768,128]{1,0:T(8,128)S(1)}, f32[768,128]{1,0:T(8,128)}, u32[]{:S(2)}) copy-start(f32[768,128]{1,0:T(8,128)} %get-tuple-element.39) | copy-start | bytes 1179652
  9.8 26.3 %copy-start = (f32[512,128]{1,0:T(8,128)S(1)}, f32[512,128]{1,0:T(8,128)}, u32[]{:S(2)}) copy-start(f32[512,128]{1,0:T(8,128)} %get-tuple-element.24.refs_8_.refs_2_) | copy-start | bytes 786436
  9.8 8.5 %collective-permute-start.9 = (f32[512,128]{1,0:T(8,128)}, f32[512,128]{1,0:T(8,128)S(1)}, u32[]{:S(2)}, u32[]{:S(2)}) collective-permute-start(f32[512,128]{1,0:T(8,128)} %get-tuple-element.33), channel_id=1, source_target_pairs={{0,1},{1,0},{2,3},{3,2},{4,5},{5,4},{6,7},{7,6},{8,9},{9,8},{10,11... | collective-permute-start | bytes 786440 | tf_op jit(solution)/shard_map/ppermute | solution.py:245
  10.2 7.5 %collective-permute-start = (f32[128,128]{1,0:T(8,128)S(1)}, f32[128,128]{1,0:T(8,128)S(1)}, u32[]{:S(2)}, u32[]{:S(2)}) collective-permute-start(f32[128,128]{1,0:T(8,128)S(1)} %bitcast.25), channel_id=1, source_target_pairs={{0,4},{4,8},{8,12},{12,16},{16,20},{20,24},{24,28},{1,5},{5,9},{9,... | collective-permute-start | bytes 196616 | tf_op jit(solution)/shard_map/ppermute | solution.py:267
  16.1 41.9 %copy-start.3 = (f32[768,128]{1,0:T(8,128)S(1)}, f32[768,128]{1,0:T(8,128)}, u32[]{:S(2)}) copy-start(f32[768,128]{1,0:T(8,128)} %get-tuple-element.36.refs_14_) | copy-start | bytes 1179652
  16.1 41.9 %copy-start.5 = (s32[64]{0:T(128)S(1)}, s32[64]{0:T(128)}, u32[]{:S(2)}) copy-start(s32[64]{0:T(128)} %refs_0_.3) | copy-start | bytes 772
  16.1 9.5 %collective-permute-start.2 = (f32[512,128]{1,0:T(8,128)}, f32[512,128]{1,0:T(8,128)S(1)}, u32[]{:S(2)}, u32[]{:S(2)}) collective-permute-start(f32[512,128]{1,0:T(8,128)} %get-tuple-element.26), channel_id=1, source_target_pairs={{0,2},{1,3},{2,0},{3,1},{4,6},{5,7},{6,4},{7,5},{8,10},{9,11},{10,... | collective-permute-start | bytes 786440 | tf_op jit(solution)/shard_map/ppermute | solution.py:245
  17.7 12.6 %collective-permute-start.3 = (f32[512,128]{1,0:T(8,128)}, f32[512,128]{1,0:T(8,128)S(1)}, u32[]{:S(2)}, u32[]{:S(2)}) collective-permute-start(f32[512,128]{1,0:T(8,128)} %get-tuple-element.27), channel_id=1, source_target_pairs={{0,3},{1,2},{2,1},{3,0},{4,7},{5,6},{6,5},{7,4},{8,11},{9,10},{10,... | collective-permute-start | bytes 786440 | tf_op jit(solution)/shard_map/ppermute | solution.py:245
  17.7 13.9 %collective-permute-start.1 = (f32[512,128]{1,0:T(8,128)}, f32[512,128]{1,0:T(8,128)S(1)}, u32[]{:S(2)}, u32[]{:S(2)}) collective-permute-start(f32[512,128]{1,0:T(8,128)} %get-tuple-element.25), channel_id=1, source_target_pairs={{0,1},{1,0},{2,3},{3,2},{4,5},{5,4},{6,7},{7,6},{8,9},{9,8},{10,11... | collective-permute-start | bytes 786440 | tf_op jit(solution)/shard_map/ppermute | solution.py:245
  18.3 18.0 %collective-permute-start.14 = (f32[768,128]{1,0:T(8,128)}, f32[768,128]{1,0:T(8,128)S(1)}, u32[]{:S(2)}, u32[]{:S(2)}) collective-permute-start(f32[768,128]{1,0:T(8,128)} %get-tuple-element.37), channel_id=1, source_target_pairs={{0,1},{1,0},{2,3},{3,2},{4,5},{5,4},{6,7},{7,6},{8,9},{9,8},{10,11... | collective-permute-start | bytes 1179656 | tf_op jit(solution)/shard_map/ppermute | solution.py:245
  18.4 21.2 %collective-permute-start.15 = (f32[768,128]{1,0:T(8,128)}, f32[768,128]{1,0:T(8,128)S(1)}, u32[]{:S(2)}, u32[]{:S(2)}) collective-permute-start(f32[768,128]{1,0:T(8,128)} %get-tuple-element.38), channel_id=1, source_target_pairs={{0,2},{1,3},{2,0},{3,1},{4,6},{5,7},{6,4},{7,5},{8,10},{9,11},{10,... | collective-permute-start | bytes 1179656 | tf_op jit(solution)/shard_map/ppermute | solution.py:245
  25.5 20.4 %collective-permute-start.16 = (f32[768,128]{1,0:T(8,128)S(1)}, f32[768,128]{1,0:T(8,128)S(1)}, u32[]{:S(2)}, u32[]{:S(2)}) collective-permute-start(f32[768,128]{1,0:T(8,128)S(1)} %copy-done.6), channel_id=1, source_target_pairs={{0,3},{1,2},{2,1},{3,0},{4,7},{5,6},{6,5},{7,4},{8,11},{9,10},{10,... | collective-permute-start | bytes 1179656 | tf_op jit(solution)/shard_map/ppermute | solution.py:245
  30.3 16.7 %collective-permute-start.13 = (f32[512,128]{1,0:T(8,128)S(1)}, f32[512,128]{1,0:T(8,128)S(1)}, u32[]{:S(2)}, u32[]{:S(2)}) collective-permute-start(f32[512,128]{1,0:T(8,128)S(1)} %get-tuple-element.46), channel_id=1, source_target_pairs={{4,0},{8,4},{12,8},{16,12},{20,16},{24,20},{28,24},{5,1},{9,5},{13... | collective-permute-start | bytes 786440 | tf_op jit(solution)/shard_map/ppermute | solution.py:282
  31.6 20.7 %collective-permute-start.12 = (f32[512,128]{1,0:T(8,128)S(1)}, f32[512,128]{1,0:T(8,128)S(1)}, u32[]{:S(2)}, u32[]{:S(2)}) collective-permute-start(f32[512,128]{1,0:T(8,128)S(1)} %get-tuple-element.47), channel_id=1, source_target_pairs={{0,4},{4,8},{8,12},{12,16},{16,20},{20,24},{24,28},{1,5},{5,9},{9,... | collective-permute-start | bytes 786440 | tf_op jit(solution)/shard_map/ppermute | solution.py:283
  36.3 17.3 %collective-permute-start.5 = (f32[512,128]{1,0:T(8,128)S(1)}, f32[512,128]{1,0:T(8,128)S(1)}, u32[]{:S(2)}, u32[]{:S(2)}) collective-permute-start(f32[512,128]{1,0:T(8,128)S(1)} %get-tuple-element.48), channel_id=1, source_target_pairs={{4,0},{8,4},{12,8},{16,12},{20,16},{24,20},{28,24},{5,1},{9,5},{13... | collective-permute-start | bytes 786440 | tf_op jit(solution)/shard_map/ppermute | solution.py:282
  39.6 18.3 %collective-permute-start.4 = (f32[512,128]{1,0:T(8,128)S(1)}, f32[512,128]{1,0:T(8,128)S(1)}, u32[]{:S(2)}, u32[]{:S(2)}) collective-permute-start(f32[512,128]{1,0:T(8,128)S(1)} %get-tuple-element.49), channel_id=1, source_target_pairs={{0,4},{4,8},{8,12},{12,16},{16,20},{20,24},{24,28},{1,5},{5,9},{9,... | collective-permute-start | bytes 786440 | tf_op jit(solution)/shard_map/ppermute | solution.py:283
  46.0 16.4 %collective-permute-start.6 = (f32[256,128]{1,0:T(8,128)}, f32[256,128]{1,0:T(8,128)S(1)}, u32[]{:S(2)}, u32[]{:S(2)}) collective-permute-start(f32[256,128]{1,0:T(8,128)} %get-tuple-element.29), channel_id=1, source_target_pairs={{0,1},{1,0},{2,3},{3,2},{4,5},{5,4},{6,7},{7,6},{8,9},{9,8},{10,11... | collective-permute-start | bytes 393224 | tf_op jit(solution)/shard_map/ppermute | solution.py:245
  47.0 15.3 %collective-permute-start.7 = (f32[256,128]{1,0:T(8,128)}, f32[256,128]{1,0:T(8,128)S(1)}, u32[]{:S(2)}, u32[]{:S(2)}) collective-permute-start(f32[256,128]{1,0:T(8,128)} %get-tuple-element.30), channel_id=1, source_target_pairs={{0,2},{1,3},{2,0},{3,1},{4,6},{5,7},{6,4},{7,5},{8,10},{9,11},{10,... | collective-permute-start | bytes 393224 | tf_op jit(solution)/shard_map/ppermute | solution.py:245
  52.3 10.0 %collective-permute-start.8 = (f32[256,128]{1,0:T(8,128)}, f32[256,128]{1,0:T(8,128)S(1)}, u32[]{:S(2)}, u32[]{:S(2)}) collective-permute-start(f32[256,128]{1,0:T(8,128)} %get-tuple-element.31), channel_id=1, source_target_pairs={{0,3},{1,2},{2,1},{3,0},{4,7},{5,6},{6,5},{7,4},{8,11},{9,10},{10,... | collective-permute-start | bytes 393224 | tf_op jit(solution)/shard_map/ppermute | solution.py:245
  52.8 9.5 %copy-start.4 = (f32[256,128]{1,0:T(8,128)S(1)}, f32[256,128]{1,0:T(8,128)}, u32[]{:S(2)}) copy-start(f32[256,128]{1,0:T(8,128)} %get-tuple-element.28.refs_8_) | copy-start | bytes 393220

commit v4 on v3

--- a/solution.py
+++ b/solution.py
@@ -188,7 +188,7 @@
 
 
 def scale_kernel(chunks, size, *refs):
-    total, parts, out, norms, buf, out_sem = refs[0], refs[1:-4], *refs[-4:]
+    total, parts, out, norms, buf, spread, out_sem = refs[0], refs[1:-5], *refs[-5:]
     group = sum(n for _, n in chunks)
     per = out.shape[0] // group
     sums = total[pl.ds(0, group), :]
@@ -198,8 +198,10 @@
     norm = jnp.sqrt(sums / size + 1e-06)
     lane = lax.broadcasted_iota(jnp.int32, (group, LANES), 1)
     sub = lax.broadcasted_iota(jnp.int32, (group, LANES), 0)
-    spread = jnp.where(lane == sub, jnp.broadcast_to(norm, (group, LANES)), 0.0)
-    norms[...] = jnp.sum(spread, axis=0, keepdims=True)[:, :group]
+    diagonal = jnp.where(lane == sub, jnp.broadcast_to(norm, (group, LANES)), 0.0)
+    spread[...] = jnp.sum(diagonal, axis=0, keepdims=True)[:, :group]
+    norms_copy = pltpu.make_async_copy(spread, norms, out_sem.at[group])
+    norms_copy.start()
     buf[pl.ds(group * per, group), :] = jnp.broadcast_to(1.0 / norm, (group, LANES))
 
     def copy_of(i):
@@ -223,6 +225,7 @@
         return 0
 
     lax.fori_loop(0, group, finish, 0)
+    norms_copy.wait()
 
 
 def program(heat, cotan, source_index):
@@ -238,7 +241,8 @@
     outer_rows = (0, own_rows - 1)
     order = [k for k in range(1, senders) if k >= 2] + [1]
     halves = [(0, group // 2), (group // 2, group - group // 2)]
-    chunks = [(0, group - group // 4), (group - group // 4, group // 4)]
+    cuts = (0, group // 2, group - group * 3 // 16, group)
+    chunks = [(lo, hi - lo) for lo, hi in zip(cuts[:-1], cuts[1:], strict=True) if hi > lo]
     common = (group, cb, own_rows, senders)
 
     def send(k, piece):
@@ -325,10 +329,11 @@
             jax.ShapeDtypeStruct((1, group), jnp.float32),
         ),
         in_specs=[vmem] + [vmem] * len(parts),
-        out_specs=(pl.BlockSpec(memory_space=pltpu.HBM), vmem),
+        out_specs=(pl.BlockSpec(memory_space=pltpu.HBM), pl.BlockSpec(memory_space=pltpu.HBM)),
         scratch_shapes=[
             pltpu.VMEM((group * per + group, LANES), jnp.float32),
-            pltpu.SemaphoreType.DMA((group,)),
+            pltpu.VMEM((1, group), jnp.float32),
+            pltpu.SemaphoreType.DMA((group + 1,)),
         ],
         cost_estimate=pl.CostEstimate(flops=group * per * LANES, bytes_accessed=8 * group * per * LANES, transcendentals=0),
         compiler_params=pltpu.CompilerParams(vmem_limit_bytes=12 << 20),

time: 79.7 us -> 91.6 us (1.15)
  waiting for transfers between devices: 23.7 us -> 31.1 us
  starting transfers between devices: 24.3 us -> 27.2 us
    ppermute x12 -> x15, waiting for transfers between devices: 15.3 us -> 22.4 us  [send(): lax.ppermute(piece, 'src', [(i, i ^ k) for i in range(senders)])]
    ppermute x12 -> x15, starting transfers between devices: 9.92 us -> 13.2 us  [send(): lax.ppermute(piece, 'src', [(i, i ^ k) for i in range(senders)])]
    pallas_call x2 -> x3, Pallas kernels: 6.21 us -> 7.58 us  [program(): pl.pallas_call(functools.partial(defect_kernel, meta, lo, n, group, ampli...]
  transfers between devices with their start and end apart: 17 -> 20, of which waited for: 6 -> 4; matrix products, arithmetic and copies ran while one was open for 0% -> 0% of each run, Pallas kernels for 14% -> 12%
where the time goes in v4:
time: 91.6 us; the launch traced here: 91.2 us
  waiting for transfers between devices  31.1 us (34%)
  starting transfers between devices  27.2 us (30%)
  Pallas kernels  18.6 us (20%)
  blocking collectives  13 us (14%)
  between operations  0.99 us (1%)
    ppermute x15, waiting for transfers between devices, send(): lax.ppermute(piece, 'src', [(i, i ^ k) for i in range(senders)])  22.4 us
    ppermute x15, starting transfers between devices, send(): lax.ppermute(piece, 'src', [(i, i ^ k) for i in range(senders)])  13.2 us
    all_to_all x1, blocking collectives, program(): sums = lax.all_to_all(sums, 'vtx', 0, 0, tiled=True)  13 us
    ppermute x2, waiting for transfers between devices, program(): below.append(lax.ppermute(last, 'vtx', up))  8.78 us
    pallas_call x3, Pallas kernels, pack(): pl.pallas_call(functools.partial(pack_kernel, (tuple(plan), group, cb, ow...  8.08 us
    ppermute x2, starting transfers between devices, program(): below.append(lax.ppermute(last, 'vtx', up))  7.97 us
    pallas_call x3, Pallas kernels, program(): pl.pallas_call(functools.partial(defect_kernel, meta, lo, n, group, ampli...  7.58 us
    ppermute x1, starting transfers between devices, program(): lax.ppermute(cotan[2:4, rows_dev - 1].reshape(2 * cb, LANES), 'vtx', up)  3.53 us
  transfers between devices with their start and end apart: 20, of which 4 were waited for; matrix products, arithmetic and copies ran while one was open for 0% of the time, Pallas kernels for 12%

profile of v4, /device:TPU:0, one launch (start us, length us, event | category | flops | bytes accessed | tf_op | source)
XLA Modules:
  0.0 91.2 jit_solution(8604177811687665148)
XLA Ops:
  0.6 4.0 %shard_map.50 = (f32[512,128]{1,0:T(8,128)}, f32[512,128]{1,0:T(8,128)}, f32[512,128]{1,0:T(8,128)}, f32[512,128]{1,0:T(8,128)}, f32[512,128]{1,0:T(8,128)}, /*i...) custom-call(f32[8192,128]{1,0:T(8,128)} %bitcast.22), custom_call_target="tpu_custom_call" | custom-call | flops 786432 | bytes 7340032 | tf_op jit(solution)/shard_map/pallas_call | solution.py:60
  4.6 0.0 copy-start.1
  4.6 0.6 collective-permute-start.12
  5.2 2.0 %shard_map.52 = (f32[512,128]{1,0:T(8,128)}, f32[512,128]{1,0:T(8,128)}) custom-call(f32[8192,128]{1,0:T(8,128)} %bitcast.23), custom_call_target="tpu_custom_call" | custom-call | flops 131072 | bytes 1572864 | tf_op jit(solution)/shard_map/pallas_call | solution.py:60
  7.2 2.7 %collective-permute-start.13 = (f32[512,128]{1,0:T(8,128)}, f32[512,128]{1,0:T(8,128)S(1)}, u32[]{:S(2)}, u32[]{:S(2)}) collective-permute-start(f32[512,128]{1,0:T(8,128)} %get-tuple-element.44), channel_id=1, source_target_pairs={{0,2},{1,3},{2,0},{3,1},{4,6},{5,7},{6,4},{7,5},{8,10},{9,11},{10,... | collective-permute-start | bytes 786440 | tf_op jit(solution)/shard_map/ppermute | solution.py:249
  9.9 0.1 collective-permute-start.14
  10.0 1.7 %collective-permute-start.10 = (f32[320,128]{1,0:T(8,128)}, f32[320,128]{1,0:T(8,128)S(1)}, u32[]{:S(2)}, u32[]{:S(2)}) collective-permute-start(f32[320,128]{1,0:T(8,128)} %get-tuple-element.40), channel_id=1, source_target_pairs={{0,2},{1,3},{2,0},{3,1},{4,6},{5,7},{6,4},{7,5},{8,10},{9,11},{10,... | collective-permute-start | bytes 491528 | tf_op jit(solution)/shard_map/ppermute | solution.py:249
  11.7 0.0 copy-done.1
  11.7 0.1 slice.3
  11.7 0.0 copy-start.2
  11.7 0.0 copy-start.9
  11.8 3.5 %collective-permute-start = (f32[128,128]{1,0:T(8,128)S(1)}, f32[128,128]{1,0:T(8,128)S(1)}, u32[]{:S(2)}, u32[]{:S(2)}) collective-permute-start(f32[128,128]{1,0:T(8,128)S(1)} %bitcast.25), channel_id=1, source_target_pairs={{0,4},{4,8},{8,12},{12,16},{16,20},{20,24},{24,28},{1,5},{5,9},{9,... | collective-permute-start | bytes 196616 | tf_op jit(solution)/shard_map/ppermute | solution.py:271
  15.3 2.1 %shard_map.51 = (f32[512,128]{1,0:T(8,128)}, f32[512,128]{1,0:T(8,128)}) custom-call(f32[8192,128]{1,0:T(8,128)} %bitcast.24), custom_call_target="tpu_custom_call" | custom-call | flops 131072 | bytes 1572864 | tf_op jit(solution)/shard_map/pallas_call | solution.py:60
  17.4 0.0 copy-start.10
  17.4 0.0 copy-start.12
  17.4 0.0 copy-start.11
  17.4 0.0 collective-permute-done.lower
  17.4 0.1 collective-permute-start.1
  17.5 8.6 %collective-permute-done.10.refs_10_ = f32[320,128]{1,0:T(8,128)S(1)} collective-permute-done((f32[320,128]{1,0:T(8,128)}, f32[320,128]{1,0:T(8,128)S(1)}, u32[]{:S(2)}, u32[]{:S(2)}) %collective-permute-start.10) | collective-permute-done | bytes 163872 | tf_op jit(solution)/shard_map/ppermute | solution.py:249
  26.1 1.7 %collective-permute-start.2 = (f32[512,128]{1,0:T(8,128)}, f32[512,128]{1,0:T(8,128)S(1)}, u32[]{:S(2)}, u32[]{:S(2)}) collective-permute-start(f32[512,128]{1,0:T(8,128)} %get-tuple-element.32), channel_id=1, source_target_pairs={{0,2},{1,3},{2,0},{3,1},{4,6},{5,7},{6,4},{7,5},{8,10},{9,11},{10,... | collective-permute-start | bytes 786440 | tf_op jit(solution)/shard_map/ppermute | solution.py:249
  27.9 0.0 collective-permute-done.12.refs_3_
  27.9 0.0 collective-permute-start.3
  27.9 0.0 collective-permute-done.13.refs_4_
  27.9 1.7 %collective-permute-start.11 = (f32[320,128]{1,0:T(8,128)}, f32[320,128]{1,0:T(8,128)S(1)}, u32[]{:S(2)}, u32[]{:S(2)}) collective-permute-start(f32[320,128]{1,0:T(8,128)} %get-tuple-element.41), channel_id=1, source_target_pairs={{0,3},{1,2},{2,1},{3,0},{4,7},{5,6},{6,5},{7,4},{8,11},{9,10},{10,... | collective-permute-start | bytes 491528 | tf_op jit(solution)/shard_map/ppermute | solution.py:249
  29.6 0.0 collective-permute-done.14.refs_5_
  29.6 0.0 collective-permute-start.9
  29.6 0.1 select_select_fusion
  29.7 12.9 %collective-permute-done.11.refs_11_ = f32[320,128]{1,0:T(8,128)S(1)} collective-permute-done((f32[320,128]{1,0:T(8,128)}, f32[320,128]{1,0:T(8,128)S(1)}, u32[]{:S(2)}, u32[]{:S(2)}) %collective-permute-start.11) | collective-permute-done | bytes 163872 | tf_op jit(solution)/shard_map/ppermute | solution.py:249
  42.6 0.7 collective-permute-start.17
  43.3 0.0 collective-permute-done.9.refs_9_
  43.3 0.0 copy-done.8
  43.3 1.5 %collective-permute-start.18 = (f32[512,128]{1,0:T(8,128)S(1)}, f32[512,128]{1,0:T(8,128)S(1)}, u32[]{:S(2)}, u32[]{:S(2)}) collective-permute-start(f32[512,128]{1,0:T(8,128)S(1)} %copy-done.8), channel_id=1, source_target_pairs={{0,2},{1,3},{2,0},{3,1},{4,6},{5,7},{6,4},{7,5},{8,10},{9,11},{10,... | collective-permute-start | bytes 786440 | tf_op jit(solution)/shard_map/ppermute | solution.py:249
  44.8 0.0 collective-permute-done.1.refs_3_
  44.8 0.0 collective-permute-start.19
  44.8 0.0 collective-permute-done.2.refs_4_
  44.8 3.4 %collective-permute-start.15 = (f32[512,128]{1,0:T(8,128)S(1)}, f32[512,128]{1,0:T(8,128)S(1)}, u32[]{:S(2)}, u32[]{:S(2)}) collective-permute-start(f32[512,128]{1,0:T(8,128)S(1)} %get-tuple-element.59), channel_id=1, source_target_pairs={{0,4},{4,8},{8,12},{12,16},{16,20},{20,24},{24,28},{1,5},{5,9},{9,... | collective-permute-start | bytes 786440 | tf_op jit(solution)/shard_map/ppermute | solution.py:287
  48.2 0.0 collective-permute-done.3.refs_5_
  48.3 1.3 %collective-permute-start.16 = (f32[512,128]{1,0:T(8,128)S(1)}, f32[512,128]{1,0:T(8,128)S(1)}, u32[]{:S(2)}, u32[]{:S(2)}) collective-permute-start(f32[512,128]{1,0:T(8,128)S(1)} %get-tuple-element.58), channel_id=1, source_target_pairs={{4,0},{8,4},{12,8},{16,12},{20,16},{24,20},{28,24},{5,1},{9,5},{13... | collective-permute-start | bytes 786440 | tf_op jit(solution)/shard_map/ppermute | solution.py:286
  49.6 0.0 copy-start.6
  49.6 0.1 select_select_fusion.2
  49.7 0.0 collective-permute-done.17.refs_9_
  49.7 4.6 %collective-permute-start.4 = (f32[512,128]{1,0:T(8,128)S(1)}, f32[512,128]{1,0:T(8,128)S(1)}, u32[]{:S(2)}, u32[]{:S(2)}) collective-permute-start(f32[512,128]{1,0:T(8,128)S(1)} %get-tuple-element.61), channel_id=1, source_target_pairs={{0,4},{4,8},{8,12},{12,16},{16,20},{20,24},{24,28},{1,5},{5,9},{9,... | collective-permute-start | bytes 786440 | tf_op jit(solution)/shard_map/ppermute | solution.py:287
  54.2 0.0 collective-permute-done.18.refs_10_
  54.3 1.3 %collective-permute-start.5 = (f32[512,128]{1,0:T(8,128)S(1)}, f32[512,128]{1,0:T(8,128)S(1)}, u32[]{:S(2)}, u32[]{:S(2)}) collective-permute-start(f32[512,128]{1,0:T(8,128)S(1)} %get-tuple-element.60), channel_id=1, source_target_pairs={{4,0},{8,4},{12,8},{16,12},{20,16},{24,20},{28,24},{5,1},{9,5},{13... | collective-permute-start | bytes 786440 | tf_op jit(solution)/shard_map/ppermute | solution.py:286
  55.6 0.8 collective-permute-done.19.refs_11_
  56.4 1.0 %collective-permute-start.6 = (f32[192,128]{1,0:T(8,128)S(1)}, f32[192,128]{1,0:T(8,128)S(1)}, u32[]{:S(2)}, u32[]{:S(2)}) collective-permute-start(f32[192,128]{1,0:T(8,128)S(1)} %copy-done.12), channel_id=1, source_target_pairs={{0,1},{1,0},{2,3},{3,2},{4,5},{5,4},{6,7},{7,6},{8,9},{9,8},{10,11... | collective-permute-start | bytes 294920 | tf_op jit(solution)/shard_map/ppermute | solution.py:249
  57.4 8.8 %collective-permute-done.15.refs_6_ = f32[512,128]{1,0:T(8,128)S(1)} collective-permute-done((f32[512,128]{1,0:T(8,128)S(1)}, f32[512,128]{1,0:T(8,128)S(1)}, u32[]{:S(2)}, u32[]{:S(2)}) %collective-permute-start.15) | collective-permute-done | bytes 262176 | tf_op jit(solution)/shard_map/ppermute | solution.py:287
  66.2 1.4 %collective-permute-start.7 = (f32[192,128]{1,0:T(8,128)S(1)}, f32[192,128]{1,0:T(8,128)S(1)}, u32[]{:S(2)}, u32[]{:S(2)}) collective-permute-start(f32[192,128]{1,0:T(8,128)S(1)} %copy-done.11), channel_id=1, source_target_pairs={{0,2},{1,3},{2,0},{3,1},{4,6},{5,7},{6,4},{7,5},{8,10},{9,11},{10,... | collective-permute-start | bytes 294920 | tf_op jit(solution)/shard_map/ppermute | solution.py:249
  67.6 0.0 collective-permute-done.16.refs_7_
  67.6 0.0 collective-permute-start.8
  67.6 0.7 weights.1.refs_1_
  68.3 0.0 copy-done.3
  68.3 0.0 copy-done.6
  68.3 0.0 copy-start.4
  68.3 3.5 %defect.3 = (f32[4096,128]{1,0:T(8,128)S(1)}, f32[16,128]{1,0:T(8,128)S(1)}) custom-call(s32[64]{0:T(128)S(1)} %copy-done.6, f32[7,8,72,128]{3,2,1,0:T(8,128)S(1)} %weights.1.refs_1_, f32[512,128]{1,0:T(8,128)S(1)} %copy-done.2, f32[512,128]{1,0:T(8,128)S(1)} %collective-permute-done.12.refs_3_, f32[512,128]{1,0:T(8,128)S(1)} %collective-permute-done.13.refs_4_, ...), custom_call_target="tpu_custom_call" | custom-call | flops 10485760 | bytes 4194304 | tf_op jit(solution)/shard_map/defect/pallas_call | solution.py:308
  71.8 0.0 collective-permute-done.4.refs_6_
  71.8 0.0 collective-permute-done.5.refs_7_
  71.9 2.4 %defect.4 = (f32[2560,128]{1,0:T(8,128)S(1)}, f32[16,128]{1,0:T(8,128)S(1)}) custom-call(s32[64]{0:T(128)S(1)} %copy-done.6, f32[7,8,72,128]{3,2,1,0:T(8,128)S(1)} %weights.1.refs_1_, f32[512,128]{1,0:T(8,128)S(1)} %copy-done, f32[512,128]{1,0:T(8,128)S(1)} %collective-permute-done.1.refs_3_, f32[512,128]{1,0:T(8,128)S(1)} %collective-permute-done.2.refs_4_, ...), custom_call_target="tpu_custom_call" | custom-call | flops 6553600 | bytes 2621440 | tf_op jit(solution)/shard_map/defect/pallas_call | solution.py:308
  74.3 0.0 collective-permute-done.6.refs_9_
  74.3 0.0 collective-permute-done.7.refs_10_
  74.3 0.0 collective-permute-done.8.refs_11_
  74.3 1.7 %defect.5 = (f32[1536,128]{1,0:T(8,128)S(1)}, f32[128,128]{1,0:T(8,128)S(1)}) custom-call(s32[64]{0:T(128)S(1)} %copy-done.6, f32[7,8,72,128]{3,2,1,0:T(8,128)S(1)} %weights.1.refs_1_, f32[512,128]{1,0:T(8,128)S(1)} %copy-done, f32[512,128]{1,0:T(8,128)S(1)} %collective-permute-done.1.refs_3_, f32[512,128]{1,0:T(8,128)S(1)} %collective-permute-done.2.refs_4_, ...), custom_call_target="tpu_custom_call" | custom-call | flops 3932160 | bytes 1572864 | tf_op jit(solution)/shard_map/defect/pallas_call | solution.py:308
  76.0 13.0 %all_to_all.11 = f32[8,16,128]{2,1,0:T(8,128)S(1)} all-to-all(f32[8,16,128]{2,1,0:T(8,128)S(1)} %bitcast.21), channel_id=1, replica_groups=mesh['vtx'=8,'src'=4] {'vtx'}, dimensions={0} | all-to-all | bytes 131072 | tf_op jit(solution)/shard_map/all_to_all | solution.py:324
  89.0 2.3 %scale.1 = (f32[8192,128]{1,0:T(8,128)}, f32[1,16]{1,0:T(1,128)}) custom-call(f32[128,128]{1,0:T(8,128)S(1)} %bitcast.20, f32[4096,128]{1,0:T(8,128)S(1)} %get-tuple-element.53.refs_1_, f32[2560,128]{1,0:T(8,128)S(1)} %get-tuple-element.54.refs_2_, f32[1536,128]{1,0:T(8,128)S(1)} %get-tuple-element.55.refs_3_), custom_call_target="tpu_custom_call" | custom-call | flops 1048576 | bytes 8388608 | tf_op jit(solution)/shard_map/scale/pallas_call | solution.py:325
  (14 shorter events, 0.0 us)
Async XLA Ops:
  4.6 7.1 %copy-start.1 = (f32[4,8,8192]{2,1,0:T(8,128)S(1)}, f32[4,8,8192]{2,1,0:T(8,128)}, u32[]{:S(2)}) copy-start(f32[4,8,8192]{2,1,0:T(8,128)} %param.4) | copy-start | bytes 3145732
  4.6 23.2 %collective-permute-start.12 = (f32[512,128]{1,0:T(8,128)}, f32[512,128]{1,0:T(8,128)S(1)}, u32[]{:S(2)}, u32[]{:S(2)}) collective-permute-start(f32[512,128]{1,0:T(8,128)} %get-tuple-element.43), channel_id=1, source_target_pairs={{0,1},{1,0},{2,3},{3,2},{4,5},{5,4},{6,7},{7,6},{8,9},{9,8},{10,11... | collective-permute-start | bytes 786440 | tf_op jit(solution)/shard_map/ppermute | solution.py:249
  7.2 20.6 %collective-permute-start.13 = (f32[512,128]{1,0:T(8,128)}, f32[512,128]{1,0:T(8,128)S(1)}, u32[]{:S(2)}, u32[]{:S(2)}) collective-permute-start(f32[512,128]{1,0:T(8,128)} %get-tuple-element.44), channel_id=1, source_target_pairs={{0,2},{1,3},{2,0},{3,1},{4,6},{5,7},{6,4},{7,5},{8,10},{9,11},{10,... | collective-permute-start | bytes 786440 | tf_op jit(solution)/shard_map/ppermute | solution.py:249
  9.9 19.7 %collective-permute-start.14 = (f32[512,128]{1,0:T(8,128)}, f32[512,128]{1,0:T(8,128)S(1)}, u32[]{:S(2)}, u32[]{:S(2)}) collective-permute-start(f32[512,128]{1,0:T(8,128)} %get-tuple-element.45), channel_id=1, source_target_pairs={{0,3},{1,2},{2,1},{3,0},{4,7},{5,6},{6,5},{7,4},{8,11},{9,10},{10,... | collective-permute-start | bytes 786440 | tf_op jit(solution)/shard_map/ppermute | solution.py:249
  10.0 16.1 %collective-permute-start.10 = (f32[320,128]{1,0:T(8,128)}, f32[320,128]{1,0:T(8,128)S(1)}, u32[]{:S(2)}, u32[]{:S(2)}) collective-permute-start(f32[320,128]{1,0:T(8,128)} %get-tuple-element.40), channel_id=1, source_target_pairs={{0,2},{1,3},{2,0},{3,1},{4,6},{5,7},{6,4},{7,5},{8,10},{9,11},{10,... | collective-permute-start | bytes 491528 | tf_op jit(solution)/shard_map/ppermute | solution.py:249
  11.7 17.9 %copy-start.2 = (f32[512,128]{1,0:T(8,128)S(1)}, f32[512,128]{1,0:T(8,128)}, u32[]{:S(2)}) copy-start(f32[512,128]{1,0:T(8,128)} %get-tuple-element.42.refs_2_) | copy-start | bytes 786436
  11.7 30.9 %copy-start.9 = (f32[512,128]{1,0:T(8,128)S(1)}, f32[512,128]{1,0:T(8,128)}, u32[]{:S(2)}) copy-start(f32[512,128]{1,0:T(8,128)} %get-tuple-element.47) | copy-start | bytes 786436
  11.8 31.6 %copy-start.8 = (f32[512,128]{1,0:T(8,128)S(1)}, f32[512,128]{1,0:T(8,128)}, u32[]{:S(2)}) copy-start(f32[512,128]{1,0:T(8,128)} %get-tuple-element.48) | copy-start | bytes 786436
  11.8 33.1 %copy-start.7 = (f32[512,128]{1,0:T(8,128)S(1)}, f32[512,128]{1,0:T(8,128)}, u32[]{:S(2)}) copy-start(f32[512,128]{1,0:T(8,128)} %get-tuple-element.49) | copy-start | bytes 786436
  11.8 37.8 %copy-start = (f32[512,128]{1,0:T(8,128)S(1)}, f32[512,128]{1,0:T(8,128)}, u32[]{:S(2)}) copy-start(f32[512,128]{1,0:T(8,128)} %get-tuple-element.30.refs_2_) | copy-start | bytes 786436
  11.8 5.6 %collective-permute-start = (f32[128,128]{1,0:T(8,128)S(1)}, f32[128,128]{1,0:T(8,128)S(1)}, u32[]{:S(2)}, u32[]{:S(2)}) collective-permute-start(f32[128,128]{1,0:T(8,128)S(1)} %bitcast.25), channel_id=1, source_target_pairs={{0,4},{4,8},{8,12},{12,16},{16,20},{20,24},{24,28},{1,5},{5,9},{9,... | collective-permute-start | bytes 196616 | tf_op jit(solution)/shard_map/ppermute | solution.py:271
  17.4 50.2 %copy-start.10 = (f32[192,128]{1,0:T(8,128)S(1)}, f32[192,128]{1,0:T(8,128)}, u32[]{:S(2)}) copy-start(f32[192,128]{1,0:T(8,128)} %get-tuple-element.37) | copy-start | bytes 294916
  17.4 39.0 %copy-start.12 = (f32[192,128]{1,0:T(8,128)S(1)}, f32[192,128]{1,0:T(8,128)}, u32[]{:S(2)}) copy-start(f32[192,128]{1,0:T(8,128)} %get-tuple-element.35) | copy-start | bytes 294916
  17.4 48.7 %copy-start.11 = (f32[192,128]{1,0:T(8,128)S(1)}, f32[192,128]{1,0:T(8,128)}, u32[]{:S(2)}) copy-start(f32[192,128]{1,0:T(8,128)} %get-tuple-element.36) | copy-start | bytes 294916
  17.4 27.4 %collective-permute-start.1 = (f32[512,128]{1,0:T(8,128)}, f32[512,128]{1,0:T(8,128)S(1)}, u32[]{:S(2)}, u32[]{:S(2)}) collective-permute-start(f32[512,128]{1,0:T(8,128)} %get-tuple-element.31), channel_id=1, source_target_pairs={{0,1},{1,0},{2,3},{3,2},{4,5},{5,4},{6,7},{7,6},{8,9},{9,8},{10,11... | collective-permute-start | bytes 786440 | tf_op jit(solution)/shard_map/ppermute | solution.py:249
  26.1 18.7 %collective-permute-start.2 = (f32[512,128]{1,0:T(8,128)}, f32[512,128]{1,0:T(8,128)S(1)}, u32[]{:S(2)}, u32[]{:S(2)}) collective-permute-start(f32[512,128]{1,0:T(8,128)} %get-tuple-element.32), channel_id=1, source_target_pairs={{0,2},{1,3},{2,0},{3,1},{4,6},{5,7},{6,4},{7,5},{8,10},{9,11},{10,... | collective-permute-start | bytes 786440 | tf_op jit(solution)/shard_map/ppermute | solution.py:249
  27.9 20.4 %collective-permute-start.3 = (f32[512,128]{1,0:T(8,128)}, f32[512,128]{1,0:T(8,128)S(1)}, u32[]{:S(2)}, u32[]{:S(2)}) collective-permute-start(f32[512,128]{1,0:T(8,128)} %get-tuple-element.33), channel_id=1, source_target_pairs={{0,3},{1,2},{2,1},{3,0},{4,7},{5,6},{6,5},{7,4},{8,11},{9,10},{10,... | collective-permute-start | bytes 786440 | tf_op jit(solution)/shard_map/ppermute | solution.py:249
  27.9 14.7 %collective-permute-start.11 = (f32[320,128]{1,0:T(8,128)}, f32[320,128]{1,0:T(8,128)S(1)}, u32[]{:S(2)}, u32[]{:S(2)}) collective-permute-start(f32[320,128]{1,0:T(8,128)} %get-tuple-element.41), channel_id=1, source_target_pairs={{0,3},{1,2},{2,1},{3,0},{4,7},{5,6},{6,5},{7,4},{8,11},{9,10},{10,... | collective-permute-start | bytes 491528 | tf_op jit(solution)/shard_map/ppermute | solution.py:249
  29.6 13.7 %collective-permute-start.9 = (f32[320,128]{1,0:T(8,128)}, f32[320,128]{1,0:T(8,128)S(1)}, u32[]{:S(2)}, u32[]{:S(2)}) collective-permute-start(f32[320,128]{1,0:T(8,128)} %get-tuple-element.39), channel_id=1, source_target_pairs={{0,1},{1,0},{2,3},{3,2},{4,5},{5,4},{6,7},{7,6},{8,9},{9,8},{10,11... | collective-permute-start | bytes 491528 | tf_op jit(solution)/shard_map/ppermute | solution.py:249
  42.6 7.1 %collective-permute-start.17 = (f32[512,128]{1,0:T(8,128)S(1)}, f32[512,128]{1,0:T(8,128)S(1)}, u32[]{:S(2)}, u32[]{:S(2)}) collective-permute-start(f32[512,128]{1,0:T(8,128)S(1)} %copy-done.9), channel_id=1, source_target_pairs={{0,1},{1,0},{2,3},{3,2},{4,5},{5,4},{6,7},{7,6},{8,9},{9,8},{10,11... | collective-permute-start | bytes 786440 | tf_op jit(solution)/shard_map/ppermute | solution.py:249
  43.3 10.9 %collective-permute-start.18 = (f32[512,128]{1,0:T(8,128)S(1)}, f32[512,128]{1,0:T(8,128)S(1)}, u32[]{:S(2)}, u32[]{:S(2)}) collective-permute-start(f32[512,128]{1,0:T(8,128)S(1)} %copy-done.8), channel_id=1, source_target_pairs={{0,2},{1,3},{2,0},{3,1},{4,6},{5,7},{6,4},{7,5},{8,10},{9,11},{10,... | collective-permute-start | bytes 786440 | tf_op jit(solution)/shard_map/ppermute | solution.py:249
  44.8 11.5 %collective-permute-start.19 = (f32[512,128]{1,0:T(8,128)S(1)}, f32[512,128]{1,0:T(8,128)S(1)}, u32[]{:S(2)}, u32[]{:S(2)}) collective-permute-start(f32[512,128]{1,0:T(8,128)S(1)} %copy-done.7), channel_id=1, source_target_pairs={{0,3},{1,2},{2,1},{3,0},{4,7},{5,6},{6,5},{7,4},{8,11},{9,10},{10,... | collective-permute-start | bytes 786440 | tf_op jit(solution)/shard_map/ppermute | solution.py:249
  44.8 21.3 %collective-permute-start.15 = (f32[512,128]{1,0:T(8,128)S(1)}, f32[512,128]{1,0:T(8,128)S(1)}, u32[]{:S(2)}, u32[]{:S(2)}) collective-permute-start(f32[512,128]{1,0:T(8,128)S(1)} %get-tuple-element.59), channel_id=1, source_target_pairs={{0,4},{4,8},{8,12},{12,16},{16,20},{20,24},{24,28},{1,5},{5,9},{9,... | collective-permute-start | bytes 786440 | tf_op jit(solution)/shard_map/ppermute | solution.py:287
  48.3 19.3 %collective-permute-start.16 = (f32[512,128]{1,0:T(8,128)S(1)}, f32[512,128]{1,0:T(8,128)S(1)}, u32[]{:S(2)}, u32[]{:S(2)}) collective-permute-start(f32[512,128]{1,0:T(8,128)S(1)} %get-tuple-element.58), channel_id=1, source_target_pairs={{4,0},{8,4},{12,8},{16,12},{20,16},{24,20},{28,24},{5,1},{9,5},{13... | collective-permute-start | bytes 786440 | tf_op jit(solution)/shard_map/ppermute | solution.py:286
  49.6 18.7 %copy-start.3 = (f32[512,128]{1,0:T(8,128)S(1)}, f32[512,128]{1,0:T(8,128)}, u32[]{:S(2)}) copy-start(f32[512,128]{1,0:T(8,128)} %get-tuple-element.46.refs_8_) | copy-start | bytes 786436
  49.6 18.7 %copy-start.6 = (s32[64]{0:T(128)S(1)}, s32[64]{0:T(128)}, u32[]{:S(2)}) copy-start(s32[64]{0:T(128)} %refs_0_.5) | copy-start | bytes 772
  49.7 22.2 %collective-permute-start.4 = (f32[512,128]{1,0:T(8,128)S(1)}, f32[512,128]{1,0:T(8,128)S(1)}, u32[]{:S(2)}, u32[]{:S(2)}) collective-permute-start(f32[512,128]{1,0:T(8,128)S(1)} %get-tuple-element.61), channel_id=1, source_target_pairs={{0,4},{4,8},{8,12},{12,16},{16,20},{20,24},{24,28},{1,5},{5,9},{9,... | collective-permute-start | bytes 786440 | tf_op jit(solution)/shard_map/ppermute | solution.py:287
  54.3 17.6 %collective-permute-start.5 = (f32[512,128]{1,0:T(8,128)S(1)}, f32[512,128]{1,0:T(8,128)S(1)}, u32[]{:S(2)}, u32[]{:S(2)}) collective-permute-start(f32[512,128]{1,0:T(8,128)S(1)} %get-tuple-element.60), channel_id=1, source_target_pairs={{4,0},{8,4},{12,8},{16,12},{20,16},{24,20},{28,24},{5,1},{9,5},{13... | collective-permute-start | bytes 786440 | tf_op jit(solution)/shard_map/ppermute | solution.py:286
  56.4 17.9 %collective-permute-start.6 = (f32[192,128]{1,0:T(8,128)S(1)}, f32[192,128]{1,0:T(8,128)S(1)}, u32[]{:S(2)}, u32[]{:S(2)}) collective-permute-start(f32[192,128]{1,0:T(8,128)S(1)} %copy-done.12), channel_id=1, source_target_pairs={{0,1},{1,0},{2,3},{3,2},{4,5},{5,4},{6,7},{7,6},{8,9},{9,8},{10,11... | collective-permute-start | bytes 294920 | tf_op jit(solution)/shard_map/ppermute | solution.py:249
  66.2 8.1 %collective-permute-start.7 = (f32[192,128]{1,0:T(8,128)S(1)}, f32[192,128]{1,0:T(8,128)S(1)}, u32[]{:S(2)}, u32[]{:S(2)}) collective-permute-start(f32[192,128]{1,0:T(8,128)S(1)} %copy-done.11), channel_id=1, source_target_pairs={{0,2},{1,3},{2,0},{3,1},{4,6},{5,7},{6,4},{7,5},{8,10},{9,11},{10,... | collective-permute-start | bytes 294920 | tf_op jit(solution)/shard_map/ppermute | solution.py:249
  67.6 6.7 %collective-permute-start.8 = (f32[192,128]{1,0:T(8,128)S(1)}, f32[192,128]{1,0:T(8,128)S(1)}, u32[]{:S(2)}, u32[]{:S(2)}) collective-permute-start(f32[192,128]{1,0:T(8,128)S(1)} %copy-done.10), channel_id=1, source_target_pairs={{0,3},{1,2},{2,1},{3,0},{4,7},{5,6},{6,5},{7,4},{8,11},{9,10},{10,... | collective-permute-start | bytes 294920 | tf_op jit(solution)/shard_map/ppermute | solution.py:249
  68.3 3.5 %copy-start.4 = (f32[320,128]{1,0:T(8,128)S(1)}, f32[320,128]{1,0:T(8,128)}, u32[]{:S(2)}) copy-start(f32[320,128]{1,0:T(8,128)} %get-tuple-element.38.refs_8_) | copy-start | bytes 491524
  71.9 2.4 %copy-start.5 = (f32[192,128]{1,0:T(8,128)S(1)}, f32[192,128]{1,0:T(8,128)}, u32[]{:S(2)}) copy-start(f32[192,128]{1,0:T(8,128)} %get-tuple-element.34.refs_8_) | copy-start | bytes 294916

commit v5 on v4

--- a/solution.py
+++ b/solution.py
@@ -71,9 +71,13 @@
     )(heat)
 
 
-def weights_kernel(meta, cotan, lower, out):
+def weights_kernel(meta, sources, cotan, lower, out, spots):
     rows_dev, cb, total_rows = meta
     block_start = lax.axis_index("vtx") * rows_dev
+    group = spots.shape[0]
+    first = lax.axis_index("src") * group
+    for i in range(group):
+        spots[pl.ds(i, 1), :] = jnp.full((1, LANES), sources[first + i] - block_start * cb * LANES, jnp.int32)
     lane = lax.broadcasted_iota(jnp.int32, (SUB, LANES), 1)
     index = lax.broadcasted_iota(jnp.int32, (SUB, LANES), 0) * LANES + lane
     last_lane = lane == LANES - 1
@@ -114,10 +118,12 @@
 def defect_kernel(meta, lo, n, group, amplitude, *refs):
     pieces, rows_dev, cb, senders, own_rows = meta
     n_in = len(pieces)
-    sources, weights = refs[:2]
+    spots, weights = refs[:2]
     ins = refs[2 : 2 + n_in]
     prev = refs[2 + n_in] if lo else None
-    out, sums, grid = refs[-3:]
+    last = lo + n == group
+    out, sums, grid = refs[-4:-1] if last else refs[-3:]
+    total_of = refs[-1] if last else sums
     me = lax.axis_index("src")
     for ref, (kind, k, first, count, skip) in zip(ins, pieces, strict=True):
         t = me ^ k
@@ -142,18 +148,14 @@
     for row in range(rows_dev + 2):
         grid[row, pl.ds(0, PAD), :] = zero
         grid[row, pl.ds(PAD + n * cb, PAD), :] = zero
-    if lo:
-        sums[pl.ds(0, group), :] = prev[...]
-    else:
-        sums[...] = jnp.zeros(sums.shape, jnp.float32)
+    total_of[...] = prev[...] if lo else jnp.zeros((group, LANES), jnp.float32)
     lane = lax.broadcasted_iota(jnp.int32, (SUB, LANES), 1)
     index = lax.broadcasted_iota(jnp.int32, (SUB, LANES), 0) * LANES + lane
     first_lane, last_lane = lane == 0, lane == LANES - 1
     width = cb * LANES
-    start = lax.axis_index("vtx") * rows_dev * width
 
     def source_step(i, _):
-        source = sources[me * group + lo + i] - start
+        spot = jnp.broadcast_to(spots[pl.ds(lo + i, 1), :], (SUB, LANES)) - index
 
         def column_step(q, total):
             base = pl.multiple_of(PAD + i * cb + q * SUB, SUB)
@@ -172,37 +174,36 @@
                 value = c[0] * here[row + 1] - c[1] * right[row + 1] - c[2] * left[row + 1]
                 value = value - c[3] * here[row + 2] - c[4] * here[row]
                 value = value - c[5] * right[row + 2] - c[6] * left[row]
-                spot = source - row * width - q * SUB * LANES
-                value = value - jnp.where(index == spot, amplitude, 0.0)
+                value = value - jnp.where(spot == row * width + q * SUB * LANES, amplitude, 0.0)
                 out[pl.ds((i * cb + q * SUB) * rows_dev + row, SUB, stride=rows_dev), :] = value
                 total = total + value * value
             return total
 
         total = lax.fori_loop(0, cb // SUB, column_step, zero, unroll=math.gcd(cb // SUB, 8))
-        sums[pl.ds(lo + i, 1), :] = jnp.sum(total, axis=0, keepdims=True)
+        total_of[pl.ds(lo + i, 1), :] = jnp.sum(total, axis=0, keepdims=True)
         return 0
 
-    lax.fori_loop(0, n, source_step, 0)
-    for first in range(group, sums.shape[0], group):
-        sums[pl.ds(first, group), :] = sums[pl.ds(0, group), :]
+    lax.fori_loop(0, n, source_step, 0, unroll=math.gcd(n, 2))
+    if last:
+        whole = jnp.sum(total_of[...], axis=1, keepdims=True)
+        lane = lax.broadcasted_iota(jnp.int32, (group, LANES), 1)
+        diagonal = lane == lax.broadcasted_iota(jnp.int32, (group, LANES), 0)
+        row = jnp.sum(jnp.where(diagonal, whole, 0.0), axis=0, keepdims=True)
+        sums[...] = jnp.broadcast_to(row, sums.shape)
 
 
 def scale_kernel(chunks, size, *refs):
     total, parts, out, norms, buf, spread, out_sem = refs[0], refs[1:-5], *refs[-5:]
     group = sum(n for _, n in chunks)
     per = out.shape[0] // group
-    sums = total[pl.ds(0, group), :]
-    for first in range(group, total.shape[0], group):
-        sums = sums + total[pl.ds(first, group), :]
-    sums = jnp.sum(sums, axis=1, keepdims=True)
-    norm = jnp.sqrt(sums / size + 1e-06)
-    lane = lax.broadcasted_iota(jnp.int32, (group, LANES), 1)
-    sub = lax.broadcasted_iota(jnp.int32, (group, LANES), 0)
-    diagonal = jnp.where(lane == sub, jnp.broadcast_to(norm, (group, LANES)), 0.0)
-    spread[...] = jnp.sum(diagonal, axis=0, keepdims=True)[:, :group]
+    norm = jnp.sqrt(jnp.sum(total[...], axis=0, keepdims=True) / size + 1e-06)
+    spread[...] = norm[:, :group]
     norms_copy = pltpu.make_async_copy(spread, norms, out_sem.at[group])
     norms_copy.start()
-    buf[pl.ds(group * per, group), :] = jnp.broadcast_to(1.0 / norm, (group, LANES))
+    lane = lax.broadcasted_iota(jnp.int32, (group, LANES), 1)
+    diagonal = lane == lax.broadcasted_iota(jnp.int32, (group, LANES), 0)
+    inverse = jnp.sum(jnp.where(diagonal, 1.0 / norm, 0.0), axis=1, keepdims=True)
+    buf[pl.ds(group * per, group), :] = jnp.broadcast_to(inverse, (group, LANES))
 
     def copy_of(i):
         spot = pl.ds(pl.multiple_of(i * per, per), per)
@@ -241,7 +242,7 @@
     outer_rows = (0, own_rows - 1)
     order = [k for k in range(1, senders) if k >= 2] + [1]
     halves = [(0, group // 2), (group // 2, group - group // 2)]
-    cuts = (0, group // 2, group - group * 3 // 16, group)
+    cuts = (0, group // 2, group - group // 4, group - group // 8, group)
     chunks = [(lo, hi - lo) for lo, hi in zip(cuts[:-1], cuts[1:], strict=True) if hi > lo]
     common = (group, cb, own_rows, senders)
 
@@ -251,10 +252,10 @@
     wanted = [(k, outer_rows, *half) for half in halves for k in (1, 0)]
     wanted += [(k, (1 + j, j), *chunk) for chunk in chunks for j in range(own_rows - 1) for k in order + [0]]
     table = {}
-    for half in halves:
-        early = [(k, outer_rows, *half) for k in order[:-1]]
-        packed = pack(view, early, [(k, *half) for k in order[:-1]], *common, 60)
-        table.update(zip(early, packed, strict=True))
+    early = [(k, outer_rows, *half) for half in halves for k in order[:-1]]
+    for part in (early[:1], early[1:]):
+        packed = pack(view, part, [(k, *at) for k, _, *at in part], *common, 60)
+        table.update(zip(part, packed, strict=True))
     packed = pack(view, wanted, [(k, *half) for half in halves for k in order + [0]], *common, 60)
     table.update(zip(wanted, packed, strict=True))
     for key, piece in table.items():
@@ -266,19 +267,21 @@
     up = [(i, i + 1) for i in range(peers - 1)]
     down = [(j, i) for i, j in up]
     vmem = pl.BlockSpec(memory_space=pltpu.VMEM)
-    smem = pl.BlockSpec(memory_space=pltpu.SMEM)
     per = cb * rows_dev
     lower = lax.ppermute(cotan[2:4, rows_dev - 1].reshape(2 * cb, LANES), "vtx", up)
     tiles = cotan.reshape(4, rows_dev, cb, LANES).transpose(0, 2, 1, 3).reshape(4 * per, LANES)
-    weights = pl.pallas_call(
+    weights, spots = pl.pallas_call(
         functools.partial(weights_kernel, (rows_dev, cb, total_rows)),
-        out_shape=jax.ShapeDtypeStruct((7, rows_dev, cb + PAD, LANES), jnp.float32),
-        in_specs=[vmem, vmem],
-        out_specs=vmem,
+        out_shape=(
+            jax.ShapeDtypeStruct((7, rows_dev, cb + PAD, LANES), jnp.float32),
+            jax.ShapeDtypeStruct((group, LANES), jnp.int32),
+        ),
+        in_specs=[pl.BlockSpec(memory_space=pltpu.SMEM), vmem, vmem],
+        out_specs=(vmem, vmem),
         compiler_params=pltpu.CompilerParams(vmem_limit_bytes=8 << 20),
         cost_estimate=pl.CostEstimate(flops=20 * per * LANES, bytes_accessed=44 * per * LANES, transcendentals=0),
         name="weights",
-    )(tiles, lower)
+    )(source_index, tiles, lower)
     below, above = [], []
     for got in outer:
         first = lax.select_n(me, *[got[k] for k in range(senders)])
@@ -309,17 +312,18 @@
             functools.partial(defect_kernel, meta, lo, n, group, amplitude),
             out_shape=(
                 jax.ShapeDtypeStruct((n * per, LANES), jnp.float32),
-                jax.ShapeDtypeStruct((group * peers if lo + n == group else group, LANES), jnp.float32),
+                jax.ShapeDtypeStruct((peers if lo + n == group else group, LANES), jnp.float32),
             ),
-            in_specs=[smem, vmem] + [vmem] * len(ins) + ([vmem] if lo else []),
+            in_specs=[vmem, vmem] + [vmem] * len(ins) + ([vmem] if lo else []),
             out_specs=(vmem, vmem),
             scratch_shapes=[
                 pltpu.VMEM((rows_dev + 2, n * cb + PAD + TAIL, LANES), jnp.float32),
-            ],
+            ]
+            + ([pltpu.VMEM((group, LANES), jnp.float32)] if lo + n == group else []),
             cost_estimate=pl.CostEstimate(flops=20 * n * per * LANES, bytes_accessed=8 * n * per * LANES, transcendentals=0),
             compiler_params=pltpu.CompilerParams(vmem_limit_bytes=24 << 20),
             name="defect",
-        )(source_index, weights, *ins, *([sums] if lo else []))
+        )(spots, weights, *ins, *([sums] if lo else []))
         parts.append(part)
     sums = lax.all_to_all(sums, "vtx", 0, 0, tiled=True)
     out, norms = pl.pallas_call(

time: 91.6 us -> 87.4 us (0.954)
  waiting for transfers between devices: 31.1 us -> 24.5 us
  starting transfers between devices: 27.2 us -> 30.3 us
  Pallas kernels: 18.6 us -> 16.5 us
  other arithmetic: 0.12 us -> 2.07 us
    ppermute x15 -> x18, waiting for transfers between devices: 22.4 us -> 11.8 us  [send(): lax.ppermute(piece, 'src', [(i, i ^ k) for i in range(senders)])]
    pallas_call x3 -> x4, Pallas kernels: 7.58 us -> 4.84 us  [program(): pl.pallas_call(functools.partial(defect_kernel, meta, lo, n, group, ampli...]
    ppermute x2, waiting for transfers between devices: 8.78 us -> 10.9 us  [program(): below.append(lax.ppermute(last, 'vtx', up))]
    ppermute x2, starting transfers between devices: 7.97 us -> 10.1 us  [program(): below.append(lax.ppermute(last, 'vtx', up))]
    select_n x2, other arithmetic: 0.12 us -> 2.07 us  [program(): first = lax.select_n(me, *[got[k] for k in range(senders)])]
    ppermute x1, waiting for transfers between devices: 0.01 us -> 1.8 us  [program(): lax.ppermute(cotan[2:4, rows_dev - 1].reshape(2 * cb, LANES), 'vtx', up)]
    ppermute x15 -> x18, starting transfers between devices: 13.2 us -> 13.9 us  [send(): lax.ppermute(piece, 'src', [(i, i ^ k) for i in range(senders)])]
  transfers between devices with their start and end apart: 20 -> 23, of which waited for: 4 -> 4; matrix products, arithmetic and copies ran while one was open for 0% -> 2% of each run, Pallas kernels for 12% -> 14%
where the time goes in v5:
time: 87.4 us; the launch traced here: 87 us
  starting transfers between devices  30.3 us (35%)
  waiting for transfers between devices  24.5 us (28%)
  Pallas kernels  16.5 us (19%)
  blocking collectives  12.5 us (14%)
  other arithmetic  2.07 us (2%)
  between operations  0.97 us (1%)
    ppermute x18, starting transfers between devices, send(): lax.ppermute(piece, 'src', [(i, i ^ k) for i in range(senders)])  13.9 us
    all_to_all x1, blocking collectives, program(): sums = lax.all_to_all(sums, 'vtx', 0, 0, tiled=True)  12.5 us
    ppermute x18, waiting for transfers between devices, send(): lax.ppermute(piece, 'src', [(i, i ^ k) for i in range(senders)])  11.8 us
    ppermute x2, waiting for transfers between devices, program(): below.append(lax.ppermute(last, 'vtx', up))  10.9 us
    ppermute x2, starting transfers between devices, program(): below.append(lax.ppermute(last, 'vtx', up))  10.1 us
    pallas_call x3, Pallas kernels, pack(): pl.pallas_call(functools.partial(pack_kernel, (tuple(plan), group, cb, ow...  8.13 us
    pallas_call x4, Pallas kernels, program(): pl.pallas_call(functools.partial(defect_kernel, meta, lo, n, group, ampli...  4.84 us
    ppermute x1, starting transfers between devices, program(): lax.ppermute(cotan[2:4, rows_dev - 1].reshape(2 * cb, LANES), 'vtx', up)  3.81 us
  transfers between devices with their start and end apart: 23, of which 4 were waited for; matrix products, arithmetic and copies ran while one was open for 2% of the time, Pallas kernels for 14%

profile of v5, /device:TPU:0, one launch (start us, length us, event | category | flops | bytes accessed | tf_op | source)
XLA Modules:
  0.0 87.0 jit_solution(518010422768902343)
XLA Ops:
  0.6 1.8 %shard_map.52 = f32[512,128]{1,0:T(8,128)} custom-call(f32[8192,128]{1,0:T(8,128)} %bitcast.24), custom_call_target="tpu_custom_call" | custom-call | flops 65536 | bytes 786432 | tf_op jit(solution)/shard_map/pallas_call | solution.py:60
  2.4 0.0 copy-start.1
  2.4 3.1 %collective-permute-start.16 = (f32[512,128]{1,0:T(8,128)}, f32[512,128]{1,0:T(8,128)S(1)}, u32[]{:S(2)}, u32[]{:S(2)}) collective-permute-start(f32[512,128]{1,0:T(8,128)} %shard_map.52), channel_id=1, source_target_pairs={{0,2},{1,3},{2,0},{3,1},{4,6},{5,7},{6,4},{7,5},{8,10},{9,11},{10,... | collective-permute-start | bytes 786440 | tf_op jit(solution)/shard_map/ppermute | solution.py:250
  5.5 2.3 %shard_map.51 = (f32[512,128]{1,0:T(8,128)}, f32[512,128]{1,0:T(8,128)}, f32[512,128]{1,0:T(8,128)}) custom-call(f32[8192,128]{1,0:T(8,128)} %bitcast.25), custom_call_target="tpu_custom_call" | custom-call | flops 196608 | bytes 2359296 | tf_op jit(solution)/shard_map/pallas_call | solution.py:60
  7.8 0.0 copy-start.7
  7.9 0.1 collective-permute-start.17
  7.9 4.0 %shard_map.50 = (f32[512,128]{1,0:T(8,128)}, f32[512,128]{1,0:T(8,128)}, f32[512,128]{1,0:T(8,128)}, f32[512,128]{1,0:T(8,128)}, f32[512,128]{1,0:T(8,128)}, /*i...) custom-call(f32[8192,128]{1,0:T(8,128)} %bitcast.26), custom_call_target="tpu_custom_call" | custom-call | flops 786432 | bytes 7340032 | tf_op jit(solution)/shard_map/pallas_call | solution.py:60
  12.0 0.2 collective-permute-start.15
  12.2 0.1 slice.3
  12.3 3.8 %collective-permute-start = (f32[128,128]{1,0:T(8,128)S(1)}, f32[128,128]{1,0:T(8,128)S(1)}, u32[]{:S(2)}, u32[]{:S(2)}) collective-permute-start(f32[128,128]{1,0:T(8,128)S(1)} %bitcast.27), channel_id=1, source_target_pairs={{0,4},{4,8},{8,12},{12,16},{16,20},{20,24},{24,28},{1,5},{5,9},{9,... | collective-permute-start | bytes 196616 | tf_op jit(solution)/shard_map/ppermute | solution.py:271
  16.1 0.1 collective-permute-start.9
  16.2 1.8 %collective-permute-done.lower = f32[128,128]{1,0:T(8,128)S(1)} collective-permute-done((f32[128,128]{1,0:T(8,128)S(1)}, f32[128,128]{1,0:T(8,128)S(1)}, u32[]{:S(2)}, u32[]{:S(2)}) %collective-permute-start) | collective-permute-done | bytes 65568 | tf_op jit(solution)/shard_map/ppermute | solution.py:271
  18.0 1.5 %collective-permute-start.2 = (f32[512,128]{1,0:T(8,128)S(1)}, f32[512,128]{1,0:T(8,128)S(1)}, u32[]{:S(2)}, u32[]{:S(2)}) collective-permute-start(f32[512,128]{1,0:T(8,128)S(1)} %copy-done.9), channel_id=1, source_target_pairs={{0,2},{1,3},{2,0},{3,1},{4,6},{5,7},{6,4},{7,5},{8,10},{9,11},{10,... | collective-permute-start | bytes 786440 | tf_op jit(solution)/shard_map/ppermute | solution.py:250
  19.5 0.0 collective-permute-done.9.refs_9_
  19.5 0.0 collective-permute-start.3
  19.5 0.0 collective-permute-done.16.refs_4_
  19.5 0.6 collective-permute-start.12
  20.1 0.0 collective-permute-done.17.refs_5_
  20.1 1.5 %collective-permute-start.13 = (f32[256,128]{1,0:T(8,128)}, f32[256,128]{1,0:T(8,128)S(1)}, u32[]{:S(2)}, u32[]{:S(2)}) collective-permute-start(f32[256,128]{1,0:T(8,128)} %get-tuple-element.53), channel_id=1, source_target_pairs={{0,2},{1,3},{2,0},{3,1},{4,6},{5,7},{6,4},{7,5},{8,10},{9,11},{10,... | collective-permute-start | bytes 393224 | tf_op jit(solution)/shard_map/ppermute | solution.py:250
  21.6 0.0 collective-permute-done.15.refs_3_
  21.6 0.0 collective-permute-start.1
  21.7 1.1 %select_select_fusion = (f32[512,128]{1,0:T(8,128)S(1)}, f32[512,128]{1,0:T(8,128)S(1)}) fusion(f32[512,128]{1,0:T(8,128)S(1)} %collective-permute-done.16.refs_4_, f32[512,128]{1,0:T(8,128)S(1)} %collective-permute-done.17.refs_5_, f32[512,128]{1,0:T(8,128)} %get-tuple-element.55.refs_2_, f32[512,128]{1,0:T(8,128)S(1)} %collective-permute-done.15.refs_3_, ...), kind=kLoop, calls=%fused_computation | loop fusion | flops 393216 | bytes 1572867 | tf_op jit(solution)/shard_map/select_n | solution.py:287
  22.7 0.0 collective-permute-done.12.refs_9_
  22.7 0.7 collective-permute-start.14
  23.4 11.8 %collective-permute-done.13.refs_10_ = f32[256,128]{1,0:T(8,128)S(1)} collective-permute-done((f32[256,128]{1,0:T(8,128)}, f32[256,128]{1,0:T(8,128)S(1)}, u32[]{:S(2)}, u32[]{:S(2)}) %collective-permute-start.13) | collective-permute-done | bytes 131104 | tf_op jit(solution)/shard_map/ppermute | solution.py:250
  35.2 0.0 collective-permute-start.20
  35.2 0.0 collective-permute-done.2.refs_4_
  35.2 1.5 %collective-permute-start.21 = (f32[512,128]{1,0:T(8,128)}, f32[512,128]{1,0:T(8,128)S(1)}, u32[]{:S(2)}, u32[]{:S(2)}) collective-permute-start(f32[512,128]{1,0:T(8,128)} %get-tuple-element.60), channel_id=1, source_target_pairs={{0,2},{1,3},{2,0},{3,1},{4,6},{5,7},{6,4},{7,5},{8,10},{9,11},{10,... | collective-permute-start | bytes 786440 | tf_op jit(solution)/shard_map/ppermute | solution.py:250
  36.7 0.0 collective-permute-done.3.refs_5_
  36.7 0.3 collective-permute-start.22
  37.0 0.0 collective-permute-done.1.refs_3_
  37.0 1.3 %collective-permute-start.19 = (f32[512,128]{1,0:T(8,128)S(1)}, f32[512,128]{1,0:T(8,128)S(1)}, u32[]{:S(2)}, u32[]{:S(2)}) collective-permute-start(f32[512,128]{1,0:T(8,128)S(1)} %get-tuple-element.72), channel_id=1, source_target_pairs={{4,0},{8,4},{12,8},{16,12},{20,16},{24,20},{28,24},{5,1},{9,5},{13... | collective-permute-start | bytes 786440 | tf_op jit(solution)/shard_map/ppermute | solution.py:289
  38.3 1.0 %select_select_fusion.2 = (f32[512,128]{1,0:T(8,128)S(1)}, f32[512,128]{1,0:T(8,128)S(1)}) fusion(f32[512,128]{1,0:T(8,128)S(1)} %collective-permute-done.2.refs_4_, f32[512,128]{1,0:T(8,128)S(1)} %collective-permute-done.3.refs_5_, f32[512,128]{1,0:T(8,128)} %get-tuple-element.39.refs_2_, f32[512,128]{1,0:T(8,128)S(1)} %collective-permute-done.1.refs_3_, ...), kind=kLoop, calls=%fused_computation.2 | loop fusion | flops 393216 | bytes 1572867 | tf_op jit(solution)/shard_map/select_n | solution.py:287
  39.3 0.0 collective-permute-done.14.refs_11_
  39.4 4.6 %collective-permute-start.18 = (f32[512,128]{1,0:T(8,128)S(1)}, f32[512,128]{1,0:T(8,128)S(1)}, u32[]{:S(2)}, u32[]{:S(2)}) collective-permute-start(f32[512,128]{1,0:T(8,128)S(1)} %get-tuple-element.73), channel_id=1, source_target_pairs={{0,4},{4,8},{8,12},{12,16},{16,20},{20,24},{24,28},{1,5},{5,9},{9,... | collective-permute-start | bytes 786440 | tf_op jit(solution)/shard_map/ppermute | solution.py:290
  44.0 0.0 collective-permute-done.20.refs_9_
  44.0 1.3 %collective-permute-start.5 = (f32[512,128]{1,0:T(8,128)S(1)}, f32[512,128]{1,0:T(8,128)S(1)}, u32[]{:S(2)}, u32[]{:S(2)}) collective-permute-start(f32[512,128]{1,0:T(8,128)S(1)} %get-tuple-element.74), channel_id=1, source_target_pairs={{4,0},{8,4},{12,8},{16,12},{20,16},{24,20},{28,24},{5,1},{9,5},{13... | collective-permute-start | bytes 786440 | tf_op jit(solution)/shard_map/ppermute | solution.py:289
  45.3 0.0 collective-permute-done.21.refs_10_
  45.3 5.4 %collective-permute-start.4 = (f32[512,128]{1,0:T(8,128)S(1)}, f32[512,128]{1,0:T(8,128)S(1)}, u32[]{:S(2)}, u32[]{:S(2)}) collective-permute-start(f32[512,128]{1,0:T(8,128)S(1)} %get-tuple-element.75), channel_id=1, source_target_pairs={{0,4},{4,8},{8,12},{12,16},{16,20},{20,24},{24,28},{1,5},{5,9},{9,... | collective-permute-start | bytes 786440 | tf_op jit(solution)/shard_map/ppermute | solution.py:290
  50.8 0.0 collective-permute-done.22.refs_11_
  50.8 1.6 %collective-permute-start.10 = (f32[128,128]{1,0:T(8,128)}, f32[128,128]{1,0:T(8,128)S(1)}, u32[]{:S(2)}, u32[]{:S(2)}) collective-permute-start(f32[128,128]{1,0:T(8,128)} %get-tuple-element.49), channel_id=1, source_target_pairs={{0,2},{1,3},{2,0},{3,1},{4,6},{5,7},{6,4},{7,5},{8,10},{9,11},{10,... | collective-permute-start | bytes 196616 | tf_op jit(solution)/shard_map/ppermute | solution.py:250
  52.4 0.0 collective-permute-done.19.refs_7_
  52.4 0.0 collective-permute-start.11
  52.4 6.8 %collective-permute-done.18.refs_6_ = f32[512,128]{1,0:T(8,128)S(1)} collective-permute-done((f32[512,128]{1,0:T(8,128)S(1)}, f32[512,128]{1,0:T(8,128)S(1)}, u32[]{:S(2)}, u32[]{:S(2)}) %collective-permute-start.18) | collective-permute-done | bytes 262176 | tf_op jit(solution)/shard_map/ppermute | solution.py:290
  59.2 0.0 collective-permute-start.6
  59.2 0.0 collective-permute-done.5.refs_7_
  59.2 1.5 %collective-permute-start.7 = (f32[128,128]{1,0:T(8,128)}, f32[128,128]{1,0:T(8,128)S(1)}, u32[]{:S(2)}, u32[]{:S(2)}) collective-permute-start(f32[128,128]{1,0:T(8,128)} %get-tuple-element.45), channel_id=1, source_target_pairs={{0,2},{1,3},{2,0},{3,1},{4,6},{5,7},{6,4},{7,5},{8,10},{9,11},{10,... | collective-permute-start | bytes 196616 | tf_op jit(solution)/shard_map/ppermute | solution.py:250
  60.7 4.0 %collective-permute-done.4.refs_6_ = f32[512,128]{1,0:T(8,128)S(1)} collective-permute-done((f32[512,128]{1,0:T(8,128)S(1)}, f32[512,128]{1,0:T(8,128)S(1)}, u32[]{:S(2)}, u32[]{:S(2)}) %collective-permute-start.4) | collective-permute-done | bytes 262176 | tf_op jit(solution)/shard_map/ppermute | solution.py:290
  64.8 1.2 %collective-permute-start.8 = (f32[128,128]{1,0:T(8,128)}, f32[128,128]{1,0:T(8,128)S(1)}, u32[]{:S(2)}, u32[]{:S(2)}) collective-permute-start(f32[128,128]{1,0:T(8,128)} %get-tuple-element.46), channel_id=1, source_target_pairs={{0,3},{1,2},{2,1},{3,0},{4,7},{5,6},{6,5},{7,4},{8,11},{9,10},{10,... | collective-permute-start | bytes 196616 | tf_op jit(solution)/shard_map/ppermute | solution.py:250
  65.9 1.3 %weights.1 = (f32[7,8,72,128]{3,2,1,0:T(8,128)S(1)}, s32[16,128]{1,0:T(8,128)S(1)}) custom-call(s32[64]{0:T(128)S(1)} %copy-done.7, f32[2048,128]{1,0:T(8,128)S(1)} %bitcast.21, f32[128,128]{1,0:T(8,128)S(1)} %collective-permute-done.lower), custom_call_target="tpu_custom_call" | custom-call | flops 1310720 | bytes 2883584 | tf_op jit(solution)/shard_map/weights/pallas_call | solution.py:273
  67.2 0.0 copy-done.2
  67.2 0.0 copy-done.3
  67.2 0.0 copy-start.6
  67.2 2.4 %defect.4 = (f32[4096,128]{1,0:T(8,128)S(1)}, f32[16,128]{1,0:T(8,128)S(1)}) custom-call(s32[16,128]{1,0:T(8,128)S(1)} %get-tuple-element.37.refs_0_, f32[7,8,72,128]{3,2,1,0:T(8,128)S(1)} %get-tuple-element.38.refs_1_, f32[512,128]{1,0:T(8,128)S(1)} %copy-done.2, f32[512,128]{1,0:T(8,128)S(1)} %collective-permute-done.15.refs_3_, ...), custom_call_target="tpu_custom_call" | custom-call | flops 10485760 | bytes 4194304 | tf_op jit(solution)/shard_map/defect/pallas_call | solution.py:311
  69.6 1.2 %defect.5 = (f32[2048,128]{1,0:T(8,128)S(1)}, f32[16,128]{1,0:T(8,128)S(1)}) custom-call(s32[16,128]{1,0:T(8,128)S(1)} %get-tuple-element.37.refs_0_, f32[7,8,72,128]{3,2,1,0:T(8,128)S(1)} %get-tuple-element.38.refs_1_, f32[512,128]{1,0:T(8,128)S(1)} %copy-done, f32[512,128]{1,0:T(8,128)S(1)} %collective-permute-done.1.refs_3_, ...), custom_call_target="tpu_custom_call" | custom-call | flops 5242880 | bytes 2097152 | tf_op jit(solution)/shard_map/defect/pallas_call | solution.py:311
  70.8 0.0 collective-permute-done.10.refs_10_
  70.8 0.0 collective-permute-done.11.refs_11_
  70.9 0.6 defect.6
  71.5 0.0 collective-permute-done.6.refs_9_
  71.5 0.0 collective-permute-done.7.refs_10_
  71.5 0.0 collective-permute-done.8.refs_11_
  71.5 0.7 defect.7
  72.2 12.5 %all_to_all.11 = f32[8,1,128]{2,1,0:T(1,128)S(1)} all-to-all(f32[8,1,128]{2,1,0:T(1,128)S(1)} %bitcast.23), channel_id=1, replica_groups=mesh['vtx'=8,'src'=4] {'vtx'}, dimensions={0} | all-to-all | bytes 8192 | tf_op jit(solution)/shard_map/all_to_all | solution.py:328
  84.7 2.3 %scale.1 = (f32[8192,128]{1,0:T(8,128)}, f32[1,16]{1,0:T(1,128)}) custom-call(f32[8,128]{1,0:T(8,128)S(1)} %bitcast.22, f32[4096,128]{1,0:T(8,128)S(1)} %get-tuple-element.66.refs_1_, f32[2048,128]{1,0:T(8,128)S(1)} %get-tuple-element.67.refs_2_, f32[1024,128]{1,0:T(8,128)S(1)} %get-tuple-element.68.refs_3_, f32[1024,128]{1,0:T(8,128)S(1)} %get-tuple-element.69.refs_4_), custom_call_target="tpu_custom_call" | custom-call | flops 1048576 | bytes 8388608 | tf_op jit(solution)/shard_map/scale/pallas_call | solution.py:329
  (15 shorter events, 0.0 us)
Async XLA Ops:
  2.4 9.8 %copy-start.1 = (f32[4,8,8192]{2,1,0:T(8,128)S(1)}, f32[4,8,8192]{2,1,0:T(8,128)}, u32[]{:S(2)}) copy-start(f32[4,8,8192]{2,1,0:T(8,128)} %param.4) | copy-start | bytes 3145732
  2.4 17.1 %collective-permute-start.16 = (f32[512,128]{1,0:T(8,128)}, f32[512,128]{1,0:T(8,128)S(1)}, u32[]{:S(2)}, u32[]{:S(2)}) collective-permute-start(f32[512,128]{1,0:T(8,128)} %shard_map.52), channel_id=1, source_target_pairs={{0,2},{1,3},{2,0},{3,1},{4,6},{5,7},{6,4},{7,5},{8,10},{9,11},{10,... | collective-permute-start | bytes 786440 | tf_op jit(solution)/shard_map/ppermute | solution.py:250
  7.8 10.1 %copy-start.9 = (f32[512,128]{1,0:T(8,128)S(1)}, f32[512,128]{1,0:T(8,128)}, u32[]{:S(2)}) copy-start(f32[512,128]{1,0:T(8,128)} %get-tuple-element.41) | copy-start | bytes 786436
  7.8 11.6 %copy-start.8 = (f32[512,128]{1,0:T(8,128)S(1)}, f32[512,128]{1,0:T(8,128)}, u32[]{:S(2)}) copy-start(f32[512,128]{1,0:T(8,128)} %get-tuple-element.42) | copy-start | bytes 786436
  7.8 58.1 %copy-start.7 = (s32[64]{0:T(128)S(1)}, s32[64]{0:T(128)}, u32[]{:S(2)}) copy-start(s32[64]{0:T(128)} %sources.1) | copy-start | bytes 772
  7.9 12.3 %collective-permute-start.17 = (f32[512,128]{1,0:T(8,128)}, f32[512,128]{1,0:T(8,128)S(1)}, u32[]{:S(2)}, u32[]{:S(2)}) collective-permute-start(f32[512,128]{1,0:T(8,128)} %get-tuple-element.57), channel_id=1, source_target_pairs={{0,3},{1,2},{2,1},{3,0},{4,7},{5,6},{6,5},{7,4},{8,11},{9,10},{10,... | collective-permute-start | bytes 786440 | tf_op jit(solution)/shard_map/ppermute | solution.py:250
  12.0 55.3 %copy-start.2 = (f32[512,128]{1,0:T(8,128)S(1)}, f32[512,128]{1,0:T(8,128)}, u32[]{:S(2)}) copy-start(f32[512,128]{1,0:T(8,128)} %get-tuple-element.55.refs_2_) | copy-start | bytes 786436
  12.0 55.3 %copy-start.3 = (f32[512,128]{1,0:T(8,128)S(1)}, f32[512,128]{1,0:T(8,128)}, u32[]{:S(2)}) copy-start(f32[512,128]{1,0:T(8,128)} %get-tuple-element.58.refs_8_) | copy-start | bytes 786436
  12.0 9.7 %collective-permute-start.15 = (f32[512,128]{1,0:T(8,128)}, f32[512,128]{1,0:T(8,128)S(1)}, u32[]{:S(2)}, u32[]{:S(2)}) collective-permute-start(f32[512,128]{1,0:T(8,128)} %get-tuple-element.56), channel_id=1, source_target_pairs={{0,1},{1,0},{2,3},{3,2},{4,5},{5,4},{6,7},{7,6},{8,9},{9,8},{10,11... | collective-permute-start | bytes 786440 | tf_op jit(solution)/shard_map/ppermute | solution.py:250
  12.3 5.7 %collective-permute-start = (f32[128,128]{1,0:T(8,128)S(1)}, f32[128,128]{1,0:T(8,128)S(1)}, u32[]{:S(2)}, u32[]{:S(2)}) collective-permute-start(f32[128,128]{1,0:T(8,128)S(1)} %bitcast.27), channel_id=1, source_target_pairs={{0,4},{4,8},{8,12},{12,16},{16,20},{20,24},{24,28},{1,5},{5,9},{9,... | collective-permute-start | bytes 196616 | tf_op jit(solution)/shard_map/ppermute | solution.py:271
  16.1 3.4 %collective-permute-start.9 = (f32[128,128]{1,0:T(8,128)}, f32[128,128]{1,0:T(8,128)S(1)}, u32[]{:S(2)}, u32[]{:S(2)}) collective-permute-start(f32[128,128]{1,0:T(8,128)} %get-tuple-element.48), channel_id=1, source_target_pairs={{0,1},{1,0},{2,3},{3,2},{4,5},{5,4},{6,7},{7,6},{8,9},{9,8},{10,11... | collective-permute-start | bytes 196616 | tf_op jit(solution)/shard_map/ppermute | solution.py:250
  18.0 17.2 %collective-permute-start.2 = (f32[512,128]{1,0:T(8,128)S(1)}, f32[512,128]{1,0:T(8,128)S(1)}, u32[]{:S(2)}, u32[]{:S(2)}) collective-permute-start(f32[512,128]{1,0:T(8,128)S(1)} %copy-done.9), channel_id=1, source_target_pairs={{0,2},{1,3},{2,0},{3,1},{4,6},{5,7},{6,4},{7,5},{8,10},{9,11},{10,... | collective-permute-start | bytes 786440 | tf_op jit(solution)/shard_map/ppermute | solution.py:250
  19.5 17.2 %collective-permute-start.3 = (f32[512,128]{1,0:T(8,128)S(1)}, f32[512,128]{1,0:T(8,128)S(1)}, u32[]{:S(2)}, u32[]{:S(2)}) collective-permute-start(f32[512,128]{1,0:T(8,128)S(1)} %copy-done.8), channel_id=1, source_target_pairs={{0,3},{1,2},{2,1},{3,0},{4,7},{5,6},{6,5},{7,4},{8,11},{9,10},{10,... | collective-permute-start | bytes 786440 | tf_op jit(solution)/shard_map/ppermute | solution.py:250
  19.5 3.2 %collective-permute-start.12 = (f32[256,128]{1,0:T(8,128)}, f32[256,128]{1,0:T(8,128)S(1)}, u32[]{:S(2)}, u32[]{:S(2)}) collective-permute-start(f32[256,128]{1,0:T(8,128)} %get-tuple-element.52), channel_id=1, source_target_pairs={{0,1},{1,0},{2,3},{3,2},{4,5},{5,4},{6,7},{7,6},{8,9},{9,8},{10,11... | collective-permute-start | bytes 393224 | tf_op jit(solution)/shard_map/ppermute | solution.py:250
  20.1 15.1 %collective-permute-start.13 = (f32[256,128]{1,0:T(8,128)}, f32[256,128]{1,0:T(8,128)S(1)}, u32[]{:S(2)}, u32[]{:S(2)}) collective-permute-start(f32[256,128]{1,0:T(8,128)} %get-tuple-element.53), channel_id=1, source_target_pairs={{0,2},{1,3},{2,0},{3,1},{4,6},{5,7},{6,4},{7,5},{8,10},{9,11},{10,... | collective-permute-start | bytes 393224 | tf_op jit(solution)/shard_map/ppermute | solution.py:250
  21.6 15.4 %collective-permute-start.1 = (f32[512,128]{1,0:T(8,128)}, f32[512,128]{1,0:T(8,128)S(1)}, u32[]{:S(2)}, u32[]{:S(2)}) collective-permute-start(f32[512,128]{1,0:T(8,128)} %get-tuple-element.40), channel_id=1, source_target_pairs={{0,1},{1,0},{2,3},{3,2},{4,5},{5,4},{6,7},{7,6},{8,9},{9,8},{10,11... | collective-permute-start | bytes 786440 | tf_op jit(solution)/shard_map/ppermute | solution.py:250
  21.6 48.0 %copy-start = (f32[512,128]{1,0:T(8,128)S(1)}, f32[512,128]{1,0:T(8,128)}, u32[]{:S(2)}) copy-start(f32[512,128]{1,0:T(8,128)} %get-tuple-element.39.refs_2_) | copy-start | bytes 786436
  21.6 48.0 %copy-start.4 = (f32[256,128]{1,0:T(8,128)S(1)}, f32[256,128]{1,0:T(8,128)}, u32[]{:S(2)}) copy-start(f32[256,128]{1,0:T(8,128)} %get-tuple-element.51.refs_8_) | copy-start | bytes 393220
  22.7 16.6 %collective-permute-start.14 = (f32[256,128]{1,0:T(8,128)}, f32[256,128]{1,0:T(8,128)S(1)}, u32[]{:S(2)}, u32[]{:S(2)}) collective-permute-start(f32[256,128]{1,0:T(8,128)} %get-tuple-element.54), channel_id=1, source_target_pairs={{0,3},{1,2},{2,1},{3,0},{4,7},{5,6},{6,5},{7,4},{8,11},{9,10},{10,... | collective-permute-start | bytes 393224 | tf_op jit(solution)/shard_map/ppermute | solution.py:250
  35.2 8.8 %collective-permute-start.20 = (f32[512,128]{1,0:T(8,128)}, f32[512,128]{1,0:T(8,128)S(1)}, u32[]{:S(2)}, u32[]{:S(2)}) collective-permute-start(f32[512,128]{1,0:T(8,128)} %get-tuple-element.59), channel_id=1, source_target_pairs={{0,1},{1,0},{2,3},{3,2},{4,5},{5,4},{6,7},{7,6},{8,9},{9,8},{10,11... | collective-permute-start | bytes 786440 | tf_op jit(solution)/shard_map/ppermute | solution.py:250
  35.2 10.1 %collective-permute-start.21 = (f32[512,128]{1,0:T(8,128)}, f32[512,128]{1,0:T(8,128)S(1)}, u32[]{:S(2)}, u32[]{:S(2)}) collective-permute-start(f32[512,128]{1,0:T(8,128)} %get-tuple-element.60), channel_id=1, source_target_pairs={{0,2},{1,3},{2,0},{3,1},{4,6},{5,7},{6,4},{7,5},{8,10},{9,11},{10,... | collective-permute-start | bytes 786440 | tf_op jit(solution)/shard_map/ppermute | solution.py:250
  36.7 14.1 %collective-permute-start.22 = (f32[512,128]{1,0:T(8,128)}, f32[512,128]{1,0:T(8,128)S(1)}, u32[]{:S(2)}, u32[]{:S(2)}) collective-permute-start(f32[512,128]{1,0:T(8,128)} %get-tuple-element.61), channel_id=1, source_target_pairs={{0,3},{1,2},{2,1},{3,0},{4,7},{5,6},{6,5},{7,4},{8,11},{9,10},{10,... | collective-permute-start | bytes 786440 | tf_op jit(solution)/shard_map/ppermute | solution.py:250
  37.0 15.3 %collective-permute-start.19 = (f32[512,128]{1,0:T(8,128)S(1)}, f32[512,128]{1,0:T(8,128)S(1)}, u32[]{:S(2)}, u32[]{:S(2)}) collective-permute-start(f32[512,128]{1,0:T(8,128)S(1)} %get-tuple-element.72), channel_id=1, source_target_pairs={{4,0},{8,4},{12,8},{16,12},{20,16},{24,20},{28,24},{5,1},{9,5},{13... | collective-permute-start | bytes 786440 | tf_op jit(solution)/shard_map/ppermute | solution.py:289
  39.4 19.8 %collective-permute-start.18 = (f32[512,128]{1,0:T(8,128)S(1)}, f32[512,128]{1,0:T(8,128)S(1)}, u32[]{:S(2)}, u32[]{:S(2)}) collective-permute-start(f32[512,128]{1,0:T(8,128)S(1)} %get-tuple-element.73), channel_id=1, source_target_pairs={{0,4},{4,8},{8,12},{12,16},{16,20},{20,24},{24,28},{1,5},{5,9},{9,... | collective-permute-start | bytes 786440 | tf_op jit(solution)/shard_map/ppermute | solution.py:290
  44.0 15.2 %collective-permute-start.5 = (f32[512,128]{1,0:T(8,128)S(1)}, f32[512,128]{1,0:T(8,128)S(1)}, u32[]{:S(2)}, u32[]{:S(2)}) collective-permute-start(f32[512,128]{1,0:T(8,128)S(1)} %get-tuple-element.74), channel_id=1, source_target_pairs={{4,0},{8,4},{12,8},{16,12},{20,16},{24,20},{28,24},{5,1},{9,5},{13... | collective-permute-start | bytes 786440 | tf_op jit(solution)/shard_map/ppermute | solution.py:289
  45.3 19.5 %collective-permute-start.4 = (f32[512,128]{1,0:T(8,128)S(1)}, f32[512,128]{1,0:T(8,128)S(1)}, u32[]{:S(2)}, u32[]{:S(2)}) collective-permute-start(f32[512,128]{1,0:T(8,128)S(1)} %get-tuple-element.75), channel_id=1, source_target_pairs={{0,4},{4,8},{8,12},{12,16},{16,20},{20,24},{24,28},{1,5},{5,9},{9,... | collective-permute-start | bytes 786440 | tf_op jit(solution)/shard_map/ppermute | solution.py:290
  50.8 20.1 %collective-permute-start.10 = (f32[128,128]{1,0:T(8,128)}, f32[128,128]{1,0:T(8,128)S(1)}, u32[]{:S(2)}, u32[]{:S(2)}) collective-permute-start(f32[128,128]{1,0:T(8,128)} %get-tuple-element.49), channel_id=1, source_target_pairs={{0,2},{1,3},{2,0},{3,1},{4,6},{5,7},{6,4},{7,5},{8,10},{9,11},{10,... | collective-permute-start | bytes 196616 | tf_op jit(solution)/shard_map/ppermute | solution.py:250
  52.4 18.5 %collective-permute-start.11 = (f32[128,128]{1,0:T(8,128)}, f32[128,128]{1,0:T(8,128)S(1)}, u32[]{:S(2)}, u32[]{:S(2)}) collective-permute-start(f32[128,128]{1,0:T(8,128)} %get-tuple-element.50), channel_id=1, source_target_pairs={{0,3},{1,2},{2,1},{3,0},{4,7},{5,6},{6,5},{7,4},{8,11},{9,10},{10,... | collective-permute-start | bytes 196616 | tf_op jit(solution)/shard_map/ppermute | solution.py:250
  59.2 12.3 %collective-permute-start.6 = (f32[128,128]{1,0:T(8,128)}, f32[128,128]{1,0:T(8,128)S(1)}, u32[]{:S(2)}, u32[]{:S(2)}) collective-permute-start(f32[128,128]{1,0:T(8,128)} %get-tuple-element.44), channel_id=1, source_target_pairs={{0,1},{1,0},{2,3},{3,2},{4,5},{5,4},{6,7},{7,6},{8,9},{9,8},{10,11... | collective-permute-start | bytes 196616 | tf_op jit(solution)/shard_map/ppermute | solution.py:250
  59.2 12.3 %collective-permute-start.7 = (f32[128,128]{1,0:T(8,128)}, f32[128,128]{1,0:T(8,128)S(1)}, u32[]{:S(2)}, u32[]{:S(2)}) collective-permute-start(f32[128,128]{1,0:T(8,128)} %get-tuple-element.45), channel_id=1, source_target_pairs={{0,2},{1,3},{2,0},{3,1},{4,6},{5,7},{6,4},{7,5},{8,10},{9,11},{10,... | collective-permute-start | bytes 196616 | tf_op jit(solution)/shard_map/ppermute | solution.py:250
  64.8 6.7 %collective-permute-start.8 = (f32[128,128]{1,0:T(8,128)}, f32[128,128]{1,0:T(8,128)S(1)}, u32[]{:S(2)}, u32[]{:S(2)}) collective-permute-start(f32[128,128]{1,0:T(8,128)} %get-tuple-element.46), channel_id=1, source_target_pairs={{0,3},{1,2},{2,1},{3,0},{4,7},{5,6},{6,5},{7,4},{8,11},{9,10},{10,... | collective-permute-start | bytes 196616 | tf_op jit(solution)/shard_map/ppermute | solution.py:250
  67.2 3.6 %copy-start.6 = (f32[128,128]{1,0:T(8,128)S(1)}, f32[128,128]{1,0:T(8,128)}, u32[]{:S(2)}) copy-start(f32[128,128]{1,0:T(8,128)} %get-tuple-element.47.refs_8_) | copy-start | bytes 196612
  69.6 1.9 %copy-start.5 = (f32[128,128]{1,0:T(8,128)S(1)}, f32[128,128]{1,0:T(8,128)}, u32[]{:S(2)}) copy-start(f32[128,128]{1,0:T(8,128)} %get-tuple-element.43.refs_8_) | copy-start | bytes 196612

commit v6 on v5

--- a/solution.py
+++ b/solution.py
@@ -189,14 +189,15 @@
         lane = lax.broadcasted_iota(jnp.int32, (group, LANES), 1)
         diagonal = lane == lax.broadcasted_iota(jnp.int32, (group, LANES), 0)
         row = jnp.sum(jnp.where(diagonal, whole, 0.0), axis=0, keepdims=True)
-        sums[...] = jnp.broadcast_to(row, sums.shape)
+        top = lax.broadcasted_iota(jnp.int32, sums.shape, 0) == 0
+        sums[...] = jnp.where(top, row, 0.0)
 
 
 def scale_kernel(chunks, size, *refs):
-    total, parts, out, norms, buf, spread, out_sem = refs[0], refs[1:-5], *refs[-5:]
+    total, other, parts, out, norms, buf, spread, out_sem = refs[0], refs[1], refs[2:-5], *refs[-5:]
     group = sum(n for _, n in chunks)
     per = out.shape[0] // group
-    norm = jnp.sqrt(jnp.sum(total[...], axis=0, keepdims=True) / size + 1e-06)
+    norm = jnp.sqrt(jnp.sum(total[...] + other[...], axis=0, keepdims=True) / size + 1e-06)
     spread[...] = norm[:, :group]
     norms_copy = pltpu.make_async_copy(spread, norms, out_sem.at[group])
     norms_copy.start()
@@ -325,14 +326,18 @@
             name="defect",
         )(spots, weights, *ins, *([sums] if lo else []))
         parts.append(part)
-    sums = lax.all_to_all(sums, "vtx", 0, 0, tiled=True)
+    steps = [1 << i for i in range((peers - 1).bit_length())]
+    for step in steps:
+        other = lax.ppermute(sums, "vtx", [(i, i ^ step) for i in range(peers)])
+        if step != steps[-1]:
+            sums = sums + other
     out, norms = pl.pallas_call(
         functools.partial(scale_kernel, chunks, float(total_rows * width)),
         out_shape=(
             jax.ShapeDtypeStruct((group * per, LANES), jnp.float32),
             jax.ShapeDtypeStruct((1, group), jnp.float32),
         ),
-        in_specs=[vmem] + [vmem] * len(parts),
+        in_specs=[vmem, vmem] + [vmem] * len(parts),
         out_specs=(pl.BlockSpec(memory_space=pltpu.HBM), pl.BlockSpec(memory_space=pltpu.HBM)),
         scratch_shapes=[
             pltpu.VMEM((group * per + group, LANES), jnp.float32),
@@ -342,7 +347,7 @@
         cost_estimate=pl.CostEstimate(flops=group * per * LANES, bytes_accessed=8 * group * per * LANES, transcendentals=0),
         compiler_params=pltpu.CompilerParams(vmem_limit_bytes=12 << 20),
         name="scale",
-    )(sums, *parts)
+    )(sums, other, *parts)
     out = out.reshape(group, cb, rows_dev, LANES).transpose(0, 2, 1, 3).reshape(group, rows_dev, width)
     return out, norms.reshape(group)
 

time: 87.4 us -> 87.6 us (level)
  blocking collectives: 12.5 us -> 0 us
  starting transfers between devices: 30.3 us -> 38.3 us
  waiting for transfers between devices: 24.5 us -> 29.2 us
    all_to_all x1 -> x0, blocking collectives: 12.5 us -> none  [program(): sums = lax.all_to_all(sums, 'vtx', 0, 0, tiled=True)]
    ppermute x0 -> x3, starting transfers between devices: none -> 7.98 us  [program(): other = lax.ppermute(sums, 'vtx', [(i, i ^ step) for i in range(peers)])]
    ppermute x0 -> x3, waiting for transfers between devices: none -> 4.75 us  [program(): other = lax.ppermute(sums, 'vtx', [(i, i ^ step) for i in range(peers)])]
  transfers between devices with their start and end apart: 23 -> 26, of which waited for: 4 -> 7; matrix products, arithmetic and copies ran while one was open for 2% -> 2% of each run, Pallas kernels for 14% -> 13%
where the time goes in v6:
time: 87.6 us; the launch traced here: 87.2 us
  starting transfers between devices  38.3 us (44%)
  waiting for transfers between devices  29.2 us (33%)
  Pallas kernels  16.5 us (19%)
  other arithmetic  2.08 us (2%)
  between operations  0.98 us (1%)
    ppermute x18, starting transfers between devices, send(): lax.ppermute(piece, 'src', [(i, i ^ k) for i in range(senders)])  13.9 us
    ppermute x18, waiting for transfers between devices, send(): lax.ppermute(piece, 'src', [(i, i ^ k) for i in range(senders)])  11.8 us
    ppermute x2, waiting for transfers between devices, program(): below.append(lax.ppermute(last, 'vtx', up))  10.9 us
    ppermute x2, starting transfers between devices, program(): below.append(lax.ppermute(last, 'vtx', up))  10.1 us
    pallas_call x3, Pallas kernels, pack(): pl.pallas_call(functools.partial(pack_kernel, (tuple(plan), group, cb, ow...  8.11 us
    ppermute x3, starting transfers between devices, program(): other = lax.ppermute(sums, 'vtx', [(i, i ^ step) for i in range(peers)])  7.98 us
    pallas_call x4, Pallas kernels, program(): pl.pallas_call(functools.partial(defect_kernel, meta, lo, n, group, ampli...  4.84 us
    ppermute x3, waiting for transfers between devices, program(): other = lax.ppermute(sums, 'vtx', [(i, i ^ step) for i in range(peers)])  4.75 us
  transfers between devices with their start and end apart: 26, of which 7 were waited for; matrix products, arithmetic and copies ran while one was open for 2% of the time, Pallas kernels for 13%

profile of v6, /device:TPU:0, one launch (start us, length us, event | category | flops | bytes accessed | tf_op | source)
XLA Modules:
  0.0 87.2 jit_solution(9282691087882936912)
XLA Ops:
  0.6 1.8 %shard_map.52 = f32[512,128]{1,0:T(8,128)} custom-call(f32[8192,128]{1,0:T(8,128)} %bitcast.18), custom_call_target="tpu_custom_call" | custom-call | flops 65536 | bytes 786432 | tf_op jit(solution)/shard_map/pallas_call | solution.py:60
  2.4 0.0 copy-start.1
  2.4 3.1 %collective-permute-start.16 = (f32[512,128]{1,0:T(8,128)}, f32[512,128]{1,0:T(8,128)S(1)}, u32[]{:S(2)}, u32[]{:S(2)}) collective-permute-start(f32[512,128]{1,0:T(8,128)} %shard_map.52), channel_id=1, source_target_pairs={{0,2},{1,3},{2,0},{3,1},{4,6},{5,7},{6,4},{7,5},{8,10},{9,11},{10,... | collective-permute-start | bytes 786440 | tf_op jit(solution)/shard_map/ppermute | solution.py:251
  5.5 2.3 %shard_map.51 = (f32[512,128]{1,0:T(8,128)}, f32[512,128]{1,0:T(8,128)}, f32[512,128]{1,0:T(8,128)}) custom-call(f32[8192,128]{1,0:T(8,128)} %bitcast.19), custom_call_target="tpu_custom_call" | custom-call | flops 196608 | bytes 2359296 | tf_op jit(solution)/shard_map/pallas_call | solution.py:60
  7.9 0.0 copy-start.7
  7.9 0.1 collective-permute-start.17
  7.9 4.0 %shard_map.50 = (f32[512,128]{1,0:T(8,128)}, f32[512,128]{1,0:T(8,128)}, f32[512,128]{1,0:T(8,128)}, f32[512,128]{1,0:T(8,128)}, f32[512,128]{1,0:T(8,128)}, /*i...) custom-call(f32[8192,128]{1,0:T(8,128)} %bitcast.20), custom_call_target="tpu_custom_call" | custom-call | flops 786432 | bytes 7340032 | tf_op jit(solution)/shard_map/pallas_call | solution.py:60
  12.0 0.2 collective-permute-start.15
  12.2 0.1 slice.3
  12.2 3.8 %collective-permute-start = (f32[128,128]{1,0:T(8,128)S(1)}, f32[128,128]{1,0:T(8,128)S(1)}, u32[]{:S(2)}, u32[]{:S(2)}) collective-permute-start(f32[128,128]{1,0:T(8,128)S(1)} %bitcast.21), channel_id=1, source_target_pairs={{0,4},{4,8},{8,12},{12,16},{16,20},{20,24},{24,28},{1,5},{5,9},{9,... | collective-permute-start | bytes 196616 | tf_op jit(solution)/shard_map/ppermute | solution.py:272
  16.1 0.1 collective-permute-start.9
  16.1 1.8 %collective-permute-done.lower = f32[128,128]{1,0:T(8,128)S(1)} collective-permute-done((f32[128,128]{1,0:T(8,128)S(1)}, f32[128,128]{1,0:T(8,128)S(1)}, u32[]{:S(2)}, u32[]{:S(2)}) %collective-permute-start) | collective-permute-done | bytes 65568 | tf_op jit(solution)/shard_map/ppermute | solution.py:272
  17.9 1.5 %collective-permute-start.2 = (f32[512,128]{1,0:T(8,128)S(1)}, f32[512,128]{1,0:T(8,128)S(1)}, u32[]{:S(2)}, u32[]{:S(2)}) collective-permute-start(f32[512,128]{1,0:T(8,128)S(1)} %copy-done.9), channel_id=1, source_target_pairs={{0,2},{1,3},{2,0},{3,1},{4,6},{5,7},{6,4},{7,5},{8,10},{9,11},{10,... | collective-permute-start | bytes 786440 | tf_op jit(solution)/shard_map/ppermute | solution.py:251
  19.5 0.0 collective-permute-done.9.refs_9_
  19.5 0.0 collective-permute-start.3
  19.5 0.0 collective-permute-done.16.refs_4_
  19.5 0.6 collective-permute-start.12
  20.1 0.0 collective-permute-done.17.refs_5_
  20.1 1.5 %collective-permute-start.13 = (f32[256,128]{1,0:T(8,128)}, f32[256,128]{1,0:T(8,128)S(1)}, u32[]{:S(2)}, u32[]{:S(2)}) collective-permute-start(f32[256,128]{1,0:T(8,128)} %get-tuple-element.53), channel_id=1, source_target_pairs={{0,2},{1,3},{2,0},{3,1},{4,6},{5,7},{6,4},{7,5},{8,10},{9,11},{10,... | collective-permute-start | bytes 393224 | tf_op jit(solution)/shard_map/ppermute | solution.py:251
  21.6 0.0 collective-permute-done.15.refs_3_
  21.6 0.0 collective-permute-start.1
  21.6 1.1 %select_select_fusion = (f32[512,128]{1,0:T(8,128)S(1)}, f32[512,128]{1,0:T(8,128)S(1)}) fusion(f32[512,128]{1,0:T(8,128)S(1)} %collective-permute-done.16.refs_4_, f32[512,128]{1,0:T(8,128)S(1)} %collective-permute-done.17.refs_5_, f32[512,128]{1,0:T(8,128)} %get-tuple-element.55.refs_2_, f32[512,128]{1,0:T(8,128)S(1)} %collective-permute-done.15.refs_3_, ...), kind=kLoop, calls=%fused_computation | loop fusion | flops 393216 | bytes 1572867 | tf_op jit(solution)/shard_map/select_n | solution.py:288
  22.7 0.0 collective-permute-done.12.refs_9_
  22.7 0.7 collective-permute-start.14
  23.4 11.8 %collective-permute-done.13.refs_10_ = f32[256,128]{1,0:T(8,128)S(1)} collective-permute-done((f32[256,128]{1,0:T(8,128)}, f32[256,128]{1,0:T(8,128)S(1)}, u32[]{:S(2)}, u32[]{:S(2)}) %collective-permute-start.13) | collective-permute-done | bytes 131104 | tf_op jit(solution)/shard_map/ppermute | solution.py:251
  35.2 0.0 collective-permute-start.20
  35.2 0.0 collective-permute-done.2.refs_4_
  35.2 1.5 %collective-permute-start.21 = (f32[512,128]{1,0:T(8,128)}, f32[512,128]{1,0:T(8,128)S(1)}, u32[]{:S(2)}, u32[]{:S(2)}) collective-permute-start(f32[512,128]{1,0:T(8,128)} %get-tuple-element.60), channel_id=1, source_target_pairs={{0,2},{1,3},{2,0},{3,1},{4,6},{5,7},{6,4},{7,5},{8,10},{9,11},{10,... | collective-permute-start | bytes 786440 | tf_op jit(solution)/shard_map/ppermute | solution.py:251
  36.7 0.0 collective-permute-done.3.refs_5_
  36.7 0.3 collective-permute-start.22
  37.0 0.0 collective-permute-done.1.refs_3_
  37.0 1.3 %collective-permute-start.19 = (f32[512,128]{1,0:T(8,128)S(1)}, f32[512,128]{1,0:T(8,128)S(1)}, u32[]{:S(2)}, u32[]{:S(2)}) collective-permute-start(f32[512,128]{1,0:T(8,128)S(1)} %get-tuple-element.72), channel_id=1, source_target_pairs={{4,0},{8,4},{12,8},{16,12},{20,16},{24,20},{28,24},{5,1},{9,5},{13... | collective-permute-start | bytes 786440 | tf_op jit(solution)/shard_map/ppermute | solution.py:290
  38.3 1.0 %select_select_fusion.2 = (f32[512,128]{1,0:T(8,128)S(1)}, f32[512,128]{1,0:T(8,128)S(1)}) fusion(f32[512,128]{1,0:T(8,128)S(1)} %collective-permute-done.2.refs_4_, f32[512,128]{1,0:T(8,128)S(1)} %collective-permute-done.3.refs_5_, f32[512,128]{1,0:T(8,128)} %get-tuple-element.39.refs_2_, f32[512,128]{1,0:T(8,128)S(1)} %collective-permute-done.1.refs_3_, ...), kind=kLoop, calls=%fused_computation.2 | loop fusion | flops 393216 | bytes 1572867 | tf_op jit(solution)/shard_map/select_n | solution.py:288
  39.3 0.0 collective-permute-done.14.refs_11_
  39.3 4.6 %collective-permute-start.18 = (f32[512,128]{1,0:T(8,128)S(1)}, f32[512,128]{1,0:T(8,128)S(1)}, u32[]{:S(2)}, u32[]{:S(2)}) collective-permute-start(f32[512,128]{1,0:T(8,128)S(1)} %get-tuple-element.73), channel_id=1, source_target_pairs={{0,4},{4,8},{8,12},{12,16},{16,20},{20,24},{24,28},{1,5},{5,9},{9,... | collective-permute-start | bytes 786440 | tf_op jit(solution)/shard_map/ppermute | solution.py:291
  44.0 0.0 collective-permute-done.20.refs_9_
  44.0 1.3 %collective-permute-start.5 = (f32[512,128]{1,0:T(8,128)S(1)}, f32[512,128]{1,0:T(8,128)S(1)}, u32[]{:S(2)}, u32[]{:S(2)}) collective-permute-start(f32[512,128]{1,0:T(8,128)S(1)} %get-tuple-element.74), channel_id=1, source_target_pairs={{4,0},{8,4},{12,8},{16,12},{20,16},{24,20},{28,24},{5,1},{9,5},{13... | collective-permute-start | bytes 786440 | tf_op jit(solution)/shard_map/ppermute | solution.py:290
  45.3 0.0 collective-permute-done.21.refs_10_
  45.3 5.4 %collective-permute-start.4 = (f32[512,128]{1,0:T(8,128)S(1)}, f32[512,128]{1,0:T(8,128)S(1)}, u32[]{:S(2)}, u32[]{:S(2)}) collective-permute-start(f32[512,128]{1,0:T(8,128)S(1)} %get-tuple-element.75), channel_id=1, source_target_pairs={{0,4},{4,8},{8,12},{12,16},{16,20},{20,24},{24,28},{1,5},{5,9},{9,... | collective-permute-start | bytes 786440 | tf_op jit(solution)/shard_map/ppermute | solution.py:291
  50.7 0.0 collective-permute-done.22.refs_11_
  50.8 1.6 %collective-permute-start.10 = (f32[128,128]{1,0:T(8,128)}, f32[128,128]{1,0:T(8,128)S(1)}, u32[]{:S(2)}, u32[]{:S(2)}) collective-permute-start(f32[128,128]{1,0:T(8,128)} %get-tuple-element.49), channel_id=1, source_target_pairs={{0,2},{1,3},{2,0},{3,1},{4,6},{5,7},{6,4},{7,5},{8,10},{9,11},{10,... | collective-permute-start | bytes 196616 | tf_op jit(solution)/shard_map/ppermute | solution.py:251
  52.3 0.0 collective-permute-done.19.refs_7_
  52.3 0.0 collective-permute-start.11
  52.3 6.8 %collective-permute-done.18.refs_6_ = f32[512,128]{1,0:T(8,128)S(1)} collective-permute-done((f32[512,128]{1,0:T(8,128)S(1)}, f32[512,128]{1,0:T(8,128)S(1)}, u32[]{:S(2)}, u32[]{:S(2)}) %collective-permute-start.18) | collective-permute-done | bytes 262176 | tf_op jit(solution)/shard_map/ppermute | solution.py:291
  59.2 0.0 collective-permute-start.6
  59.2 1.5 %collective-permute-start.7 = (f32[128,128]{1,0:T(8,128)}, f32[128,128]{1,0:T(8,128)S(1)}, u32[]{:S(2)}, u32[]{:S(2)}) collective-permute-start(f32[128,128]{1,0:T(8,128)} %get-tuple-element.45), channel_id=1, source_target_pairs={{0,2},{1,3},{2,0},{3,1},{4,6},{5,7},{6,4},{7,5},{8,10},{9,11},{10,... | collective-permute-start | bytes 196616 | tf_op jit(solution)/shard_map/ppermute | solution.py:251
  60.7 4.0 %collective-permute-done.4.refs_6_ = f32[512,128]{1,0:T(8,128)S(1)} collective-permute-done((f32[512,128]{1,0:T(8,128)S(1)}, f32[512,128]{1,0:T(8,128)S(1)}, u32[]{:S(2)}, u32[]{:S(2)}) %collective-permute-start.4) | collective-permute-done | bytes 262176 | tf_op jit(solution)/shard_map/ppermute | solution.py:291
  64.8 1.2 %collective-permute-start.8 = (f32[128,128]{1,0:T(8,128)}, f32[128,128]{1,0:T(8,128)S(1)}, u32[]{:S(2)}, u32[]{:S(2)}) collective-permute-start(f32[128,128]{1,0:T(8,128)} %get-tuple-element.46), channel_id=1, source_target_pairs={{0,3},{1,2},{2,1},{3,0},{4,7},{5,6},{6,5},{7,4},{8,11},{9,10},{10,... | collective-permute-start | bytes 196616 | tf_op jit(solution)/shard_map/ppermute | solution.py:251
  65.9 1.3 %weights.1 = (f32[7,8,72,128]{3,2,1,0:T(8,128)S(1)}, s32[16,128]{1,0:T(8,128)S(1)}) custom-call(s32[64]{0:T(128)S(1)} %copy-done.7, f32[2048,128]{1,0:T(8,128)S(1)} %bitcast.17, f32[128,128]{1,0:T(8,128)S(1)} %collective-permute-done.lower), custom_call_target="tpu_custom_call" | custom-call | flops 1310720 | bytes 2883584 | tf_op jit(solution)/shard_map/weights/pallas_call | solution.py:274
  67.2 2.4 %defect.4 = (f32[4096,128]{1,0:T(8,128)S(1)}, f32[16,128]{1,0:T(8,128)S(1)}) custom-call(s32[16,128]{1,0:T(8,128)S(1)} %get-tuple-element.37.refs_0_, f32[7,8,72,128]{3,2,1,0:T(8,128)S(1)} %get-tuple-element.38.refs_1_, f32[512,128]{1,0:T(8,128)S(1)} %copy-done.2, f32[512,128]{1,0:T(8,128)S(1)} %collective-permute-done.15.refs_3_, ...), custom_call_target="tpu_custom_call" | custom-call | flops 10485760 | bytes 4194304 | tf_op jit(solution)/shard_map/defect/pallas_call | solution.py:312
  69.6 1.2 %defect.5 = (f32[2048,128]{1,0:T(8,128)S(1)}, f32[16,128]{1,0:T(8,128)S(1)}) custom-call(s32[16,128]{1,0:T(8,128)S(1)} %get-tuple-element.37.refs_0_, f32[7,8,72,128]{3,2,1,0:T(8,128)S(1)} %get-tuple-element.38.refs_1_, f32[512,128]{1,0:T(8,128)S(1)} %copy-done, f32[512,128]{1,0:T(8,128)S(1)} %collective-permute-done.1.refs_3_, ...), custom_call_target="tpu_custom_call" | custom-call | flops 5242880 | bytes 2097152 | tf_op jit(solution)/shard_map/defect/pallas_call | solution.py:312
  70.8 0.0 collective-permute-done.10.refs_10_
  70.8 0.0 collective-permute-done.11.refs_11_
  70.8 0.6 defect.6
  71.5 0.0 collective-permute-done.7.refs_10_
  71.5 0.0 collective-permute-done.8.refs_11_
  71.5 0.7 defect.7
  72.2 2.5 %collective-permute-start.23 = (f32[8,128]{1,0:T(8,128)S(1)}, f32[8,128]{1,0:T(8,128)S(1)}, u32[]{:S(2)}, u32[]{:S(2)}) collective-permute-start(f32[8,128]{1,0:T(8,128)S(1)} %get-tuple-element.65), channel_id=1, source_target_pairs={{0,4},{4,0},{8,12},{12,8},{16,20},{20,16},{24,28},{28,24},{1,5},{5... | collective-permute-start | bytes 12296 | tf_op jit(solution)/shard_map/ppermute | solution.py:331
  74.7 1.6 %collective-permute-done.23 = f32[8,128]{1,0:T(8,128)S(1)} collective-permute-done((f32[8,128]{1,0:T(8,128)S(1)}, f32[8,128]{1,0:T(8,128)S(1)}, u32[]{:S(2)}, u32[]{:S(2)}) %collective-permute-start.23) | collective-permute-done | bytes 4128 | tf_op jit(solution)/shard_map/ppermute | solution.py:331
  76.3 2.5 %collective-permute-start.24 = (f32[8,128]{1,0:T(8,128)S(1)}, f32[8,128]{1,0:T(8,128)S(1)}, u32[]{:S(2)}, u32[]{:S(2)}) collective-permute-start(f32[8,128]{1,0:T(8,128)S(1)} %add.6), channel_id=1, source_target_pairs={{0,8},{4,12},{8,0},{12,4},{16,24},{20,28},{24,16},{28,20},{1,9},{5... | collective-permute-start | bytes 12296 | tf_op jit(solution)/shard_map/ppermute | solution.py:331
  78.7 1.6 %collective-permute-done.24 = f32[8,128]{1,0:T(8,128)S(1)} collective-permute-done((f32[8,128]{1,0:T(8,128)S(1)}, f32[8,128]{1,0:T(8,128)S(1)}, u32[]{:S(2)}, u32[]{:S(2)}) %collective-permute-start.24) | collective-permute-done | bytes 4128 | tf_op jit(solution)/shard_map/ppermute | solution.py:331
  80.3 3.0 %collective-permute-start.25 = (f32[8,128]{1,0:T(8,128)S(1)}, f32[8,128]{1,0:T(8,128)S(1)}, u32[]{:S(2)}, u32[]{:S(2)}) collective-permute-start(f32[8,128]{1,0:T(8,128)S(1)} %add.7.refs_0_), channel_id=1, source_target_pairs={{0,16},{4,20},{8,24},{12,28},{16,0},{20,4},{24,8},{28,12},{1,17},{... | collective-permute-start | bytes 12296 | tf_op jit(solution)/shard_map/ppermute | solution.py:331
  83.4 1.6 %collective-permute-done.25.refs_1_ = f32[8,128]{1,0:T(8,128)S(1)} collective-permute-done((f32[8,128]{1,0:T(8,128)S(1)}, f32[8,128]{1,0:T(8,128)S(1)}, u32[]{:S(2)}, u32[]{:S(2)}) %collective-permute-start.25) | collective-permute-done | bytes 4128 | tf_op jit(solution)/shard_map/ppermute | solution.py:331
  84.9 2.3 %scale.1 = (f32[8192,128]{1,0:T(8,128)}, f32[1,16]{1,0:T(1,128)}) custom-call(f32[8,128]{1,0:T(8,128)S(1)} %add.7.refs_0_, f32[8,128]{1,0:T(8,128)S(1)} %collective-permute-done.25.refs_1_, f32[4096,128]{1,0:T(8,128)S(1)} %get-tuple-element.66.refs_2_, f32[2048,128]{1,0:T(8,128)S(1)} %get-tuple-element.67.refs_3_, ...), custom_call_target="tpu_custom_call" | custom-call | flops 1048576 | bytes 8388608 | tf_op jit(solution)/shard_map/scale/pallas_call | solution.py:334
  (22 shorter events, 0.0 us)
Async XLA Ops:
  2.4 9.7 %copy-start.1 = (f32[4,8,8192]{2,1,0:T(8,128)S(1)}, f32[4,8,8192]{2,1,0:T(8,128)}, u32[]{:S(2)}) copy-start(f32[4,8,8192]{2,1,0:T(8,128)} %param.4) | copy-start | bytes 3145732
  2.4 17.0 %collective-permute-start.16 = (f32[512,128]{1,0:T(8,128)}, f32[512,128]{1,0:T(8,128)S(1)}, u32[]{:S(2)}, u32[]{:S(2)}) collective-permute-start(f32[512,128]{1,0:T(8,128)} %shard_map.52), channel_id=1, source_target_pairs={{0,2},{1,3},{2,0},{3,1},{4,6},{5,7},{6,4},{7,5},{8,10},{9,11},{10,... | collective-permute-start | bytes 786440 | tf_op jit(solution)/shard_map/ppermute | solution.py:251
  7.8 10.1 %copy-start.9 = (f32[512,128]{1,0:T(8,128)S(1)}, f32[512,128]{1,0:T(8,128)}, u32[]{:S(2)}) copy-start(f32[512,128]{1,0:T(8,128)} %get-tuple-element.41) | copy-start | bytes 786436
  7.8 11.6 %copy-start.8 = (f32[512,128]{1,0:T(8,128)S(1)}, f32[512,128]{1,0:T(8,128)}, u32[]{:S(2)}) copy-start(f32[512,128]{1,0:T(8,128)} %get-tuple-element.42) | copy-start | bytes 786436
  7.9 58.1 %copy-start.7 = (s32[64]{0:T(128)S(1)}, s32[64]{0:T(128)}, u32[]{:S(2)}) copy-start(s32[64]{0:T(128)} %sources.1) | copy-start | bytes 772
  7.9 12.2 %collective-permute-start.17 = (f32[512,128]{1,0:T(8,128)}, f32[512,128]{1,0:T(8,128)S(1)}, u32[]{:S(2)}, u32[]{:S(2)}) collective-permute-start(f32[512,128]{1,0:T(8,128)} %get-tuple-element.57), channel_id=1, source_target_pairs={{0,3},{1,2},{2,1},{3,0},{4,7},{5,6},{6,5},{7,4},{8,11},{9,10},{10,... | collective-permute-start | bytes 786440 | tf_op jit(solution)/shard_map/ppermute | solution.py:251
  11.9 55.3 %copy-start.2 = (f32[512,128]{1,0:T(8,128)S(1)}, f32[512,128]{1,0:T(8,128)}, u32[]{:S(2)}) copy-start(f32[512,128]{1,0:T(8,128)} %get-tuple-element.55.refs_2_) | copy-start | bytes 786436
  12.0 55.3 %copy-start.3 = (f32[512,128]{1,0:T(8,128)S(1)}, f32[512,128]{1,0:T(8,128)}, u32[]{:S(2)}) copy-start(f32[512,128]{1,0:T(8,128)} %get-tuple-element.58.refs_8_) | copy-start | bytes 786436
  12.0 9.7 %collective-permute-start.15 = (f32[512,128]{1,0:T(8,128)}, f32[512,128]{1,0:T(8,128)S(1)}, u32[]{:S(2)}, u32[]{:S(2)}) collective-permute-start(f32[512,128]{1,0:T(8,128)} %get-tuple-element.56), channel_id=1, source_target_pairs={{0,1},{1,0},{2,3},{3,2},{4,5},{5,4},{6,7},{7,6},{8,9},{9,8},{10,11... | collective-permute-start | bytes 786440 | tf_op jit(solution)/shard_map/ppermute | solution.py:251
  12.2 5.7 %collective-permute-start = (f32[128,128]{1,0:T(8,128)S(1)}, f32[128,128]{1,0:T(8,128)S(1)}, u32[]{:S(2)}, u32[]{:S(2)}) collective-permute-start(f32[128,128]{1,0:T(8,128)S(1)} %bitcast.21), channel_id=1, source_target_pairs={{0,4},{4,8},{8,12},{12,16},{16,20},{20,24},{24,28},{1,5},{5,9},{9,... | collective-permute-start | bytes 196616 | tf_op jit(solution)/shard_map/ppermute | solution.py:272
  16.1 3.4 %collective-permute-start.9 = (f32[128,128]{1,0:T(8,128)}, f32[128,128]{1,0:T(8,128)S(1)}, u32[]{:S(2)}, u32[]{:S(2)}) collective-permute-start(f32[128,128]{1,0:T(8,128)} %get-tuple-element.48), channel_id=1, source_target_pairs={{0,1},{1,0},{2,3},{3,2},{4,5},{5,4},{6,7},{7,6},{8,9},{9,8},{10,11... | collective-permute-start | bytes 196616 | tf_op jit(solution)/shard_map/ppermute | solution.py:251
  17.9 17.2 %collective-permute-start.2 = (f32[512,128]{1,0:T(8,128)S(1)}, f32[512,128]{1,0:T(8,128)S(1)}, u32[]{:S(2)}, u32[]{:S(2)}) collective-permute-start(f32[512,128]{1,0:T(8,128)S(1)} %copy-done.9), channel_id=1, source_target_pairs={{0,2},{1,3},{2,0},{3,1},{4,6},{5,7},{6,4},{7,5},{8,10},{9,11},{10,... | collective-permute-start | bytes 786440 | tf_op jit(solution)/shard_map/ppermute | solution.py:251
  19.5 17.2 %collective-permute-start.3 = (f32[512,128]{1,0:T(8,128)S(1)}, f32[512,128]{1,0:T(8,128)S(1)}, u32[]{:S(2)}, u32[]{:S(2)}) collective-permute-start(f32[512,128]{1,0:T(8,128)S(1)} %copy-done.8), channel_id=1, source_target_pairs={{0,3},{1,2},{2,1},{3,0},{4,7},{5,6},{6,5},{7,4},{8,11},{9,10},{10,... | collective-permute-start | bytes 786440 | tf_op jit(solution)/shard_map/ppermute | solution.py:251
  19.5 3.2 %collective-permute-start.12 = (f32[256,128]{1,0:T(8,128)}, f32[256,128]{1,0:T(8,128)S(1)}, u32[]{:S(2)}, u32[]{:S(2)}) collective-permute-start(f32[256,128]{1,0:T(8,128)} %get-tuple-element.52), channel_id=1, source_target_pairs={{0,1},{1,0},{2,3},{3,2},{4,5},{5,4},{6,7},{7,6},{8,9},{9,8},{10,11... | collective-permute-start | bytes 393224 | tf_op jit(solution)/shard_map/ppermute | solution.py:251
  20.1 15.1 %collective-permute-start.13 = (f32[256,128]{1,0:T(8,128)}, f32[256,128]{1,0:T(8,128)S(1)}, u32[]{:S(2)}, u32[]{:S(2)}) collective-permute-start(f32[256,128]{1,0:T(8,128)} %get-tuple-element.53), channel_id=1, source_target_pairs={{0,2},{1,3},{2,0},{3,1},{4,6},{5,7},{6,4},{7,5},{8,10},{9,11},{10,... | collective-permute-start | bytes 393224 | tf_op jit(solution)/shard_map/ppermute | solution.py:251
  21.6 15.4 %collective-permute-start.1 = (f32[512,128]{1,0:T(8,128)}, f32[512,128]{1,0:T(8,128)S(1)}, u32[]{:S(2)}, u32[]{:S(2)}) collective-permute-start(f32[512,128]{1,0:T(8,128)} %get-tuple-element.40), channel_id=1, source_target_pairs={{0,1},{1,0},{2,3},{3,2},{4,5},{5,4},{6,7},{7,6},{8,9},{9,8},{10,11... | collective-permute-start | bytes 786440 | tf_op jit(solution)/shard_map/ppermute | solution.py:251
  21.6 48.0 %copy-start = (f32[512,128]{1,0:T(8,128)S(1)}, f32[512,128]{1,0:T(8,128)}, u32[]{:S(2)}) copy-start(f32[512,128]{1,0:T(8,128)} %get-tuple-element.39.refs_2_) | copy-start | bytes 786436
  21.6 48.0 %copy-start.4 = (f32[256,128]{1,0:T(8,128)S(1)}, f32[256,128]{1,0:T(8,128)}, u32[]{:S(2)}) copy-start(f32[256,128]{1,0:T(8,128)} %get-tuple-element.51.refs_8_) | copy-start | bytes 393220
  22.7 16.6 %collective-permute-start.14 = (f32[256,128]{1,0:T(8,128)}, f32[256,128]{1,0:T(8,128)S(1)}, u32[]{:S(2)}, u32[]{:S(2)}) collective-permute-start(f32[256,128]{1,0:T(8,128)} %get-tuple-element.54), channel_id=1, source_target_pairs={{0,3},{1,2},{2,1},{3,0},{4,7},{5,6},{6,5},{7,4},{8,11},{9,10},{10,... | collective-permute-start | bytes 393224 | tf_op jit(solution)/shard_map/ppermute | solution.py:251
  35.2 8.8 %collective-permute-start.20 = (f32[512,128]{1,0:T(8,128)}, f32[512,128]{1,0:T(8,128)S(1)}, u32[]{:S(2)}, u32[]{:S(2)}) collective-permute-start(f32[512,128]{1,0:T(8,128)} %get-tuple-element.59), channel_id=1, source_target_pairs={{0,1},{1,0},{2,3},{3,2},{4,5},{5,4},{6,7},{7,6},{8,9},{9,8},{10,11... | collective-permute-start | bytes 786440 | tf_op jit(solution)/shard_map/ppermute | solution.py:251
  35.2 10.1 %collective-permute-start.21 = (f32[512,128]{1,0:T(8,128)}, f32[512,128]{1,0:T(8,128)S(1)}, u32[]{:S(2)}, u32[]{:S(2)}) collective-permute-start(f32[512,128]{1,0:T(8,128)} %get-tuple-element.60), channel_id=1, source_target_pairs={{0,2},{1,3},{2,0},{3,1},{4,6},{5,7},{6,4},{7,5},{8,10},{9,11},{10,... | collective-permute-start | bytes 786440 | tf_op jit(solution)/shard_map/ppermute | solution.py:251
  36.7 14.1 %collective-permute-start.22 = (f32[512,128]{1,0:T(8,128)}, f32[512,128]{1,0:T(8,128)S(1)}, u32[]{:S(2)}, u32[]{:S(2)}) collective-permute-start(f32[512,128]{1,0:T(8,128)} %get-tuple-element.61), channel_id=1, source_target_pairs={{0,3},{1,2},{2,1},{3,0},{4,7},{5,6},{6,5},{7,4},{8,11},{9,10},{10,... | collective-permute-start | bytes 786440 | tf_op jit(solution)/shard_map/ppermute | solution.py:251
  37.0 15.3 %collective-permute-start.19 = (f32[512,128]{1,0:T(8,128)S(1)}, f32[512,128]{1,0:T(8,128)S(1)}, u32[]{:S(2)}, u32[]{:S(2)}) collective-permute-start(f32[512,128]{1,0:T(8,128)S(1)} %get-tuple-element.72), channel_id=1, source_target_pairs={{4,0},{8,4},{12,8},{16,12},{20,16},{24,20},{28,24},{5,1},{9,5},{13... | collective-permute-start | bytes 786440 | tf_op jit(solution)/shard_map/ppermute | solution.py:290
  39.3 19.8 %collective-permute-start.18 = (f32[512,128]{1,0:T(8,128)S(1)}, f32[512,128]{1,0:T(8,128)S(1)}, u32[]{:S(2)}, u32[]{:S(2)}) collective-permute-start(f32[512,128]{1,0:T(8,128)S(1)} %get-tuple-element.73), channel_id=1, source_target_pairs={{0,4},{4,8},{8,12},{12,16},{16,20},{20,24},{24,28},{1,5},{5,9},{9,... | collective-permute-start | bytes 786440 | tf_op jit(solution)/shard_map/ppermute | solution.py:291
  44.0 15.2 %collective-permute-start.5 = (f32[512,128]{1,0:T(8,128)S(1)}, f32[512,128]{1,0:T(8,128)S(1)}, u32[]{:S(2)}, u32[]{:S(2)}) collective-permute-start(f32[512,128]{1,0:T(8,128)S(1)} %get-tuple-element.74), channel_id=1, source_target_pairs={{4,0},{8,4},{12,8},{16,12},{20,16},{24,20},{28,24},{5,1},{9,5},{13... | collective-permute-start | bytes 786440 | tf_op jit(solution)/shard_map/ppermute | solution.py:290
  45.3 19.5 %collective-permute-start.4 = (f32[512,128]{1,0:T(8,128)S(1)}, f32[512,128]{1,0:T(8,128)S(1)}, u32[]{:S(2)}, u32[]{:S(2)}) collective-permute-start(f32[512,128]{1,0:T(8,128)S(1)} %get-tuple-element.75), channel_id=1, source_target_pairs={{0,4},{4,8},{8,12},{12,16},{16,20},{20,24},{24,28},{1,5},{5,9},{9,... | collective-permute-start | bytes 786440 | tf_op jit(solution)/shard_map/ppermute | solution.py:291
  50.8 20.1 %collective-permute-start.10 = (f32[128,128]{1,0:T(8,128)}, f32[128,128]{1,0:T(8,128)S(1)}, u32[]{:S(2)}, u32[]{:S(2)}) collective-permute-start(f32[128,128]{1,0:T(8,128)} %get-tuple-element.49), channel_id=1, source_target_pairs={{0,2},{1,3},{2,0},{3,1},{4,6},{5,7},{6,4},{7,5},{8,10},{9,11},{10,... | collective-permute-start | bytes 196616 | tf_op jit(solution)/shard_map/ppermute | solution.py:251
  52.3 18.5 %collective-permute-start.11 = (f32[128,128]{1,0:T(8,128)}, f32[128,128]{1,0:T(8,128)S(1)}, u32[]{:S(2)}, u32[]{:S(2)}) collective-permute-start(f32[128,128]{1,0:T(8,128)} %get-tuple-element.50), channel_id=1, source_target_pairs={{0,3},{1,2},{2,1},{3,0},{4,7},{5,6},{6,5},{7,4},{8,11},{9,10},{10,... | collective-permute-start | bytes 196616 | tf_op jit(solution)/shard_map/ppermute | solution.py:251
  59.2 12.3 %collective-permute-start.6 = (f32[128,128]{1,0:T(8,128)}, f32[128,128]{1,0:T(8,128)S(1)}, u32[]{:S(2)}, u32[]{:S(2)}) collective-permute-start(f32[128,128]{1,0:T(8,128)} %get-tuple-element.44), channel_id=1, source_target_pairs={{0,1},{1,0},{2,3},{3,2},{4,5},{5,4},{6,7},{7,6},{8,9},{9,8},{10,11... | collective-permute-start | bytes 196616 | tf_op jit(solution)/shard_map/ppermute | solution.py:251
  59.2 12.3 %collective-permute-start.7 = (f32[128,128]{1,0:T(8,128)}, f32[128,128]{1,0:T(8,128)S(1)}, u32[]{:S(2)}, u32[]{:S(2)}) collective-permute-start(f32[128,128]{1,0:T(8,128)} %get-tuple-element.45), channel_id=1, source_target_pairs={{0,2},{1,3},{2,0},{3,1},{4,6},{5,7},{6,4},{7,5},{8,10},{9,11},{10,... | collective-permute-start | bytes 196616 | tf_op jit(solution)/shard_map/ppermute | solution.py:251
  64.8 6.7 %collective-permute-start.8 = (f32[128,128]{1,0:T(8,128)}, f32[128,128]{1,0:T(8,128)S(1)}, u32[]{:S(2)}, u32[]{:S(2)}) collective-permute-start(f32[128,128]{1,0:T(8,128)} %get-tuple-element.46), channel_id=1, source_target_pairs={{0,3},{1,2},{2,1},{3,0},{4,7},{5,6},{6,5},{7,4},{8,11},{9,10},{10,... | collective-permute-start | bytes 196616 | tf_op jit(solution)/shard_map/ppermute | solution.py:251
  67.2 3.6 %copy-start.6 = (f32[128,128]{1,0:T(8,128)S(1)}, f32[128,128]{1,0:T(8,128)}, u32[]{:S(2)}) copy-start(f32[128,128]{1,0:T(8,128)} %get-tuple-element.47.refs_8_) | copy-start | bytes 196612
  69.6 1.9 %copy-start.5 = (f32[128,128]{1,0:T(8,128)S(1)}, f32[128,128]{1,0:T(8,128)}, u32[]{:S(2)}) copy-start(f32[128,128]{1,0:T(8,128)} %get-tuple-element.43.refs_8_) | copy-start | bytes 196612
  72.2 4.1 %collective-permute-start.23 = (f32[8,128]{1,0:T(8,128)S(1)}, f32[8,128]{1,0:T(8,128)S(1)}, u32[]{:S(2)}, u32[]{:S(2)}) collective-permute-start(f32[8,128]{1,0:T(8,128)S(1)} %get-tuple-element.65), channel_id=1, source_target_pairs={{0,4},{4,0},{8,12},{12,8},{16,20},{20,16},{24,28},{28,24},{1,5},{5... | collective-permute-start | bytes 12296 | tf_op jit(solution)/shard_map/ppermute | solution.py:331
  76.3 4.0 %collective-permute-start.24 = (f32[8,128]{1,0:T(8,128)S(1)}, f32[8,128]{1,0:T(8,128)S(1)}, u32[]{:S(2)}, u32[]{:S(2)}) collective-permute-start(f32[8,128]{1,0:T(8,128)S(1)} %add.6), channel_id=1, source_target_pairs={{0,8},{4,12},{8,0},{12,4},{16,24},{20,28},{24,16},{28,20},{1,9},{5... | collective-permute-start | bytes 12296 | tf_op jit(solution)/shard_map/ppermute | solution.py:331
  80.3 4.6 %collective-permute-start.25 = (f32[8,128]{1,0:T(8,128)S(1)}, f32[8,128]{1,0:T(8,128)S(1)}, u32[]{:S(2)}, u32[]{:S(2)}) collective-permute-start(f32[8,128]{1,0:T(8,128)S(1)} %add.7.refs_0_), channel_id=1, source_target_pairs={{0,16},{4,20},{8,24},{12,28},{16,0},{20,4},{24,8},{28,12},{1,17},{... | collective-permute-start | bytes 12296 | tf_op jit(solution)/shard_map/ppermute | solution.py:331

commit v7 on v6

--- a/solution.py
+++ b/solution.py
@@ -183,7 +183,7 @@
         total_of[pl.ds(lo + i, 1), :] = jnp.sum(total, axis=0, keepdims=True)
         return 0
 
-    lax.fori_loop(0, n, source_step, 0, unroll=math.gcd(n, 2))
+    lax.fori_loop(0, n, source_step, 0, unroll=max(u for u in (1, 2, 3, 4) if n % u == 0))
     if last:
         whole = jnp.sum(total_of[...], axis=1, keepdims=True)
         lane = lax.broadcasted_iota(jnp.int32, (group, LANES), 1)
@@ -243,7 +243,7 @@
     outer_rows = (0, own_rows - 1)
     order = [k for k in range(1, senders) if k >= 2] + [1]
     halves = [(0, group // 2), (group // 2, group - group // 2)]
-    cuts = (0, group // 2, group - group // 4, group - group // 8, group)
+    cuts = (0, group // 2, group - group // 8, group)
     chunks = [(lo, hi - lo) for lo, hi in zip(cuts[:-1], cuts[1:], strict=True) if hi > lo]
     common = (group, cb, own_rows, senders)
 
@@ -313,7 +313,7 @@
             functools.partial(defect_kernel, meta, lo, n, group, amplitude),
             out_shape=(
                 jax.ShapeDtypeStruct((n * per, LANES), jnp.float32),
-                jax.ShapeDtypeStruct((peers if lo + n == group else group, LANES), jnp.float32),
+                jax.ShapeDtypeStruct((SUB if lo + n == group else group, LANES), jnp.float32),
             ),
             in_specs=[vmem, vmem] + [vmem] * len(ins) + ([vmem] if lo else []),
             out_specs=(vmem, vmem),

time: 87.6 us -> 87.5 us (level)
  starting transfers between devices: 38.3 us -> 36.3 us
  waiting for transfers between devices: 29.2 us -> 30.9 us
    ppermute x18 -> x15, waiting for transfers between devices: 11.8 us -> 16.3 us  [send(): lax.ppermute(piece, 'src', [(i, i ^ k) for i in range(senders)])]
    ppermute x2, waiting for transfers between devices: 10.9 us -> 7.93 us  [program(): below.append(lax.ppermute(last, 'vtx', up))]
    ppermute x18 -> x15, starting transfers between devices: 13.9 us -> 11.6 us  [send(): lax.ppermute(piece, 'src', [(i, i ^ k) for i in range(senders)])]
    pallas_call x4 -> x3, Pallas kernels: 4.84 us -> 4.96 us  [program(): pl.pallas_call(functools.partial(defect_kernel, meta, lo, n, group, ampli...]
  transfers between devices with their start and end apart: 26 -> 23, of which waited for: 7 -> 8; matrix products, arithmetic and copies ran while one was open for 2% -> 2% of each run, Pallas kernels for 13% -> 14%
where the time goes in v7:
time: 87.5 us; the launch traced here: 87.1 us
  starting transfers between devices  36.3 us (41%)
  waiting for transfers between devices  30.9 us (35%)
  Pallas kernels  16.7 us (19%)
  other arithmetic  2.12 us (2%)
  between operations  0.95 us (1%)
    ppermute x15, waiting for transfers between devices, send(): lax.ppermute(piece, 'src', [(i, i ^ k) for i in range(senders)])  16.3 us
    ppermute x15, starting transfers between devices, send(): lax.ppermute(piece, 'src', [(i, i ^ k) for i in range(senders)])  11.6 us
    ppermute x2, starting transfers between devices, program(): below.append(lax.ppermute(last, 'vtx', up))  10.5 us
    pallas_call x3, Pallas kernels, pack(): pl.pallas_call(functools.partial(pack_kernel, (tuple(plan), group, cb, ow...  8.18 us
    ppermute x3, starting transfers between devices, program(): other = lax.ppermute(sums, 'vtx', [(i, i ^ step) for i in range(peers)])  8.11 us
    ppermute x2, waiting for transfers between devices, program(): below.append(lax.ppermute(last, 'vtx', up))  7.93 us
    pallas_call x3, Pallas kernels, program(): pl.pallas_call(functools.partial(defect_kernel, meta, lo, n, group, ampli...  4.96 us
    ppermute x3, waiting for transfers between devices, program(): other = lax.ppermute(sums, 'vtx', [(i, i ^ step) for i in range(peers)])  4.75 us
  transfers between devices with their start and end apart: 23, of which 8 were waited for; matrix products, arithmetic and copies ran while one was open for 2% of the time, Pallas kernels for 14%

profile of v7, /device:TPU:0, one launch (start us, length us, event | category | flops | bytes accessed | tf_op | source)
XLA Modules:
  0.0 87.1 jit_solution(9605191559225713848)
XLA Ops:
  0.6 1.8 %shard_map.52 = f32[512,128]{1,0:T(8,128)} custom-call(f32[8192,128]{1,0:T(8,128)} %bitcast.18), custom_call_target="tpu_custom_call" | custom-call | flops 65536 | bytes 786432 | tf_op jit(solution)/shard_map/pallas_call | solution.py:60
  2.4 3.1 %collective-permute-start.13 = (f32[512,128]{1,0:T(8,128)}, f32[512,128]{1,0:T(8,128)S(1)}, u32[]{:S(2)}, u32[]{:S(2)}) collective-permute-start(f32[512,128]{1,0:T(8,128)} %shard_map.52), channel_id=1, source_target_pairs={{0,2},{1,3},{2,0},{3,1},{4,6},{5,7},{6,4},{7,5},{8,10},{9,11},{10,... | collective-permute-start | bytes 786440 | tf_op jit(solution)/shard_map/ppermute | solution.py:251
  5.5 2.3 %shard_map.51 = (f32[512,128]{1,0:T(8,128)}, f32[512,128]{1,0:T(8,128)}, f32[512,128]{1,0:T(8,128)}) custom-call(f32[8192,128]{1,0:T(8,128)} %bitcast.19), custom_call_target="tpu_custom_call" | custom-call | flops 196608 | bytes 2359296 | tf_op jit(solution)/shard_map/pallas_call | solution.py:60
  7.8 0.0 copy-start.1
  7.8 0.0 copy-start.7
  7.8 0.1 collective-permute-start.14
  7.9 4.1 %shard_map.50 = (f32[512,128]{1,0:T(8,128)}, f32[512,128]{1,0:T(8,128)}, f32[512,128]{1,0:T(8,128)}, f32[512,128]{1,0:T(8,128)}, f32[512,128]{1,0:T(8,128)}, /*i...) custom-call(f32[8192,128]{1,0:T(8,128)} %bitcast.20), custom_call_target="tpu_custom_call" | custom-call | flops 786432 | bytes 7340032 | tf_op jit(solution)/shard_map/pallas_call | solution.py:60
  12.0 0.0 copy-start.10
  12.0 0.0 copy-start.6
  12.0 0.1 collective-permute-start.12
  12.1 0.5 collective-permute-start.9
  12.6 0.1 slice.3
  12.7 3.5 %collective-permute-start = (f32[128,128]{1,0:T(8,128)S(1)}, f32[128,128]{1,0:T(8,128)S(1)}, u32[]{:S(2)}, u32[]{:S(2)}) collective-permute-start(f32[128,128]{1,0:T(8,128)S(1)} %bitcast.21), channel_id=1, source_target_pairs={{0,4},{4,8},{8,12},{12,16},{16,20},{20,24},{24,28},{1,5},{5,9},{9,... | collective-permute-start | bytes 196616 | tf_op jit(solution)/shard_map/ppermute | solution.py:272
  16.2 1.9 %collective-permute-done.lower = f32[128,128]{1,0:T(8,128)S(1)} collective-permute-done((f32[128,128]{1,0:T(8,128)S(1)}, f32[128,128]{1,0:T(8,128)S(1)}, u32[]{:S(2)}, u32[]{:S(2)}) %collective-permute-start) | collective-permute-done | bytes 65568 | tf_op jit(solution)/shard_map/ppermute | solution.py:272
  18.1 1.5 %collective-permute-start.2 = (f32[512,128]{1,0:T(8,128)}, f32[512,128]{1,0:T(8,128)S(1)}, u32[]{:S(2)}, u32[]{:S(2)}) collective-permute-start(f32[512,128]{1,0:T(8,128)} %get-tuple-element.35), channel_id=1, source_target_pairs={{0,2},{1,3},{2,0},{3,1},{4,6},{5,7},{6,4},{7,5},{8,10},{9,11},{10,... | collective-permute-start | bytes 786440 | tf_op jit(solution)/shard_map/ppermute | solution.py:251
  19.6 0.0 collective-permute-done.9.refs_9_
  19.6 0.0 collective-permute-start.3
  19.6 0.0 collective-permute-done.13.refs_4_
  19.6 0.9 %collective-permute-start.10 = (f32[384,128]{1,0:T(8,128)}, f32[384,128]{1,0:T(8,128)S(1)}, u32[]{:S(2)}, u32[]{:S(2)}) collective-permute-start(f32[384,128]{1,0:T(8,128)} %get-tuple-element.43), channel_id=1, source_target_pairs={{0,2},{1,3},{2,0},{3,1},{4,6},{5,7},{6,4},{7,5},{8,10},{9,11},{10,... | collective-permute-start | bytes 589832 | tf_op jit(solution)/shard_map/ppermute | solution.py:251
  20.5 0.0 collective-permute-done.14.refs_5_
  20.5 1.1 %collective-permute-start.11 = (f32[384,128]{1,0:T(8,128)}, f32[384,128]{1,0:T(8,128)S(1)}, u32[]{:S(2)}, u32[]{:S(2)}) collective-permute-start(f32[384,128]{1,0:T(8,128)} %get-tuple-element.44), channel_id=1, source_target_pairs={{0,3},{1,2},{2,1},{3,0},{4,7},{5,6},{6,5},{7,4},{8,11},{9,10},{10,... | collective-permute-start | bytes 589832 | tf_op jit(solution)/shard_map/ppermute | solution.py:251
  21.6 0.0 collective-permute-done.12.refs_3_
  21.6 0.2 collective-permute-start.1
  21.8 1.1 %select_select_fusion = (f32[512,128]{1,0:T(8,128)S(1)}, f32[512,128]{1,0:T(8,128)S(1)}) fusion(f32[512,128]{1,0:T(8,128)S(1)} %collective-permute-done.13.refs_4_, f32[512,128]{1,0:T(8,128)S(1)} %collective-permute-done.14.refs_5_, f32[512,128]{1,0:T(8,128)} %get-tuple-element.45.refs_2_, f32[512,128]{1,0:T(8,128)S(1)} %collective-permute-done.12.refs_3_, ...), kind=kLoop, calls=%fused_computation | loop fusion | flops 393216 | bytes 1572867 | tf_op jit(solution)/shard_map/select_n | solution.py:288
  22.9 14.4 %collective-permute-done.10.refs_10_ = f32[384,128]{1,0:T(8,128)S(1)} collective-permute-done((f32[384,128]{1,0:T(8,128)}, f32[384,128]{1,0:T(8,128)S(1)}, u32[]{:S(2)}, u32[]{:S(2)}) %collective-permute-start.10) | collective-permute-done | bytes 196640 | tf_op jit(solution)/shard_map/ppermute | solution.py:251
  37.3 0.0 collective-permute-start.17
  37.3 1.9 %collective-permute-done.11.refs_11_ = f32[384,128]{1,0:T(8,128)S(1)} collective-permute-done((f32[384,128]{1,0:T(8,128)}, f32[384,128]{1,0:T(8,128)S(1)}, u32[]{:S(2)}, u32[]{:S(2)}) %collective-permute-start.11) | collective-permute-done | bytes 196640 | tf_op jit(solution)/shard_map/ppermute | solution.py:251
  39.2 0.9 %collective-permute-start.18 = (f32[512,128]{1,0:T(8,128)}, f32[512,128]{1,0:T(8,128)S(1)}, u32[]{:S(2)}, u32[]{:S(2)}) collective-permute-start(f32[512,128]{1,0:T(8,128)} %get-tuple-element.50), channel_id=1, source_target_pairs={{0,2},{1,3},{2,0},{3,1},{4,6},{5,7},{6,4},{7,5},{8,10},{9,11},{10,... | collective-permute-start | bytes 786440 | tf_op jit(solution)/shard_map/ppermute | solution.py:251
  40.2 0.0 collective-permute-done.2.refs_4_
  40.2 1.1 %collective-permute-start.19 = (f32[512,128]{1,0:T(8,128)}, f32[512,128]{1,0:T(8,128)S(1)}, u32[]{:S(2)}, u32[]{:S(2)}) collective-permute-start(f32[512,128]{1,0:T(8,128)} %get-tuple-element.51), channel_id=1, source_target_pairs={{0,3},{1,2},{2,1},{3,0},{4,7},{5,6},{6,5},{7,4},{8,11},{9,10},{10,... | collective-permute-start | bytes 786440 | tf_op jit(solution)/shard_map/ppermute | solution.py:251
  41.3 0.0 collective-permute-done.3.refs_5_
  41.3 1.3 %collective-permute-start.16 = (f32[512,128]{1,0:T(8,128)S(1)}, f32[512,128]{1,0:T(8,128)S(1)}, u32[]{:S(2)}, u32[]{:S(2)}) collective-permute-start(f32[512,128]{1,0:T(8,128)S(1)} %get-tuple-element.60), channel_id=1, source_target_pairs={{4,0},{8,4},{12,8},{16,12},{20,16},{24,20},{28,24},{5,1},{9,5},{13... | collective-permute-start | bytes 786440 | tf_op jit(solution)/shard_map/ppermute | solution.py:290
  42.6 0.0 collective-permute-done.1.refs_3_
  42.6 5.1 %collective-permute-start.15 = (f32[512,128]{1,0:T(8,128)S(1)}, f32[512,128]{1,0:T(8,128)S(1)}, u32[]{:S(2)}, u32[]{:S(2)}) collective-permute-start(f32[512,128]{1,0:T(8,128)S(1)} %get-tuple-element.61), channel_id=1, source_target_pairs={{0,4},{4,8},{8,12},{12,16},{16,20},{20,24},{24,28},{1,5},{5,9},{9,... | collective-permute-start | bytes 786440 | tf_op jit(solution)/shard_map/ppermute | solution.py:291
  47.6 1.0 %select_select_fusion.2 = (f32[512,128]{1,0:T(8,128)S(1)}, f32[512,128]{1,0:T(8,128)S(1)}) fusion(f32[512,128]{1,0:T(8,128)S(1)} %collective-permute-done.2.refs_4_, f32[512,128]{1,0:T(8,128)S(1)} %collective-permute-done.3.refs_5_, f32[512,128]{1,0:T(8,128)} %get-tuple-element.33.refs_2_, f32[512,128]{1,0:T(8,128)S(1)} %collective-permute-done.1.refs_3_, ...), kind=kLoop, calls=%fused_computation.2 | loop fusion | flops 393216 | bytes 1572867 | tf_op jit(solution)/shard_map/select_n | solution.py:288
  48.7 0.0 collective-permute-done.17.refs_9_
  48.7 1.3 %collective-permute-start.5 = (f32[512,128]{1,0:T(8,128)S(1)}, f32[512,128]{1,0:T(8,128)S(1)}, u32[]{:S(2)}, u32[]{:S(2)}) collective-permute-start(f32[512,128]{1,0:T(8,128)S(1)} %get-tuple-element.62), channel_id=1, source_target_pairs={{4,0},{8,4},{12,8},{16,12},{20,16},{24,20},{28,24},{5,1},{9,5},{13... | collective-permute-start | bytes 786440 | tf_op jit(solution)/shard_map/ppermute | solution.py:290
  50.0 0.0 collective-permute-done.18.refs_10_
  50.0 5.4 %collective-permute-start.4 = (f32[512,128]{1,0:T(8,128)S(1)}, f32[512,128]{1,0:T(8,128)S(1)}, u32[]{:S(2)}, u32[]{:S(2)}) collective-permute-start(f32[512,128]{1,0:T(8,128)S(1)} %get-tuple-element.63), channel_id=1, source_target_pairs={{0,4},{4,8},{8,12},{12,16},{16,20},{20,24},{24,28},{1,5},{5,9},{9,... | collective-permute-start | bytes 786440 | tf_op jit(solution)/shard_map/ppermute | solution.py:291
  55.5 0.0 collective-permute-done.19.refs_11_
  55.5 0.1 collective-permute-start.6
  55.5 0.0 collective-permute-done.16.refs_7_
  55.6 0.0 copy-done.9
  55.6 1.6 %collective-permute-start.7 = (f32[128,128]{1,0:T(8,128)S(1)}, f32[128,128]{1,0:T(8,128)S(1)}, u32[]{:S(2)}, u32[]{:S(2)}) collective-permute-start(f32[128,128]{1,0:T(8,128)S(1)} %copy-done.9), channel_id=1, source_target_pairs={{0,2},{1,3},{2,0},{3,1},{4,6},{5,7},{6,4},{7,5},{8,10},{9,11},{10,... | collective-permute-start | bytes 196616 | tf_op jit(solution)/shard_map/ppermute | solution.py:251
  57.2 6.6 %collective-permute-done.15.refs_6_ = f32[512,128]{1,0:T(8,128)S(1)} collective-permute-done((f32[512,128]{1,0:T(8,128)S(1)}, f32[512,128]{1,0:T(8,128)S(1)}, u32[]{:S(2)}, u32[]{:S(2)}) %collective-permute-start.15) | collective-permute-done | bytes 262176 | tf_op jit(solution)/shard_map/ppermute | solution.py:291
  63.7 0.0 copy-done.8
  63.7 0.5 collective-permute-start.8
  64.2 1.3 %weights.1 = (f32[7,8,72,128]{3,2,1,0:T(8,128)S(1)}, s32[16,128]{1,0:T(8,128)S(1)}) custom-call(s32[64]{0:T(128)S(1)} %copy-done.6, f32[2048,128]{1,0:T(8,128)S(1)} %bitcast.17, f32[128,128]{1,0:T(8,128)S(1)} %collective-permute-done.lower), custom_call_target="tpu_custom_call" | custom-call | flops 1310720 | bytes 2883584 | tf_op jit(solution)/shard_map/weights/pallas_call | solution.py:274
  65.6 2.3 %defect.3 = (f32[4096,128]{1,0:T(8,128)S(1)}, f32[16,128]{1,0:T(8,128)S(1)}) custom-call(s32[16,128]{1,0:T(8,128)S(1)} %get-tuple-element.31.refs_0_, f32[7,8,72,128]{3,2,1,0:T(8,128)S(1)} %get-tuple-element.32.refs_1_, f32[512,128]{1,0:T(8,128)S(1)} %copy-done.2, f32[512,128]{1,0:T(8,128)S(1)} %collective-permute-done.12.refs_3_, ...), custom_call_target="tpu_custom_call" | custom-call | flops 10485760 | bytes 4194304 | tf_op jit(solution)/shard_map/defect/pallas_call | solution.py:312
  67.9 0.0 collective-permute-done.5.refs_7_
  67.9 1.4 %collective-permute-done.4.refs_6_ = f32[512,128]{1,0:T(8,128)S(1)} collective-permute-done((f32[512,128]{1,0:T(8,128)S(1)}, f32[512,128]{1,0:T(8,128)S(1)}, u32[]{:S(2)}, u32[]{:S(2)}) %collective-permute-start.4) | collective-permute-done | bytes 262176 | tf_op jit(solution)/shard_map/ppermute | solution.py:291
  69.3 0.0 copy-done.4
  69.3 1.8 %defect.4 = (f32[3072,128]{1,0:T(8,128)S(1)}, f32[16,128]{1,0:T(8,128)S(1)}) custom-call(s32[16,128]{1,0:T(8,128)S(1)} %get-tuple-element.31.refs_0_, f32[7,8,72,128]{3,2,1,0:T(8,128)S(1)} %get-tuple-element.32.refs_1_, f32[512,128]{1,0:T(8,128)S(1)} %copy-done, f32[512,128]{1,0:T(8,128)S(1)} %collective-permute-done.1.refs_3_, ...), custom_call_target="tpu_custom_call" | custom-call | flops 7864320 | bytes 3145728 | tf_op jit(solution)/shard_map/defect/pallas_call | solution.py:312
  71.1 0.0 collective-permute-done.6.refs_9_
  71.1 0.0 collective-permute-done.7.refs_10_
  71.1 0.0 collective-permute-done.8.refs_11_
  71.1 0.8 defect.5
  72.0 2.5 %collective-permute-start.20 = (f32[8,128]{1,0:T(8,128)S(1)}, f32[8,128]{1,0:T(8,128)S(1)}, u32[]{:S(2)}, u32[]{:S(2)}) collective-permute-start(f32[8,128]{1,0:T(8,128)S(1)} %get-tuple-element.54), channel_id=1, source_target_pairs={{0,4},{4,0},{8,12},{12,8},{16,20},{20,16},{24,28},{28,24},{1,5},{5... | collective-permute-start | bytes 12296 | tf_op jit(solution)/shard_map/ppermute | solution.py:331
  74.5 1.6 %collective-permute-done.20 = f32[8,128]{1,0:T(8,128)S(1)} collective-permute-done((f32[8,128]{1,0:T(8,128)S(1)}, f32[8,128]{1,0:T(8,128)S(1)}, u32[]{:S(2)}, u32[]{:S(2)}) %collective-permute-start.20) | collective-permute-done | bytes 4128 | tf_op jit(solution)/shard_map/ppermute | solution.py:331
  76.0 2.6 %collective-permute-start.21 = (f32[8,128]{1,0:T(8,128)S(1)}, f32[8,128]{1,0:T(8,128)S(1)}, u32[]{:S(2)}, u32[]{:S(2)}) collective-permute-start(f32[8,128]{1,0:T(8,128)S(1)} %add.6), channel_id=1, source_target_pairs={{0,8},{4,12},{8,0},{12,4},{16,24},{20,28},{24,16},{28,20},{1,9},{5... | collective-permute-start | bytes 12296 | tf_op jit(solution)/shard_map/ppermute | solution.py:331
  78.6 1.6 %collective-permute-done.21 = f32[8,128]{1,0:T(8,128)S(1)} collective-permute-done((f32[8,128]{1,0:T(8,128)S(1)}, f32[8,128]{1,0:T(8,128)S(1)}, u32[]{:S(2)}, u32[]{:S(2)}) %collective-permute-start.21) | collective-permute-done | bytes 4128 | tf_op jit(solution)/shard_map/ppermute | solution.py:331
  80.2 3.0 %collective-permute-start.22 = (f32[8,128]{1,0:T(8,128)S(1)}, f32[8,128]{1,0:T(8,128)S(1)}, u32[]{:S(2)}, u32[]{:S(2)}) collective-permute-start(f32[8,128]{1,0:T(8,128)S(1)} %add.7.refs_0_), channel_id=1, source_target_pairs={{0,16},{4,20},{8,24},{12,28},{16,0},{20,4},{24,8},{28,12},{1,17},{... | collective-permute-start | bytes 12296 | tf_op jit(solution)/shard_map/ppermute | solution.py:331
  83.2 1.6 %collective-permute-done.22.refs_1_ = f32[8,128]{1,0:T(8,128)S(1)} collective-permute-done((f32[8,128]{1,0:T(8,128)S(1)}, f32[8,128]{1,0:T(8,128)S(1)}, u32[]{:S(2)}, u32[]{:S(2)}) %collective-permute-start.22) | collective-permute-done | bytes 4128 | tf_op jit(solution)/shard_map/ppermute | solution.py:331
  84.8 2.3 %scale.1 = (f32[8192,128]{1,0:T(8,128)}, f32[1,16]{1,0:T(1,128)}) custom-call(f32[8,128]{1,0:T(8,128)S(1)} %add.7.refs_0_, f32[8,128]{1,0:T(8,128)S(1)} %collective-permute-done.22.refs_1_, f32[4096,128]{1,0:T(8,128)S(1)} %get-tuple-element.55.refs_2_, f32[3072,128]{1,0:T(8,128)S(1)} %get-tuple-element.56.refs_3_, f32[1024,128]{1,0:T(8,128)S(1)} %get-tuple-element.57.refs_4_), custom_call_target="tpu_custom_call" | custom-call | flops 1048576 | bytes 8388608 | tf_op jit(solution)/shard_map/scale/pallas_call | solution.py:334
  (17 shorter events, 0.0 us)
Async XLA Ops:
  2.4 17.2 %collective-permute-start.13 = (f32[512,128]{1,0:T(8,128)}, f32[512,128]{1,0:T(8,128)S(1)}, u32[]{:S(2)}, u32[]{:S(2)}) collective-permute-start(f32[512,128]{1,0:T(8,128)} %shard_map.52), channel_id=1, source_target_pairs={{0,2},{1,3},{2,0},{3,1},{4,6},{5,7},{6,4},{7,5},{8,10},{9,11},{10,... | collective-permute-start | bytes 786440 | tf_op jit(solution)/shard_map/ppermute | solution.py:251
  7.8 4.8 %copy-start.1 = (f32[4,8,8192]{2,1,0:T(8,128)S(1)}, f32[4,8,8192]{2,1,0:T(8,128)}, u32[]{:S(2)}) copy-start(f32[4,8,8192]{2,1,0:T(8,128)} %param.4) | copy-start | bytes 3145732
  7.8 11.8 %copy-start.7 = (f32[512,128]{1,0:T(8,128)S(1)}, f32[512,128]{1,0:T(8,128)}, u32[]{:S(2)}) copy-start(f32[512,128]{1,0:T(8,128)} %get-tuple-element.36) | copy-start | bytes 786436
  7.8 12.7 %collective-permute-start.14 = (f32[512,128]{1,0:T(8,128)}, f32[512,128]{1,0:T(8,128)S(1)}, u32[]{:S(2)}, u32[]{:S(2)}) collective-permute-start(f32[512,128]{1,0:T(8,128)} %get-tuple-element.47), channel_id=1, source_target_pairs={{0,3},{1,2},{2,1},{3,0},{4,7},{5,6},{6,5},{7,4},{8,11},{9,10},{10,... | collective-permute-start | bytes 786440 | tf_op jit(solution)/shard_map/ppermute | solution.py:251
  12.0 43.5 %copy-start.10 = (f32[128,128]{1,0:T(8,128)S(1)}, f32[128,128]{1,0:T(8,128)}, u32[]{:S(2)}) copy-start(f32[128,128]{1,0:T(8,128)} %get-tuple-element.38) | copy-start | bytes 196612
  12.0 43.6 %copy-start.9 = (f32[128,128]{1,0:T(8,128)S(1)}, f32[128,128]{1,0:T(8,128)}, u32[]{:S(2)}) copy-start(f32[128,128]{1,0:T(8,128)} %get-tuple-element.39) | copy-start | bytes 196612
  12.0 51.7 %copy-start.8 = (f32[128,128]{1,0:T(8,128)S(1)}, f32[128,128]{1,0:T(8,128)}, u32[]{:S(2)}) copy-start(f32[128,128]{1,0:T(8,128)} %get-tuple-element.40) | copy-start | bytes 196612
  12.0 52.2 %copy-start.6 = (s32[64]{0:T(128)S(1)}, s32[64]{0:T(128)}, u32[]{:S(2)}) copy-start(s32[64]{0:T(128)} %sources.1) | copy-start | bytes 772
  12.0 9.6 %collective-permute-start.12 = (f32[512,128]{1,0:T(8,128)}, f32[512,128]{1,0:T(8,128)S(1)}, u32[]{:S(2)}, u32[]{:S(2)}) collective-permute-start(f32[512,128]{1,0:T(8,128)} %get-tuple-element.46), channel_id=1, source_target_pairs={{0,1},{1,0},{2,3},{3,2},{4,5},{5,4},{6,7},{7,6},{8,9},{9,8},{10,11... | collective-permute-start | bytes 786440 | tf_op jit(solution)/shard_map/ppermute | solution.py:251
  12.1 7.5 %collective-permute-start.9 = (f32[384,128]{1,0:T(8,128)}, f32[384,128]{1,0:T(8,128)S(1)}, u32[]{:S(2)}, u32[]{:S(2)}) collective-permute-start(f32[384,128]{1,0:T(8,128)} %get-tuple-element.42), channel_id=1, source_target_pairs={{0,1},{1,0},{2,3},{3,2},{4,5},{5,4},{6,7},{7,6},{8,9},{9,8},{10,11... | collective-permute-start | bytes 589832 | tf_op jit(solution)/shard_map/ppermute | solution.py:251
  12.7 5.4 %collective-permute-start = (f32[128,128]{1,0:T(8,128)S(1)}, f32[128,128]{1,0:T(8,128)S(1)}, u32[]{:S(2)}, u32[]{:S(2)}) collective-permute-start(f32[128,128]{1,0:T(8,128)S(1)} %bitcast.21), channel_id=1, source_target_pairs={{0,4},{4,8},{8,12},{12,16},{16,20},{20,24},{24,28},{1,5},{5,9},{9,... | collective-permute-start | bytes 196616 | tf_op jit(solution)/shard_map/ppermute | solution.py:272
  18.1 22.1 %collective-permute-start.2 = (f32[512,128]{1,0:T(8,128)}, f32[512,128]{1,0:T(8,128)S(1)}, u32[]{:S(2)}, u32[]{:S(2)}) collective-permute-start(f32[512,128]{1,0:T(8,128)} %get-tuple-element.35), channel_id=1, source_target_pairs={{0,2},{1,3},{2,0},{3,1},{4,6},{5,7},{6,4},{7,5},{8,10},{9,11},{10,... | collective-permute-start | bytes 786440 | tf_op jit(solution)/shard_map/ppermute | solution.py:251
  19.6 21.7 %collective-permute-start.3 = (f32[512,128]{1,0:T(8,128)S(1)}, f32[512,128]{1,0:T(8,128)S(1)}, u32[]{:S(2)}, u32[]{:S(2)}) collective-permute-start(f32[512,128]{1,0:T(8,128)S(1)} %copy-done.7), channel_id=1, source_target_pairs={{0,3},{1,2},{2,1},{3,0},{4,7},{5,6},{6,5},{7,4},{8,11},{9,10},{10,... | collective-permute-start | bytes 786440 | tf_op jit(solution)/shard_map/ppermute | solution.py:251
  19.6 17.7 %collective-permute-start.10 = (f32[384,128]{1,0:T(8,128)}, f32[384,128]{1,0:T(8,128)S(1)}, u32[]{:S(2)}, u32[]{:S(2)}) collective-permute-start(f32[384,128]{1,0:T(8,128)} %get-tuple-element.43), channel_id=1, source_target_pairs={{0,2},{1,3},{2,0},{3,1},{4,6},{5,7},{6,4},{7,5},{8,10},{9,11},{10,... | collective-permute-start | bytes 589832 | tf_op jit(solution)/shard_map/ppermute | solution.py:251
  20.5 18.7 %collective-permute-start.11 = (f32[384,128]{1,0:T(8,128)}, f32[384,128]{1,0:T(8,128)S(1)}, u32[]{:S(2)}, u32[]{:S(2)}) collective-permute-start(f32[384,128]{1,0:T(8,128)} %get-tuple-element.44), channel_id=1, source_target_pairs={{0,3},{1,2},{2,1},{3,0},{4,7},{5,6},{6,5},{7,4},{8,11},{9,10},{10,... | collective-permute-start | bytes 589832 | tf_op jit(solution)/shard_map/ppermute | solution.py:251
  21.6 21.0 %collective-permute-start.1 = (f32[512,128]{1,0:T(8,128)}, f32[512,128]{1,0:T(8,128)S(1)}, u32[]{:S(2)}, u32[]{:S(2)}) collective-permute-start(f32[512,128]{1,0:T(8,128)} %get-tuple-element.34), channel_id=1, source_target_pairs={{0,1},{1,0},{2,3},{3,2},{4,5},{5,4},{6,7},{7,6},{8,9},{9,8},{10,11... | collective-permute-start | bytes 786440 | tf_op jit(solution)/shard_map/ppermute | solution.py:251
  21.8 43.7 %copy-start.2 = (f32[512,128]{1,0:T(8,128)S(1)}, f32[512,128]{1,0:T(8,128)}, u32[]{:S(2)}) copy-start(f32[512,128]{1,0:T(8,128)} %get-tuple-element.45.refs_2_) | copy-start | bytes 786436
  21.8 43.7 %copy-start.3 = (f32[512,128]{1,0:T(8,128)S(1)}, f32[512,128]{1,0:T(8,128)}, u32[]{:S(2)}) copy-start(f32[512,128]{1,0:T(8,128)} %get-tuple-element.48.refs_8_) | copy-start | bytes 786436
  37.3 11.4 %collective-permute-start.17 = (f32[512,128]{1,0:T(8,128)}, f32[512,128]{1,0:T(8,128)S(1)}, u32[]{:S(2)}, u32[]{:S(2)}) collective-permute-start(f32[512,128]{1,0:T(8,128)} %get-tuple-element.49), channel_id=1, source_target_pairs={{0,1},{1,0},{2,3},{3,2},{4,5},{5,4},{6,7},{7,6},{8,9},{9,8},{10,11... | collective-permute-start | bytes 786440 | tf_op jit(solution)/shard_map/ppermute | solution.py:251
  39.2 10.8 %collective-permute-start.18 = (f32[512,128]{1,0:T(8,128)}, f32[512,128]{1,0:T(8,128)S(1)}, u32[]{:S(2)}, u32[]{:S(2)}) collective-permute-start(f32[512,128]{1,0:T(8,128)} %get-tuple-element.50), channel_id=1, source_target_pairs={{0,2},{1,3},{2,0},{3,1},{4,6},{5,7},{6,4},{7,5},{8,10},{9,11},{10,... | collective-permute-start | bytes 786440 | tf_op jit(solution)/shard_map/ppermute | solution.py:251
  40.2 15.3 %collective-permute-start.19 = (f32[512,128]{1,0:T(8,128)}, f32[512,128]{1,0:T(8,128)S(1)}, u32[]{:S(2)}, u32[]{:S(2)}) collective-permute-start(f32[512,128]{1,0:T(8,128)} %get-tuple-element.51), channel_id=1, source_target_pairs={{0,3},{1,2},{2,1},{3,0},{4,7},{5,6},{6,5},{7,4},{8,11},{9,10},{10,... | collective-permute-start | bytes 786440 | tf_op jit(solution)/shard_map/ppermute | solution.py:251
  41.3 14.3 %collective-permute-start.16 = (f32[512,128]{1,0:T(8,128)S(1)}, f32[512,128]{1,0:T(8,128)S(1)}, u32[]{:S(2)}, u32[]{:S(2)}) collective-permute-start(f32[512,128]{1,0:T(8,128)S(1)} %get-tuple-element.60), channel_id=1, source_target_pairs={{4,0},{8,4},{12,8},{16,12},{20,16},{24,20},{28,24},{5,1},{9,5},{13... | collective-permute-start | bytes 786440 | tf_op jit(solution)/shard_map/ppermute | solution.py:290
  42.6 21.2 %collective-permute-start.15 = (f32[512,128]{1,0:T(8,128)S(1)}, f32[512,128]{1,0:T(8,128)S(1)}, u32[]{:S(2)}, u32[]{:S(2)}) collective-permute-start(f32[512,128]{1,0:T(8,128)S(1)} %get-tuple-element.61), channel_id=1, source_target_pairs={{0,4},{4,8},{8,12},{12,16},{16,20},{20,24},{24,28},{1,5},{5,9},{9,... | collective-permute-start | bytes 786440 | tf_op jit(solution)/shard_map/ppermute | solution.py:291
  48.7 19.2 %collective-permute-start.5 = (f32[512,128]{1,0:T(8,128)S(1)}, f32[512,128]{1,0:T(8,128)S(1)}, u32[]{:S(2)}, u32[]{:S(2)}) collective-permute-start(f32[512,128]{1,0:T(8,128)S(1)} %get-tuple-element.62), channel_id=1, source_target_pairs={{4,0},{8,4},{12,8},{16,12},{20,16},{24,20},{28,24},{5,1},{9,5},{13... | collective-permute-start | bytes 786440 | tf_op jit(solution)/shard_map/ppermute | solution.py:290
  50.0 19.3 %collective-permute-start.4 = (f32[512,128]{1,0:T(8,128)S(1)}, f32[512,128]{1,0:T(8,128)S(1)}, u32[]{:S(2)}, u32[]{:S(2)}) collective-permute-start(f32[512,128]{1,0:T(8,128)S(1)} %get-tuple-element.63), channel_id=1, source_target_pairs={{0,4},{4,8},{8,12},{12,16},{16,20},{20,24},{24,28},{1,5},{5,9},{9,... | collective-permute-start | bytes 786440 | tf_op jit(solution)/shard_map/ppermute | solution.py:291
  55.5 15.6 %collective-permute-start.6 = (f32[128,128]{1,0:T(8,128)S(1)}, f32[128,128]{1,0:T(8,128)S(1)}, u32[]{:S(2)}, u32[]{:S(2)}) collective-permute-start(f32[128,128]{1,0:T(8,128)S(1)} %copy-done.10), channel_id=1, source_target_pairs={{0,1},{1,0},{2,3},{3,2},{4,5},{5,4},{6,7},{7,6},{8,9},{9,8},{10,11... | collective-permute-start | bytes 196616 | tf_op jit(solution)/shard_map/ppermute | solution.py:251
  55.6 15.5 %collective-permute-start.7 = (f32[128,128]{1,0:T(8,128)S(1)}, f32[128,128]{1,0:T(8,128)S(1)}, u32[]{:S(2)}, u32[]{:S(2)}) collective-permute-start(f32[128,128]{1,0:T(8,128)S(1)} %copy-done.9), channel_id=1, source_target_pairs={{0,2},{1,3},{2,0},{3,1},{4,6},{5,7},{6,4},{7,5},{8,10},{9,11},{10,... | collective-permute-start | bytes 196616 | tf_op jit(solution)/shard_map/ppermute | solution.py:251
  63.7 7.4 %collective-permute-start.8 = (f32[128,128]{1,0:T(8,128)S(1)}, f32[128,128]{1,0:T(8,128)S(1)}, u32[]{:S(2)}, u32[]{:S(2)}) collective-permute-start(f32[128,128]{1,0:T(8,128)S(1)} %copy-done.8), channel_id=1, source_target_pairs={{0,3},{1,2},{2,1},{3,0},{4,7},{5,6},{6,5},{7,4},{8,11},{9,10},{10,... | collective-permute-start | bytes 196616 | tf_op jit(solution)/shard_map/ppermute | solution.py:251
  65.5 3.7 %copy-start = (f32[512,128]{1,0:T(8,128)S(1)}, f32[512,128]{1,0:T(8,128)}, u32[]{:S(2)}) copy-start(f32[512,128]{1,0:T(8,128)} %get-tuple-element.33.refs_2_) | copy-start | bytes 786436
  65.6 3.7 %copy-start.4 = (f32[384,128]{1,0:T(8,128)S(1)}, f32[384,128]{1,0:T(8,128)}, u32[]{:S(2)}) copy-start(f32[384,128]{1,0:T(8,128)} %get-tuple-element.41.refs_8_) | copy-start | bytes 589828
  69.3 1.9 %copy-start.5 = (f32[128,128]{1,0:T(8,128)S(1)}, f32[128,128]{1,0:T(8,128)}, u32[]{:S(2)}) copy-start(f32[128,128]{1,0:T(8,128)} %get-tuple-element.37.refs_8_) | copy-start | bytes 196612
  72.0 4.1 %collective-permute-start.20 = (f32[8,128]{1,0:T(8,128)S(1)}, f32[8,128]{1,0:T(8,128)S(1)}, u32[]{:S(2)}, u32[]{:S(2)}) collective-permute-start(f32[8,128]{1,0:T(8,128)S(1)} %get-tuple-element.54), channel_id=1, source_target_pairs={{0,4},{4,0},{8,12},{12,8},{16,20},{20,16},{24,28},{28,24},{1,5},{5... | collective-permute-start | bytes 12296 | tf_op jit(solution)/shard_map/ppermute | solution.py:331
  76.0 4.2 %collective-permute-start.21 = (f32[8,128]{1,0:T(8,128)S(1)}, f32[8,128]{1,0:T(8,128)S(1)}, u32[]{:S(2)}, u32[]{:S(2)}) collective-permute-start(f32[8,128]{1,0:T(8,128)S(1)} %add.6), channel_id=1, source_target_pairs={{0,8},{4,12},{8,0},{12,4},{16,24},{20,28},{24,16},{28,20},{1,9},{5... | collective-permute-start | bytes 12296 | tf_op jit(solution)/shard_map/ppermute | solution.py:331
  80.2 4.6 %collective-permute-start.22 = (f32[8,128]{1,0:T(8,128)S(1)}, f32[8,128]{1,0:T(8,128)S(1)}, u32[]{:S(2)}, u32[]{:S(2)}) collective-permute-start(f32[8,128]{1,0:T(8,128)S(1)} %add.7.refs_0_), channel_id=1, source_target_pairs={{0,16},{4,20},{8,24},{12,28},{16,0},{20,4},{24,8},{28,12},{1,17},{... | collective-permute-start | bytes 12296 | tf_op jit(solution)/shard_map/ppermute | solution.py:331
